TPU v7x, 32 devices: a whole 2x2x4 slice. The times are simulated.
32 devices in a mesh: gx: 2 (over y), gy: 4 (over x, core), gz: 4 (over z).
Axes of the slice: x: 2, y: 2, z: 4, core: 2. Of those that a mesh axis runs over, the one named last changes fastest.
Arguments:
- residual_in: float32 [2, 8, 32, 512], P('gx', 'gy', 'gz'), may hold values from -6 to 6
- geometry: float32 [3, 2, 8, 32], P(None, 'gx', 'gy', 'gz'), may hold values from 0.5 to 2
- eig_top: float32 [2], replicated, may hold values from 1.5 to 2.5
- coarse_rows: float32 [2, 12, 32, 6, 128], P('gx', 'gy', 'gz'), may hold values from -0.5 to 0.5
- block_ids: int32 [2, 4, 4, 6], P('gx', 'gy', 'gz'), may hold values from 0 to 63, as said below
Outputs:
- correction: float32 [2, 8, 32, 512], P('gx', 'gy', 'gz')
Inputs may be any that keep to these rules, and one draw needn't show every extreme that they name: `block_ids`: the 6 ids of one row block are distinct.
All inputs are finite; a program needn't handle non-finite values.
Results may differ from a plain program's by a relative error of at most 0.00018.
Values sent between devices are 32-bit elements; how exact they have to be, the bound alone decides.
No kernel may reach another device: no remote copies, remote signals or barrier semaphores. Data moves between devices by JAX's collectives and lax.ppermute only.
A program may use at most 64 MiB of HBM per device.

v0:
```python
import functools
import math

import jax
import jax.numpy as jnp
import numpy as np
from jax import lax
from jax.experimental import pallas as pl
from jax.experimental.pallas import tpu as pltpu
from jax.sharding import PartitionSpec as P

NF = 8
NM = 4
NC = 2
LANES = 128
SUB = 8
SIGMA = 0.55 / 0.45
RHO0 = 1.0 / SIGMA
RHO1 = 1.0 / (2.0 * SIGMA - RHO0)


def legendre_pair(point, degree):
    previous = 1.0
    current = point
    for order in range(1, degree):
        following = ((2 * order + 1) * point * current - order * previous) / (order + 1)
        previous = current
        current = following
    return (current, previous)


def gll_tables(points):
    degree = points - 1
    node_list = []
    for index in range(points):
        guess = -math.cos(math.pi * index / degree)
        for sweep in range(100):
            high_val, low_val = legendre_pair(guess, degree)
            guess = guess - (guess * high_val - low_val) / (points * high_val)
        node_list.append(guess)
    node_list[0] = -1.0
    node_list[degree] = 1.0
    node_pos = np.array(node_list)
    at_nodes = np.array([legendre_pair(value, degree)[0] for value in node_list])
    weights = 2.0 / (degree * (degree + 1) * at_nodes**2)
    derivative = np.zeros((points, points))
    for row_pos in range(points):
        for col_pos in range(points):
            if row_pos != col_pos:
                derivative[row_pos, col_pos] = at_nodes[row_pos] / (
                    at_nodes[col_pos] * (node_pos[row_pos] - node_pos[col_pos])
                )
    derivative[0, 0] = -degree * (degree + 1) / 4.0
    derivative[degree, degree] = degree * (degree + 1) / 4.0
    stiffness = derivative.T @ (weights[:, None] * derivative)
    return (node_pos, weights, stiffness)


def interp_table(fine_pts, coarse_pts):
    fine_nodes = gll_tables(fine_pts)[0]
    coarse_nodes = gll_tables(coarse_pts)[0]
    lagrange = np.ones((fine_pts, coarse_pts))
    for col_pos in range(coarse_pts):
        for other_pos in range(coarse_pts):
            if other_pos != col_pos:
                lagrange[:, col_pos] *= (fine_nodes - coarse_nodes[other_pos]) / (
                    coarse_nodes[col_pos] - coarse_nodes[other_pos]
                )
    return lagrange


class Level:
    def __init__(self, points):
        self.n = points
        _, weights, stiffness = gll_tables(points)
        self.w = [float(v) for v in weights]
        self.kd = [float(v) for v in np.diag(stiffness)]
        scaled = stiffness / weights[:, None]
        half = points // 2
        flipped = scaled[:, ::-1]
        self.even = [[float(v) for v in row[:half]] for row in (scaled + flipped)[:half] / 2]
        self.odd = [[float(v) for v in row[:half]] for row in (scaled - flipped)[:half] / 2]
        self.scaled = scaled
        self.weights = weights
        self.diag = np.diag(stiffness)


FINE = Level(NF)
MID = Level(NM)
UP_F = interp_table(NF, NM)
UP_C = interp_table(NM, NC)


def shared_faces(lagrange):
    out = lagrange.copy()
    out[0] *= 0.5
    out[-1] *= 0.5
    return out


def pad_rows(column, fill=0.0):
    out = np.full((SUB,), fill)
    out[: column.shape[0]] = column
    return out


def build_tables():
    rows = []
    index = {}

    def put(name, columns):
        index[name] = len(rows)
        rows.extend(columns)

    put("kz8", [FINE.scaled[:, c] for c in range(NF)])
    put("kz4", [pad_rows(MID.scaled[:, c]) for c in range(NM)])
    put("w8", [FINE.weights])
    put("w4", [pad_rows(MID.weights, 1.0)])
    put("kd8", [FINE.diag])
    put("kd4", [pad_rows(MID.diag, 1.0)])
    put("rz8", [pad_rows(shared_faces(UP_F)[c]) for c in range(NF)])
    put("rz4", [pad_rows(shared_faces(UP_C)[c]) for c in range(NM)])
    put("pz8", [UP_F[:, c] for c in range(NM)])
    put("pz4", [pad_rows(UP_C[:, c]) for c in range(NC)])
    flat = np.concatenate(rows).astype(np.float32)
    return np.ascontiguousarray(np.broadcast_to(flat[:, None], (flat.shape[0], LANES))), index


TABLE, TINDEX = build_tables()
MASK_Y_LO, MASK_Y_HI, MASK_Z_LO, MASK_Z_HI, FAC_Y_LO, FAC_Y_HI, DEV_ID, TOP_ROW = range(8)


class Geo:
    def __init__(self, gx, gy, cy, cz, nz):
        self.gx, self.gy, self.cy, self.cz, self.nz = gx, gy, cy, cz, nz
        self.wy = gy * cy
        self.lanes = gx * self.wy * cz
        self.ne = cy * cz
        self.planes = gx * gy
        self.half = gy // 2 if gy % 2 == 0 else gy
        self.cores = gy // self.half
        self.chunks = self.lanes // LANES

    def masks(self):
        lane = np.arange(self.lanes)
        z = lane % self.cz
        y = (lane // self.cz) % self.wy
        out = np.zeros((8, self.lanes), np.float32)
        out[MASK_Y_LO] = y > 0
        out[MASK_Y_HI] = y < self.wy - 1
        out[MASK_Z_LO] = z > 0
        out[MASK_Z_HI] = z < self.cz - 1
        out[FAC_Y_LO] = np.where(y > 0, 0.5, 1.0)
        out[FAC_Y_HI] = np.where(y < self.wy - 1, 0.5, 1.0)
        out[DEV_ID] = lane // self.ne
        out[TOP_ROW] = y == self.wy - 1
        return out


def roll(value, shift):
    size = value.shape[-1]
    shift %= size
    return value if shift == 0 else pltpu.roll(value, shift, axis=value.ndim - 1)


def tab(tref, name, pos=0):
    return tref[pl.ds((TINDEX[name] + pos) * SUB, SUB), :]


def lane_ds(chunk):
    if isinstance(chunk, int):
        return pl.ds(chunk * LANES, LANES)
    return pl.ds(pl.multiple_of(chunk * LANES, LANES), LANES)


def for_tiles(geo, body):
    def step(pos, carry):
        if geo.chunks == 1:
            body(pos, 0)
        else:
            body(pos // geo.chunks, pos % geo.chunks)
        return carry

    lax.fori_loop(0, geo.nz * geo.chunks, step, 0)


def loop(count, body):
    def step(pos, carry):
        body(pos)
        return carry

    lax.fori_loop(0, count, step, 0)


def rows8(pos):
    if isinstance(pos, int):
        return pl.ds(pos * SUB, SUB)
    return pl.ds(pl.multiple_of(pos * SUB, SUB), SUB)


def wide_load(ref, zb, rows, geo):
    parts = [ref[zb, ch, rows, :] for ch in range(geo.chunks)]
    return parts[0] if len(parts) == 1 else jnp.concatenate(parts, axis=1)


def wide_store(ref, zb, rows, geo, value):
    for ch in range(geo.chunks):
        ref[zb, ch, rows, :] = value[:, ch * LANES : (ch + 1) * LANES]


def gather_sum(ref, mref, geo, n):
    xs = geo.wy * geo.cz
    last = (n - 1) * n
    for b in range(n):
        for zb in range(geo.nz):
            low = wide_load(ref, zb, rows8(b), geo)
            high = wide_load(ref, zb, rows8(last + b), geo)
            wide_store(ref, zb, rows8(b), geo, low + roll(high, xs))
            wide_store(ref, zb, rows8(last + b), geo, high + roll(low, -xs))
    y_lo = mref[MASK_Y_LO : MASK_Y_LO + 1, :]
    y_hi = mref[MASK_Y_HI : MASK_Y_HI + 1, :]
    for a in range(n):
        first, final = rows8(a * n), rows8(a * n + n - 1)
        for zb in range(geo.nz):
            low = wide_load(ref, zb, first, geo)
            high = wide_load(ref, zb, final, geo)
            wide_store(ref, zb, first, geo, low + y_lo * roll(high, geo.cz))
            wide_store(ref, zb, final, geo, high + y_hi * roll(low, -geo.cz))
    z_lo = mref[MASK_Z_LO : MASK_Z_LO + 1, :] > 0.5
    z_hi = mref[MASK_Z_HI : MASK_Z_HI + 1, :] > 0.5
    group = min(SUB, n * n)
    for g in range(n * n // group):
        first = pl.ds(g * group * SUB, group, stride=SUB)
        final = pl.ds(g * group * SUB + n - 1, group, stride=SUB)
        low = [wide_load(ref, zb, first, geo) for zb in range(geo.nz)]
        high = [wide_load(ref, zb, final, geo) for zb in range(geo.nz)]
        for zb in range(geo.nz):
            before = roll(high[(zb - 1) % geo.nz], -(geo.cz - 1))
            after = roll(low[(zb + 1) % geo.nz], geo.cz - 1)
            near = jnp.where(z_lo, roll(high[zb], 1), before)
            wide_store(ref, zb, first, geo, low[zb] + near)
            near = jnp.where(z_hi, roll(low[zb], -1), after)
            wide_store(ref, zb, final, geo, high[zb] + near)


def contract(values, level):
    half = level.n // 2
    sums = [values[a] + values[level.n - 1 - a] for a in range(half)]
    diffs = [values[a] - values[level.n - 1 - a] for a in range(half)]
    out = [None] * level.n
    for i in range(half):
        even = sums[0] * level.even[i][0]
        odd = diffs[0] * level.odd[i][0]
        for a in range(1, half):
            even = even + sums[a] * level.even[i][a]
            odd = odd + diffs[a] * level.odd[i][a]
        out[i] = even + odd
        out[level.n - 1 - i] = even - odd
    return out


def combine(values, table):
    out = []
    for i in range(table.shape[0]):
        total = values[0] * float(table[i, 0])
        for a in range(1, table.shape[1]):
            total = total + values[a] * float(table[i, a])
        out.append(total)
    return out


def sublane_mix(ref, zb, ch, row, columns):
    total = ref[zb, ch, pl.ds(row, 1), :] * columns[0]
    for c in range(1, len(columns)):
        total = total + ref[zb, ch, pl.ds(row + c, 1), :] * columns[c]
    return total


def apply_local(src, dst, gref, tref, geo, level):
    n = level.n
    kname, wname = ("kz8", "w8") if n == NF else ("kz4", "w4")

    def body(zb, ch):
        ln = lane_ds(ch)
        wc = tab(tref, wname)
        gw = [gref[zb, ch, pl.ds(i, 1), :] * wc for i in range(3)]
        columns = [tab(tref, kname, c) for c in range(n)]
        for b in range(n):
            mixed = contract([src[zb, ch, rows8(a * n + b), :] for a in range(n)], level)
            for a in range(n):
                dst[zb, ch, rows8(a * n + b), :] = mixed[a] * gw[0]
        for a in range(n):
            mixed = contract([src[zb, ch, rows8(a * n + b), :] for b in range(n)], level)
            for b in range(n):
                row = (a * n + b) * SUB
                along = sublane_mix(src, zb, ch, row, columns)
                total = dst[zb, ch, rows8(a * n + b), :] + mixed[b] * gw[1] + along * gw[2]
                dst[zb, ch, rows8(a * n + b), :] = total * (level.w[a] * level.w[b])

    for_tiles(geo, body)


def local_diagonal(dst, gref, tref, geo, level):
    n = level.n
    wname, dname = ("w8", "kd8") if n == NF else ("w4", "kd4")

    def body(zb, ch):
        ln = lane_ds(ch)
        wc = tab(tref, wname)
        gx = gref[zb, ch, pl.ds(0, 1), :] * wc
        gy = gref[zb, ch, pl.ds(1, 1), :] * wc
        gz = gref[zb, ch, pl.ds(2, 1), :] * tab(tref, dname)
        for a in range(n):
            for b in range(n):
                dst[zb, ch, rows8(a * n + b), :] = (
                    gx * (level.kd[a] * level.w[b])
                    + gy * (level.w[a] * level.kd[b])
                    + gz * (level.w[a] * level.w[b])
                )

    for_tiles(geo, body)


def each_row(geo, n, body):
    def tile(zb, ch):
        for row in range(n * n):
            body(zb, ch, rows8(row))

    for_tiles(geo, tile)


def first_smooth(res, inv, cur, tmp, mref, gref, tref, geo, level, top):
    first = 1.0 / (0.55 * top)
    second = 2.0 * RHO1 / (0.45 * top)

    def start(zb, ch, row):
        value = 1.0 / tmp[zb, ch, row, :]
        inv[zb, ch, row, :] = value
        cur[zb, ch, row, :] = value * res[zb, ch, row, :] * first

    each_row(geo, level.n, start)
    apply_local(cur, tmp, gref, tref, geo, level)
    gather_sum(tmp, mref, geo, level.n)

    def finish(zb, ch, row):
        left = res[zb, ch, row, :] - tmp[zb, ch, row, :]
        cur[zb, ch, row, :] = (1.0 + RHO0 * RHO1) * cur[zb, ch, row, :] + second * (
            inv[zb, ch, row, :] * left
        )

    each_row(geo, level.n, finish)
    apply_local(cur, tmp, gref, tref, geo, level)
    gather_sum(tmp, mref, geo, level.n)


def next_smooth(res, inv, cur, step, tmp, mref, gref, tref, geo, level, top):
    first = 1.0 / (0.55 * top)
    second = 2.0 * RHO1 / (0.45 * top)
    apply_local(cur, tmp, gref, tref, geo, level)
    gather_sum(tmp, mref, geo, level.n)

    def start(zb, ch, row):
        value = inv[zb, ch, row, :] * (res[zb, ch, row, :] - tmp[zb, ch, row, :]) * first
        step[zb, ch, row, :] = value
        cur[zb, ch, row, :] = cur[zb, ch, row, :] + value

    each_row(geo, level.n, start)
    apply_local(cur, tmp, gref, tref, geo, level)
    gather_sum(tmp, mref, geo, level.n)

    def finish(zb, ch, row):
        left = res[zb, ch, row, :] - tmp[zb, ch, row, :]
        cur[zb, ch, row, :] = (
            cur[zb, ch, row, :]
            + (RHO0 * RHO1) * step[zb, ch, row, :]
            + second * (inv[zb, ch, row, :] * left)
        )

    each_row(geo, level.n, finish)


def restrict(res, tmp, dst, mref, tref, geo, nf, nc, table, name, buf):
    scaled = shared_faces(table)

    def body(zb, ch):
        ln = lane_ds(ch)
        f_lo = mref[FAC_Y_LO : FAC_Y_LO + 1, ln]
        f_hi = mref[FAC_Y_HI : FAC_Y_HI + 1, ln]
        part = []
        for b in range(nf):
            values = []
            for a in range(nf):
                row = rows8(a * nf + b)
                values.append(res[zb, ch, row, :] - tmp[zb, ch, row, :])
            mixed = combine(values, scaled.T)
            if b == 0:
                mixed = [v * f_lo for v in mixed]
            if b == nf - 1:
                mixed = [v * f_hi for v in mixed]
            part.append(mixed)
        columns = [tab(tref, name, c) for c in range(nf)]
        for i in range(nc):
            along = combine([part[b][i] for b in range(nf)], table.T)
            for j in range(nc):
                buf[0, 0, rows8(i * nc + j), :] = along[j]
        for row in range(nc * nc):
            dst[zb, ch, rows8(row), :] = sublane_mix(buf, 0, 0, row * SUB, columns)

    for_tiles(geo, body)


def prolong_add(src, cur, tref, geo, nf, nc, table, name):
    def body(zb, ch):
        ln = lane_ds(ch)
        columns = [tab(tref, name, c) for c in range(nc)]
        part = []
        for a in range(nc):
            deep = [
                sublane_mix(src, zb, ch, (a * nc + b) * SUB, columns) for b in range(nc)
            ]
            part.append(combine(deep, table))
        for b in range(nf):
            mixed = combine([part[a][b] for a in range(nc)], table)
            for a in range(nf):
                row = rows8(a * nf + b)
                cur[zb, ch, row, :] = cur[zb, ch, row, :] + mixed[a]

    for_tiles(geo, body)


def split(value):
    high = value.astype(jnp.bfloat16)
    return high, (value - high.astype(jnp.float32)).astype(jnp.bfloat16)


def dot(left, right, dims):
    return lax.dot_general(left, right, (dims, ((), ())), preferred_element_type=jnp.float32)


def dot3(left, right_high, right_low, dims):
    high, low = split(left)
    return dot(high, right_high, dims) + (dot(high, right_low, dims) + dot(low, right_high, dims))


def down_kernel(
    own, par, eig, mref, tref, *refs, geo, nblk, prow
):
    res, inv, cur, resm, invm, curm, gref, xhi, xlo, send, tmp, tmpm, low, buf = refs
    my_x = lax.axis_index("gx")
    my_y = lax.axis_index("gy")
    my_h = my_y // geo.cores
    my_c = my_y % geo.cores

    def piece(ix, iy, start, size):
        rel = lax.rem(ix - my_x + geo.gx, geo.gx) * geo.half + lax.rem(
            iy // geo.cores - my_h + geo.half, geo.half
        )
        mine = own[rel, pl.ds(start, size), :]
        if geo.cores == 1:
            return mine
        return jnp.where(my_c == iy % geo.cores, mine, par[rel, pl.ds(start, size), :])

    devices = [(ix, iy) for ix in range(geo.gx) for iy in range(geo.gy)]
    per_chunk = LANES // geo.ne
    words = NF**3 // LANES
    for zb in range(geo.nz):
        for ch in range(geo.chunks):
            group = devices[ch * per_chunk : (ch + 1) * per_chunk]
            for blk in range(words):
                rows = [piece(ix, iy, zb * prow + blk * geo.ne, geo.ne) for ix, iy in group]
                square = jnp.concatenate(rows, axis=0)
                res[zb, ch, pl.ds(blk * LANES, LANES), :] = square.T
            total = None
            for pos, (ix, iy) in enumerate(group):
                part = roll(piece(ix, iy, zb * prow + words * geo.ne, SUB), pos * geo.ne)
                total = part if total is None else total + part
            gref[zb, ch] = total
    start = geo.nz * prow
    slots = (geo.cy + 1) * geo.cz
    for k in range(nblk):
        base = [piece(ix, iy, start + k * slots, geo.ne) for ix, iy in devices]
        extra = []
        for ix in range(geo.gx):
            extra.append(jnp.zeros(((geo.wy - 1) * geo.cz, LANES), jnp.float32))
            extra.append(piece(ix, geo.gy - 1, start + k * slots + geo.ne, geo.cz))
        high, rest = split(jnp.concatenate(base + extra, axis=0))
        xhi[k] = high
        xlo[k] = rest

    gather_sum(res, mref, geo, NF)
    local_diagonal(tmp, gref, tref, geo, FINE)
    gather_sum(tmp, mref, geo, NF)
    first_smooth(res, inv, cur, tmp, mref, gref, tref, geo, FINE, eig[0])
    restrict(res, tmp, resm, mref, tref, geo, NF, NM, UP_F, "rz8", buf)
    gather_sum(resm, mref, geo, NM)
    local_diagonal(tmpm, gref, tref, geo, MID)
    gather_sum(tmpm, mref, geo, NM)
    first_smooth(resm, invm, curm, tmpm, mref, gref, tref, geo, MID, eig[1])
    restrict(resm, tmpm, low, mref, tref, geo, NM, NC, UP_C, "rz4", buf)

    mid = geo.nz // 2
    z_lo = mref[MASK_Z_LO : MASK_Z_LO + 1, :] > 0.5
    y_lo = mref[MASK_Y_LO : MASK_Y_LO + 1, :]
    top = mref[TOP_ROW : TOP_ROW + 1, :]

    def node(zb, a, b, c):
        return wide_load(low, zb, pl.ds((a * NC + b) * SUB + c, 1), geo)

    grid = [
        [
            node(mid, a, b, 0)
            + jnp.where(
                z_lo, roll(node(mid, a, b, 1), 1), roll(node(mid - 1, a, b, 1), -(geo.cz - 1))
            )
            for b in range(NC)
        ]
        for a in range(NC)
    ]
    xs = geo.wy * geo.cz
    floor = [grid[a][0] + y_lo * roll(grid[a][1], geo.cz) for a in range(NC)]
    base = floor[0] + roll(floor[1], xs)
    ceil = top * (grid[0][1] + roll(grid[1][1], xs))
    which = mref[DEV_ID : DEV_ID + 1, :]
    lane_dev = jnp.broadcast_to(which, (geo.planes, geo.lanes))
    row_dev = lax.broadcasted_iota(jnp.int32, (geo.planes, geo.lanes), 0).astype(jnp.float32)
    mine = lane_dev == row_dev
    owned = jnp.concatenate(
        [jnp.where(mine, base, 0.0), jnp.where(mine, ceil, 0.0)], axis=1
    )
    for k in range(nblk):
        send[:, pl.ds(k * LANES, LANES)] = dot3(owned, xhi[k], xlo[k], ((1,), (0,)))
    for pos, (ix, iy) in enumerate(devices):
        send[pl.ds(pos, 1), pl.ds(nblk * LANES, LANES)] = piece(
            ix, iy, start + nblk * slots, SUB
        )[0:1]


def coarse_kernel(*refs, geo, nblk, peers):
    parts = refs[:peers]
    xhi, xlo, mref, out = refs[peers:]
    own_ids = parts[0][:, pl.ds(nblk * LANES, LANES)]
    id_rows = jnp.concatenate([own_ids[:, k : k + 1] for k in range(nblk)], axis=0)
    picked = None
    per_step = nblk if nblk * peers * geo.planes <= 1024 else 1
    for k0 in range(0, nblk, per_step):
        ks = range(k0, k0 + per_step)
        values = jnp.concatenate(
            [parts[p][:, pl.ds(k * LANES, LANES)] for k in ks for p in range(peers)], axis=0
        )
        cols = jnp.concatenate(
            [parts[p][:, pl.ds(nblk * LANES, LANES)][:, k : k + 1] for k in ks for p in range(peers)],
            axis=0,
        )
        id_lanes = jnp.broadcast_to(cols, (cols.shape[0], LANES)).T[0:1]
        hit = (id_rows == id_lanes).astype(jnp.bfloat16)
        high, rest = split(values)
        part = dot(hit, high, ((1,), (0,))) + dot(hit, rest, ((1,), (0,)))
        picked = part if picked is None else picked + part
    full = None
    for k in range(nblk):
        part = dot3(
            picked[k * geo.planes : (k + 1) * geo.planes], xhi[k], xlo[k], ((1,), (1,))
        )
        full = part if full is None else full + part
    which = mref[DEV_ID : DEV_ID + 1, :]
    lane_dev = jnp.broadcast_to(which, (geo.planes, geo.lanes))
    row_dev = lax.broadcasted_iota(jnp.int32, (geo.planes, geo.lanes), 0).astype(jnp.float32)
    mine = lane_dev == row_dev
    for pos in range(2):
        value = full[:, pos * geo.lanes : (pos + 1) * geo.lanes]
        out[pl.ds(pos, 1), :] = jnp.sum(
            jnp.where(mine, value, 0.0), axis=0, keepdims=True
        )


def up_kernel(*refs, geo):
    solved = refs[: geo.nz]
    res, inv, cur_in, resm, invm, curm_in, gref, eig, mref, tref = refs[geo.nz : geo.nz + 10]
    out, cur, curm, tmp, tmpm, step, stepm, low, turned = refs[geo.nz + 10 :]
    y_hi = mref[MASK_Y_HI : MASK_Y_HI + 1, :] > 0.5
    z_hi = mref[MASK_Z_HI : MASK_Z_HI + 1, :] > 0.5
    xs = geo.wy * geo.cz
    levels = []
    for zb in range(geo.nz):
        base = solved[zb][0:1, :]
        ceil = solved[zb][1:2, :]
        upper = jnp.where(y_hi, roll(base, -geo.cz), ceil)
        flat = [base, upper]
        levels.append([flat, [roll(v, -xs) for v in flat]])
    for zb in range(geo.nz):
        for a in range(NC):
            for b in range(NC):
                here = levels[zb][a][b]
                after = levels[(zb + 1) % geo.nz][a][b]
                row = (a * NC + b) * SUB
                wide_store(low, zb, pl.ds(row, 1), geo, here)
                deep = jnp.where(z_hi, roll(here, -1), roll(after, geo.cz - 1))
                wide_store(low, zb, pl.ds(row + 1, 1), geo, deep)

    def copy_mid(zb, ch, row):
        curm[zb, ch, row, :] = curm_in[zb, ch, row, :]

    def copy_fine(zb, ch, row):
        cur[zb, ch, row, :] = cur_in[zb, ch, row, :]

    each_row(geo, NM, copy_mid)
    each_row(geo, NF, copy_fine)
    prolong_add(low, curm, tref, geo, NM, NC, UP_C, "pz4")
    next_smooth(resm, invm, curm, stepm, tmpm, mref, gref, tref, geo, MID, eig[1])
    prolong_add(curm, cur, tref, geo, NF, NM, UP_F, "pz8")
    next_smooth(res, inv, cur, step, tmp, mref, gref, tref, geo, FINE, eig[0])
    words = NF**3 // LANES
    mid = geo.nz // 2
    for ch in range(geo.chunks):
        for blk in range(words):
            turned[pl.ds(ch * LANES, LANES), pl.ds(blk * LANES, LANES)] = cur[
                mid, ch, pl.ds(blk * LANES, LANES), :
            ].T
    my = lax.axis_index("gx") * geo.gy + lax.axis_index("gy")
    out[...] = turned[pl.ds(pl.multiple_of(my * geo.ne, SUB), geo.ne), :]


def on_device(residual_in, geometry, eig_top, coarse_rows, block_ids, sizes):
    gx, gy, gz = sizes
    cx, cy, cz = residual_in.shape[:3]
    nblk = coarse_rows.shape[3]
    geo = Geo(gx, gy, cy, cz, 3)
    ok = cx == 1 and cz % SUB == 0 and LANES % geo.ne == 0 and geo.lanes % LANES == 0
    if not ok or coarse_rows.shape[4] != LANES or geo.planes % SUB:
        raise ValueError("block shape")
    f32 = jnp.float32
    words = NF**3 // LANES
    nodal = residual_in.reshape(geo.ne, words, LANES).transpose(1, 0, 2)
    factors = jnp.pad(geometry.reshape(3, geo.ne), ((0, SUB - 3), (0, LANES - geo.ne)))
    block = jnp.concatenate([nodal.reshape(words * geo.ne, LANES), factors], axis=0)
    prow = block.shape[0]
    ring = [(i, (i + 1) % gz) for i in range(gz)]
    back = [((i + 1) % gz, i) for i in range(gz)]
    before = lax.ppermute(block, "gz", ring)
    after = lax.ppermute(block, "gz", back)
    slots = (cy + 1) * cz
    factor = coarse_rows.reshape(slots, nblk, LANES).transpose(1, 0, 2)
    labels = jnp.pad(
        block_ids.reshape(1, nblk).astype(f32), ((0, SUB - 1), (0, LANES - nblk))
    )
    column = jnp.concatenate(
        [before, block, after, factor.reshape(nblk * slots, LANES), labels], axis=0
    )
    half, cores = geo.half, geo.cores

    def rank(ix, ih, core):
        return (ix % gx) * gy + (ih % half) * cores + core

    plane = [column]
    for dx in range(gx):
        for dh in range(half):
            if dx or dh:
                pairs = [
                    (rank(ix + dx, ih + dh, core), rank(ix, ih, core))
                    for ix in range(gx)
                    for ih in range(half)
                    for core in range(cores)
                ]
                plane.append(lax.ppermute(column, ("gx", "gy"), pairs))
    own = jnp.stack(plane)
    par = own
    if cores == 2:
        par = lax.ppermute(own, "gy", [(i, i ^ 1) for i in range(gy)])

    masks = jnp.asarray(geo.masks())
    table = jnp.asarray(TABLE)
    vmem = pl.BlockSpec(memory_space=pltpu.VMEM)
    smem = pl.BlockSpec(memory_space=pltpu.SMEM)
    fine = (geo.nz, geo.chunks, NF * NF * SUB, LANES)
    middle = (geo.nz, geo.chunks, NM * NM * SUB, LANES)
    lowest = (geo.nz, geo.chunks, NC * NC * SUB, LANES)
    wide = (nblk, 2 * geo.lanes, LANES)
    params = pltpu.CompilerParams(vmem_limit_bytes=60 * 1024 * 1024)

    def shape(dims, kind=f32):
        return jax.ShapeDtypeStruct(dims, kind)

    res, inv, cur, resm, invm, curm, gfac, xhi, xlo, send = pl.pallas_call(
        functools.partial(down_kernel, geo=geo, nblk=nblk, prow=prow),
        out_shape=[
            shape(fine),
            shape(fine),
            shape(fine),
            shape(middle),
            shape(middle),
            shape(middle),
            shape((geo.nz, geo.chunks, SUB, LANES)),
            shape(wide, jnp.bfloat16),
            shape(wide, jnp.bfloat16),
            shape((geo.planes, (nblk + 1) * LANES)),
        ],
        in_specs=[vmem, vmem, smem, vmem, vmem],
        out_specs=[vmem] * 10,
        scratch_shapes=[
            pltpu.VMEM(fine, f32),
            pltpu.VMEM(middle, f32),
            pltpu.VMEM(lowest, f32),
            pltpu.VMEM((1, 1, NM * NM * SUB, LANES), f32),
        ],
        compiler_params=params,
        name="down",
    )(own, par, eig_top, masks, table)

    parts = [send]
    for d in range(1, gz):
        parts.append(lax.ppermute(send, "gz", [((i + d) % gz, i) for i in range(gz)]))
    solved = pl.pallas_call(
        functools.partial(coarse_kernel, geo=geo, nblk=nblk, peers=gz),
        out_shape=shape((SUB, geo.lanes)),
        in_specs=[vmem] * (gz + 3),
        out_specs=vmem,
        compiler_params=params,
        name="coarse",
    )(*parts, xhi, xlo, masks)

    solved_before = lax.ppermute(solved, "gz", ring)
    solved_after = lax.ppermute(solved, "gz", back)
    out = pl.pallas_call(
        functools.partial(up_kernel, geo=geo),
        out_shape=shape((geo.ne, NF**3)),
        in_specs=[vmem] * (geo.nz + 7) + [smem, vmem, vmem],
        out_specs=vmem,
        scratch_shapes=[
            pltpu.VMEM(fine, f32),
            pltpu.VMEM(middle, f32),
            pltpu.VMEM(fine, f32),
            pltpu.VMEM(middle, f32),
            pltpu.VMEM(fine, f32),
            pltpu.VMEM(middle, f32),
            pltpu.VMEM(lowest, f32),
            pltpu.VMEM((geo.lanes, NF**3), f32),
        ],
        compiler_params=params,
        name="up",
    )(
        solved_before, solved, solved_after,
        res, inv, cur, resm, invm, curm, gfac, eig_top, masks, table,
    )
    return out.reshape(cx, cy, cz, NF**3)


def solution(mesh):
    sizes = tuple(mesh.shape[name] for name in ("gx", "gy", "gz"))
    in_specs = (
        P("gx", "gy", "gz", None),
        P(None, "gx", "gy", "gz"),
        P(),
        P("gx", "gy", "gz", None, None),
        P("gx", "gy", "gz", None),
    )
    out_specs = P("gx", "gy", "gz", None)
    return jax.shard_map(
        functools.partial(on_device, sizes=sizes),
        mesh=mesh,
        in_specs=in_specs,
        out_specs=out_specs,
        check_vma=False,
    )
```

profile of v0, /device:TPU:0, one launch (start us, length us, event | category | flops | bytes accessed | tf_op | source)
XLA Modules:
  0.0 62.3 jit_solution(15656287435905330620)
XLA Ops:
  0.0 0.8 %reshape.34 = f32[3,16]{1,0:T(4,128)S(1)} reshape(f32[3,1,2,8]{3,2,1,0:T(2,128)} %param.8) | data formatting | bytes 384 | tf_op jit(solution)/shard_map/reshape | solution.py:634
  0.8 0.8 %reshape.32 = f32[16,4,128]{2,1,0:T(4,128)S(1)} reshape(f32[1,2,8,512]{3,2,1,0:T(8,128)} %param.7) | data formatting | bytes 65536 | tf_op jit(solution)/shard_map/reshape | solution.py:633
  1.5 0.0 copy-start.2
  1.6 0.0 copy-start.8
  1.6 5.1 %collective-permute-start.1 = (f32[72,128]{1,0:T(8,128)S(1)}, f32[72,128]{1,0:T(8,128)S(1)}, u32[]{:S(2)}, u32[]{:S(2)}) collective-permute-start(f32[72,128]{1,0:T(8,128)S(1)} %pad_maximum_fusion.1), channel_id=1, source_target_pairs={{1,0},{2,1},{3,2},{0,3},{5,4},{6,5},{7,6},{4,7},{9,8},{10,9},{11,1... | collective-permute-start | bytes 110600 | tf_op jit(solution)/shard_map/ppermute | solution.py:640
  6.7 0.0 collective-permute-start
  6.7 0.0 copy-done.8
  6.7 0.0 copy-done.2
  6.8 5.7 %collective-permute-done = f32[72,128]{1,0:T(8,128)S(1)} collective-permute-done((f32[72,128]{1,0:T(8,128)S(1)}, f32[72,128]{1,0:T(8,128)S(1)}, u32[]{:S(2)}, u32[]{:S(2)}) %collective-permute-start) | collective-permute-done | bytes 36896 | tf_op jit(solution)/shard_map/ppermute | solution.py:639
  12.5 0.0 collective-permute-done.1
  12.6 2.5 %collective-permute-start.4 = (f32[368,128]{1,0:T(8,128)S(1)}, f32[368,128]{1,0:T(8,128)S(1)}, u32[]{:S(2)}, u32[]{:S(2)}) collective-permute-start(f32[368,128]{1,0:T(8,128)S(1)} %constant_dynamic-update-slice_fusion), channel_id=1, source_target_pairs={{24,0},{28,4},{16,8},{20,12},{8,16},{12,20},{0,24},{4,28},{25,1},{... | collective-permute-start | bytes 565256 | tf_op jit(solution)/shard_map/ppermute | solution.py:664
  15.1 0.5 collective-permute-start.3
  15.6 0.5 collective-permute-start.2
  16.1 5.0 %collective-permute-done.4 = f32[368,128]{1,0:T(8,128)S(1)} collective-permute-done((f32[368,128]{1,0:T(8,128)S(1)}, f32[368,128]{1,0:T(8,128)S(1)}, u32[]{:S(2)}, u32[]{:S(2)}) %collective-permute-start.4) | collective-permute-done | bytes 188448 | tf_op jit(solution)/shard_map/ppermute | solution.py:664
  21.1 1.5 %collective-permute-done.3 = f32[368,128]{1,0:T(8,128)S(1)} collective-permute-done((f32[368,128]{1,0:T(8,128)S(1)}, f32[368,128]{1,0:T(8,128)S(1)}, u32[]{:S(2)}, u32[]{:S(2)}) %collective-permute-start.3) | collective-permute-done | bytes 188448 | tf_op jit(solution)/shard_map/ppermute | solution.py:664
  22.6 0.1 collective-permute-done.2
  22.7 0.0 copy-start
  22.8 0.1 collective-permute-start.5
  22.8 2.2 %collective-permute-done.5.par = f32[4,368,128]{2,1,0:T(8,128)S(1)} collective-permute-done((f32[4,368,128]{2,1,0:T(8,128)S(1)}, f32[4,368,128]{2,1,0:T(8,128)S(1)}, u32[]{:S(2)}, u32[]{:S(2)}) %collective-permute-start.5) | collective-permute-done | bytes 753696 | tf_op jit(solution)/shard_map/ppermute | solution.py:668
  25.1 0.0 copy-done
  25.1 0.0 copy-start.1
  25.1 0.9 %copy-done.1 = f32[4,368,128]{2,1,0:T(8,128)} copy-done((f32[4,368,128]{2,1,0:T(8,128)}, f32[4,368,128]{2,1,0:T(8,128)S(1)}, u32[]{:S(2)}) %copy-start.1) | copy-done | bytes 753688
  26.0 9.6 %down.1 = (f32[3,1,512,128]{3,2,1,0:T(8,128)}, f32[3,1,512,128]{3,2,1,0:T(8,128)}, f32[3,1,512,128]{3,2,1,0:T(8,128)}, f32[3,1,128,128]{3,2,1,0:T(8,128)}, f32[3...) custom-call(f32[4,368,128]{2,1,0:T(8,128)} %copy-done, ...), custom_call_target="tpu_custom_call" | custom-call | tf_op jit(solution)/shard_map/down/pallas_call | solution.py:683
  35.6 0.0 collective-permute-start.8
  35.6 0.9 %collective-permute-start.7 = (f32[8,896]{1,0:T(8,128)}, f32[8,896]{1,0:T(8,128)S(1)}, u32[]{:S(2)}, u32[]{:S(2)}) collective-permute-start(f32[8,896]{1,0:T(8,128)} %get-tuple-element.15.refs_0_), channel_id=1, source_target_pairs={{2,0},{3,1},{0,2},{1,3},{6,4},{7,5},{4,6},{5,7},{10,8},{11,9},{8,1... | collective-permute-start | bytes 86024 | tf_op jit(solution)/shard_map/ppermute | solution.py:711
  36.5 2.9 %collective-permute-start.6 = (f32[8,896]{1,0:T(8,128)}, f32[8,896]{1,0:T(8,128)S(1)}, u32[]{:S(2)}, u32[]{:S(2)}) collective-permute-start(f32[8,896]{1,0:T(8,128)} %get-tuple-element.15.refs_0_), channel_id=1, source_target_pairs={{1,0},{2,1},{3,2},{0,3},{5,4},{6,5},{7,6},{4,7},{9,8},{10,9},{11,1... | collective-permute-start | bytes 86024 | tf_op jit(solution)/shard_map/ppermute | solution.py:711
  39.4 2.1 %collective-permute-done.8.refs_3_ = f32[8,896]{1,0:T(8,128)S(1)} collective-permute-done((f32[8,896]{1,0:T(8,128)}, f32[8,896]{1,0:T(8,128)S(1)}, u32[]{:S(2)}, u32[]{:S(2)}) %collective-permute-start.8) | collective-permute-done | bytes 28704 | tf_op jit(solution)/shard_map/ppermute | solution.py:711
  41.6 0.0 copy-start.3
  41.6 0.0 collective-permute-done.7.refs_2_
  41.6 0.0 copy-start.4
  41.6 0.5 collective-permute-done.6.refs_1_
  42.1 0.0 copy-start.5
  42.1 0.1 copy-done.3
  42.2 0.0 copy-done.4
  42.2 0.5 copy-done.5
  42.7 2.6 %coarse.1.refs_1_ = f32[8,128]{1,0:T(8,128)} custom-call(f32[8,896]{1,0:T(8,128)} %get-tuple-element.15.refs_0_, f32[8,896]{1,0:T(8,128)} %copy-done.5, f32[8,896]{1,0:T(8,128)} %copy-done.4, f32[8,896]{1,0:T(8,128)} %copy-done.3, bf16[6,256,128]{2,1,0:T(8,128)(2,1)} %get-tuple-element.16.refs_4_, bf16[6,256,128]{2,1,0:T(8,128)(2,1)} %get-tuple-element.17.refs_5_, ...), custom_call_target="tpu_custom_call" | custom-call | tf_op jit(solution)/shard_map/coarse/pallas_call | solution.py:712
  45.2 3.2 %collective-permute-start.10 = (f32[8,128]{1,0:T(8,128)}, f32[8,128]{1,0:T(8,128)S(1)}, u32[]{:S(2)}, u32[]{:S(2)}) collective-permute-start(f32[8,128]{1,0:T(8,128)} %coarse.1.refs_1_), channel_id=1, source_target_pairs={{1,0},{2,1},{3,2},{0,3},{5,4},{6,5},{7,6},{4,7},{9,8},{10,9},{11,1... | collective-permute-start | bytes 12296 | tf_op jit(solution)/shard_map/ppermute | solution.py:722
  48.5 0.0 collective-permute-start.9
  48.5 1.5 %collective-permute-done.10.refs_2_ = f32[8,128]{1,0:T(8,128)S(1)} collective-permute-done((f32[8,128]{1,0:T(8,128)}, f32[8,128]{1,0:T(8,128)S(1)}, u32[]{:S(2)}, u32[]{:S(2)}) %collective-permute-start.10) | collective-permute-done | bytes 4128 | tf_op jit(solution)/shard_map/ppermute | solution.py:722
  50.0 0.0 copy-start.6
  50.0 4.1 %collective-permute-done.9.refs_0_ = f32[8,128]{1,0:T(8,128)S(1)} collective-permute-done((f32[8,128]{1,0:T(8,128)}, f32[8,128]{1,0:T(8,128)S(1)}, u32[]{:S(2)}, u32[]{:S(2)}) %collective-permute-start.9) | collective-permute-done | bytes 4128 | tf_op jit(solution)/shard_map/ppermute | solution.py:721
  54.1 0.0 copy-start.7
  54.1 0.0 copy-done.6
  54.1 0.6 copy-done.7
  54.7 7.6 %up.1 = f32[16,512]{1,0:T(8,128)} custom-call(f32[8,128]{1,0:T(8,128)} %copy-done.7, f32[8,128]{1,0:T(8,128)} %coarse.1.refs_1_, f32[8,128]{1,0:T(8,128)} %copy-done.6, f32[3,1,512,128]{3,2,1,0:T(8,128)} %get-tuple-element.18.refs_3_, f32[3,1,512,128]{3,2,1,0:T(8,128)} %get-tuple-element.19.refs_4_, f32[3,1,512,128]{3,2,1,0:T(8,128)} %get-tuple-element.20.refs_5_, ...), custom_call_target="tpu_custom_call" | custom-call | tf_op jit(solution)/shard_map/up/pallas_call | solution.py:723
  (12 shorter events, 0.1 us)
Async XLA Ops:
  1.5 5.2 %copy-start.2 = (f32[1,3,8,6,128]{4,2,3,1,0:T(8,128)S(1)}, f32[1,3,8,6,128]{4,2,3,1,0:T(8,128)}, u32[]{:S(2)}) copy-start(f32[1,3,8,6,128]{4,2,3,1,0:T(8,128)} %param.10) | copy-start | bytes 221188
  1.6 5.2 %copy-start.8 = (s32[1,1,1,6]{3,2,1,0:T(1,128)S(1)}, s32[1,1,1,6]{3,2,1,0:T(1,128)}, u32[]{:S(2)}) copy-start(s32[1,1,1,6]{3,2,1,0:T(1,128)} %param.11) | copy-start | bytes 76
  1.6 10.9 %collective-permute-start.1 = (f32[72,128]{1,0:T(8,128)S(1)}, f32[72,128]{1,0:T(8,128)S(1)}, u32[]{:S(2)}, u32[]{:S(2)}) collective-permute-start(f32[72,128]{1,0:T(8,128)S(1)} %pad_maximum_fusion.1), channel_id=1, source_target_pairs={{1,0},{2,1},{3,2},{0,3},{5,4},{6,5},{7,6},{4,7},{9,8},{10,9},{11,1... | collective-permute-start | bytes 110600 | tf_op jit(solution)/shard_map/ppermute | solution.py:640
  6.7 5.8 %collective-permute-start = (f32[72,128]{1,0:T(8,128)S(1)}, f32[72,128]{1,0:T(8,128)S(1)}, u32[]{:S(2)}, u32[]{:S(2)}) collective-permute-start(f32[72,128]{1,0:T(8,128)S(1)} %pad_maximum_fusion.1), channel_id=1, source_target_pairs={{0,1},{1,2},{2,3},{3,0},{4,5},{5,6},{6,7},{7,4},{8,9},{9,10},{10,1... | collective-permute-start | bytes 110600 | tf_op jit(solution)/shard_map/ppermute | solution.py:639
  12.6 8.6 %collective-permute-start.4 = (f32[368,128]{1,0:T(8,128)S(1)}, f32[368,128]{1,0:T(8,128)S(1)}, u32[]{:S(2)}, u32[]{:S(2)}) collective-permute-start(f32[368,128]{1,0:T(8,128)S(1)} %constant_dynamic-update-slice_fusion), channel_id=1, source_target_pairs={{24,0},{28,4},{16,8},{20,12},{8,16},{12,20},{0,24},{4,28},{25,1},{... | collective-permute-start | bytes 565256 | tf_op jit(solution)/shard_map/ppermute | solution.py:664
  15.1 7.5 %collective-permute-start.3 = (f32[368,128]{1,0:T(8,128)S(1)}, f32[368,128]{1,0:T(8,128)S(1)}, u32[]{:S(2)}, u32[]{:S(2)}) collective-permute-start(f32[368,128]{1,0:T(8,128)S(1)} %constant_dynamic-update-slice_fusion), channel_id=1, source_target_pairs={{16,0},{20,4},{24,8},{28,12},{0,16},{4,20},{8,24},{12,28},{17,1},{... | collective-permute-start | bytes 565256 | tf_op jit(solution)/shard_map/ppermute | solution.py:664
  15.6 7.1 %collective-permute-start.2 = (f32[368,128]{1,0:T(8,128)S(1)}, f32[368,128]{1,0:T(8,128)S(1)}, u32[]{:S(2)}, u32[]{:S(2)}) collective-permute-start(f32[368,128]{1,0:T(8,128)S(1)} %constant_dynamic-update-slice_fusion), channel_id=1, source_target_pairs={{8,0},{12,4},{0,8},{4,12},{24,16},{28,20},{16,24},{20,28},{9,1},{1... | collective-permute-start | bytes 565256 | tf_op jit(solution)/shard_map/ppermute | solution.py:664
  22.7 2.3 %copy-start = (f32[4,368,128]{2,1,0:T(8,128)}, f32[4,368,128]{2,1,0:T(8,128)S(1)}, u32[]{:S(2)}) copy-start(f32[4,368,128]{2,1,0:T(8,128)S(1)} %pad_maximum_fusion.own) | copy-start | bytes 2260996
  22.8 2.3 %collective-permute-start.5 = (f32[4,368,128]{2,1,0:T(8,128)S(1)}, f32[4,368,128]{2,1,0:T(8,128)S(1)}, u32[]{:S(2)}, u32[]{:S(2)}) collective-permute-start(f32[4,368,128]{2,1,0:T(8,128)S(1)} %pad_maximum_fusion.own), channel_id=1, source_target_pairs={{0,4},{4,0},{8,12},{12,8},{1,5},{5,1},{9,13},{13,9},{2,6},{6,2},{1... | collective-permute-start | bytes 2261000 | tf_op jit(solution)/shard_map/ppermute | solution.py:668
  25.1 0.9 %copy-start.1 = (f32[4,368,128]{2,1,0:T(8,128)}, f32[4,368,128]{2,1,0:T(8,128)S(1)}, u32[]{:S(2)}) copy-start(f32[4,368,128]{2,1,0:T(8,128)S(1)} %collective-permute-done.5.par) | copy-start | bytes 2260996
  35.6 6.0 %collective-permute-start.8 = (f32[8,896]{1,0:T(8,128)}, f32[8,896]{1,0:T(8,128)S(1)}, u32[]{:S(2)}, u32[]{:S(2)}) collective-permute-start(f32[8,896]{1,0:T(8,128)} %get-tuple-element.15.refs_0_), channel_id=1, source_target_pairs={{3,0},{0,1},{1,2},{2,3},{7,4},{4,5},{5,6},{6,7},{11,8},{8,9},{9,10... | collective-permute-start | bytes 86024 | tf_op jit(solution)/shard_map/ppermute | solution.py:711
  35.6 6.0 %collective-permute-start.7 = (f32[8,896]{1,0:T(8,128)}, f32[8,896]{1,0:T(8,128)S(1)}, u32[]{:S(2)}, u32[]{:S(2)}) collective-permute-start(f32[8,896]{1,0:T(8,128)} %get-tuple-element.15.refs_0_), channel_id=1, source_target_pairs={{2,0},{3,1},{0,2},{1,3},{6,4},{7,5},{4,6},{5,7},{10,8},{11,9},{8,1... | collective-permute-start | bytes 86024 | tf_op jit(solution)/shard_map/ppermute | solution.py:711
  36.5 5.6 %collective-permute-start.6 = (f32[8,896]{1,0:T(8,128)}, f32[8,896]{1,0:T(8,128)S(1)}, u32[]{:S(2)}, u32[]{:S(2)}) collective-permute-start(f32[8,896]{1,0:T(8,128)} %get-tuple-element.15.refs_0_), channel_id=1, source_target_pairs={{1,0},{2,1},{3,2},{0,3},{5,4},{6,5},{7,6},{4,7},{9,8},{10,9},{11,1... | collective-permute-start | bytes 86024 | tf_op jit(solution)/shard_map/ppermute | solution.py:711
  41.6 0.6 copy-start.3
  41.6 0.6 copy-start.4
  42.1 0.6 copy-start.5
  45.2 4.8 %collective-permute-start.10 = (f32[8,128]{1,0:T(8,128)}, f32[8,128]{1,0:T(8,128)S(1)}, u32[]{:S(2)}, u32[]{:S(2)}) collective-permute-start(f32[8,128]{1,0:T(8,128)} %coarse.1.refs_1_), channel_id=1, source_target_pairs={{1,0},{2,1},{3,2},{0,3},{5,4},{6,5},{7,6},{4,7},{9,8},{10,9},{11,1... | collective-permute-start | bytes 12296 | tf_op jit(solution)/shard_map/ppermute | solution.py:722
  48.5 5.6 %collective-permute-start.9 = (f32[8,128]{1,0:T(8,128)}, f32[8,128]{1,0:T(8,128)S(1)}, u32[]{:S(2)}, u32[]{:S(2)}) collective-permute-start(f32[8,128]{1,0:T(8,128)} %coarse.1.refs_1_), channel_id=1, source_target_pairs={{0,1},{1,2},{2,3},{3,0},{4,5},{5,6},{6,7},{7,4},{8,9},{9,10},{10,1... | collective-permute-start | bytes 12296 | tf_op jit(solution)/shard_map/ppermute | solution.py:721
  50.0 4.1 %copy-start.6 = (f32[8,128]{1,0:T(8,128)}, f32[8,128]{1,0:T(8,128)S(1)}, u32[]{:S(2)}) copy-start(f32[8,128]{1,0:T(8,128)S(1)} %collective-permute-done.10.refs_2_) | copy-start | bytes 12292
  54.1 0.6 copy-start.7
where the time goes:
time: 62.6 us; the launch traced here: 62.3 us
  waiting for transfers between devices  22.8 us (36%)
  Pallas kernels  19.8 us (32%)
  starting transfers between devices  15.8 us (25%)
  local copies, waits for them, and re-layouts  3.7 us (6%)
    pallas_call x1, Pallas kernels, on_device(): pl.pallas_call(functools.partial(down_kernel, geo=geo, nblk=nblk, prow=pr...  9.63 us
    pallas_call x1, Pallas kernels, on_device(): pl.pallas_call(functools.partial(up_kernel, geo=geo), out_shape=shape((ge...  7.64 us
    ppermute x3, waiting for transfers between devices, on_device(): plane.append(lax.ppermute(column, ('gx', 'gy'), pairs))  6.57 us
    ppermute x1, waiting for transfers between devices, on_device(): before = lax.ppermute(block, 'gz', ring)  5.72 us
    ppermute x1, starting transfers between devices, on_device(): after = lax.ppermute(block, 'gz', back)  5.13 us
    ppermute x1, waiting for transfers between devices, on_device(): solved_before = lax.ppermute(solved, 'gz', ring)  4.07 us
    ppermute x3, starting transfers between devices, on_device(): lax.ppermute(send, 'gz', [((i + d) % gz, i) for i in range(gz)])  3.83 us
    ppermute x3, starting transfers between devices, on_device(): plane.append(lax.ppermute(column, ('gx', 'gy'), pairs))  3.55 us
  transfers between devices with their start and end apart: 11, of which 9 were waited for; matrix products, arithmetic and copies ran while one was open for 0% of the time, Pallas kernels for 0%

commit v1 on v0

--- a/solution.py
+++ b/solution.py
@@ -442,10 +442,7 @@
     return dot(high, right_high, dims) + (dot(high, right_low, dims) + dot(low, right_high, dims))
 
 
-def down_kernel(
-    own, par, eig, mref, tref, *refs, geo, nblk, prow
-):
-    res, inv, cur, resm, invm, curm, gref, xhi, xlo, send, tmp, tmpm, low, buf = refs
+def pieces_of(own, par, geo):
     my_x = lax.axis_index("gx")
     my_y = lax.axis_index("gy")
     my_h = my_y // geo.cores
@@ -460,6 +457,44 @@
             return mine
         return jnp.where(my_c == iy % geo.cores, mine, par[rel, pl.ds(start, size), :])
 
+    return piece
+
+
+def pack_kernel(residual, geometry, out, *, geo):
+    words = NF**3 // LANES
+    for blk in range(words):
+        out[pl.ds(blk * geo.ne, geo.ne), :] = residual[:, pl.ds(blk * LANES, LANES)]
+    factors = [geometry[:, 0, y, :] for y in range(geo.cy)]
+    factors.append(jnp.zeros((3, LANES - geo.ne), jnp.float32))
+    out[pl.ds(words * geo.ne, SUB), :] = jnp.concatenate(
+        [jnp.concatenate(factors, axis=1), jnp.zeros((SUB - 3, LANES), jnp.float32)], axis=0
+    )
+
+
+def factor_kernel(own, par, xhi, xlo, labels, *, geo, nblk):
+    piece = pieces_of(own, par, geo)
+    devices = [(ix, iy) for ix in range(geo.gx) for iy in range(geo.gy)]
+
+    def start(slot, k):
+        return (slot * nblk + k) * geo.cz
+
+    for k in range(nblk):
+        rows = [
+            piece(ix, iy, start(slot, k), geo.cz) for ix, iy in devices for slot in range(geo.cy)
+        ]
+        for ix in range(geo.gx):
+            rows.append(jnp.zeros(((geo.wy - 1) * geo.cz, LANES), jnp.float32))
+            rows.append(piece(ix, geo.gy - 1, start(geo.cy, k), geo.cz))
+        high, rest = split(jnp.concatenate(rows, axis=0))
+        xhi[k] = high
+        xlo[k] = rest
+    for pos, (ix, iy) in enumerate(devices):
+        labels[pl.ds(pos, 1), :] = piece(ix, iy, start(geo.cy + 1, 0), SUB)[0:1]
+
+
+def down_kernel(own, par, eig, mref, tref, xhi, xlo, labels, *refs, geo, nblk, prow):
+    res, inv, cur, resm, invm, curm, gref, send, tmp, tmpm, low, buf = refs
+    piece = pieces_of(own, par, geo)
     devices = [(ix, iy) for ix in range(geo.gx) for iy in range(geo.gy)]
     per_chunk = LANES // geo.ne
     words = NF**3 // LANES
@@ -475,18 +510,6 @@
                 part = roll(piece(ix, iy, zb * prow + words * geo.ne, SUB), pos * geo.ne)
                 total = part if total is None else total + part
             gref[zb, ch] = total
-    start = geo.nz * prow
-    slots = (geo.cy + 1) * geo.cz
-    for k in range(nblk):
-        base = [piece(ix, iy, start + k * slots, geo.ne) for ix, iy in devices]
-        extra = []
-        for ix in range(geo.gx):
-            extra.append(jnp.zeros(((geo.wy - 1) * geo.cz, LANES), jnp.float32))
-            extra.append(piece(ix, geo.gy - 1, start + k * slots + geo.ne, geo.cz))
-        high, rest = split(jnp.concatenate(base + extra, axis=0))
-        xhi[k] = high
-        xlo[k] = rest
-
     gather_sum(res, mref, geo, NF)
     local_diagonal(tmp, gref, tref, geo, FINE)
     gather_sum(tmp, mref, geo, NF)
@@ -529,10 +552,7 @@
     )
     for k in range(nblk):
         send[:, pl.ds(k * LANES, LANES)] = dot3(owned, xhi[k], xlo[k], ((1,), (0,)))
-    for pos, (ix, iy) in enumerate(devices):
-        send[pl.ds(pos, 1), pl.ds(nblk * LANES, LANES)] = piece(
-            ix, iy, start + nblk * slots, SUB
-        )[0:1]
+    send[:, pl.ds(nblk * LANES, LANES)] = labels[...]
 
 
 def coarse_kernel(*refs, geo, nblk, peers):
@@ -629,115 +649,127 @@
     if not ok or coarse_rows.shape[4] != LANES or geo.planes % SUB:
         raise ValueError("block shape")
     f32 = jnp.float32
-    words = NF**3 // LANES
-    nodal = residual_in.reshape(geo.ne, words, LANES).transpose(1, 0, 2)
-    factors = jnp.pad(geometry.reshape(3, geo.ne), ((0, SUB - 3), (0, LANES - geo.ne)))
-    block = jnp.concatenate([nodal.reshape(words * geo.ne, LANES), factors], axis=0)
-    prow = block.shape[0]
+    vmem = pl.BlockSpec(memory_space=pltpu.VMEM)
+    smem = pl.BlockSpec(memory_space=pltpu.SMEM)
+    half, cores = geo.half, geo.cores
+    slots = (cy + 1) * cz
+    prow = NF**3 // LANES * geo.ne + SUB
+
+    def shape(dims, kind=f32):
+        return jax.ShapeDtypeStruct(dims, kind)
+
+    def call(body, name, specs, outs, scratch, *operands):
+        kept = list(operands) + list(outs) + list(scratch)
+        total = sum(math.prod(a.shape) * a.dtype.itemsize for a in kept)
+        return pl.pallas_call(
+            body,
+            out_shape=list(outs),
+            in_specs=specs,
+            out_specs=[vmem] * len(outs),
+            scratch_shapes=[pltpu.VMEM(a.shape, a.dtype) for a in scratch],
+            compiler_params=pltpu.CompilerParams(
+                vmem_limit_bytes=min(total + (3 << 20), 60 << 20)
+            ),
+            name=name,
+        )(*operands)
+
+    def rank(ix, ih, core):
+        return (ix % gx) * gy + (ih % half) * cores + core
+
+    def across_chips(value):
+        parts = [value]
+        for dx in range(gx):
+            for dh in range(half):
+                if dx or dh:
+                    pairs = [
+                        (rank(ix + dx, ih + dh, core), rank(ix, ih, core))
+                        for ix in range(gx)
+                        for ih in range(half)
+                        for core in range(cores)
+                    ]
+                    parts.append(lax.ppermute(value, ("gx", "gy"), pairs))
+        return jnp.stack(parts)
+
+    def between_cores(value):
+        if cores == 1:
+            return value
+        return lax.ppermute(value, "gy", [(i, i ^ 1) for i in range(gy)])
+
+    (block,) = call(
+        functools.partial(pack_kernel, geo=geo),
+        "pack",
+        [vmem, vmem],
+        [shape((prow, LANES))],
+        [],
+        residual_in.reshape(geo.ne, NF**3),
+        geometry,
+    )
     ring = [(i, (i + 1) % gz) for i in range(gz)]
     back = [((i + 1) % gz, i) for i in range(gz)]
     before = lax.ppermute(block, "gz", ring)
     after = lax.ppermute(block, "gz", back)
-    slots = (cy + 1) * cz
-    factor = coarse_rows.reshape(slots, nblk, LANES).transpose(1, 0, 2)
+
     labels = jnp.pad(
         block_ids.reshape(1, nblk).astype(f32), ((0, SUB - 1), (0, LANES - nblk))
     )
-    column = jnp.concatenate(
-        [before, block, after, factor.reshape(nblk * slots, LANES), labels], axis=0
-    )
-    half, cores = geo.half, geo.cores
-
-    def rank(ix, ih, core):
-        return (ix % gx) * gy + (ih % half) * cores + core
-
-    plane = [column]
-    for dx in range(gx):
-        for dh in range(half):
-            if dx or dh:
-                pairs = [
-                    (rank(ix + dx, ih + dh, core), rank(ix, ih, core))
-                    for ix in range(gx)
-                    for ih in range(half)
-                    for core in range(cores)
-                ]
-                plane.append(lax.ppermute(column, ("gx", "gy"), pairs))
-    own = jnp.stack(plane)
-    par = own
-    if cores == 2:
-        par = lax.ppermute(own, "gy", [(i, i ^ 1) for i in range(gy)])
+    factor = coarse_rows.reshape(cy + 1, cz, nblk, LANES).transpose(0, 2, 1, 3)
+    factor = jnp.concatenate([factor.reshape(slots * nblk, LANES), labels], axis=0)
+    factor_own = across_chips(factor)
+    factor_par = between_cores(factor_own)
+
+    own = across_chips(jnp.concatenate([before, block, after], axis=0))
+    par = between_cores(own)
 
     masks = jnp.asarray(geo.masks())
     table = jnp.asarray(TABLE)
-    vmem = pl.BlockSpec(memory_space=pltpu.VMEM)
-    smem = pl.BlockSpec(memory_space=pltpu.SMEM)
-    fine = (geo.nz, geo.chunks, NF * NF * SUB, LANES)
-    middle = (geo.nz, geo.chunks, NM * NM * SUB, LANES)
-    lowest = (geo.nz, geo.chunks, NC * NC * SUB, LANES)
-    wide = (nblk, 2 * geo.lanes, LANES)
-    params = pltpu.CompilerParams(vmem_limit_bytes=60 * 1024 * 1024)
-
-    def shape(dims, kind=f32):
-        return jax.ShapeDtypeStruct(dims, kind)
-
-    res, inv, cur, resm, invm, curm, gfac, xhi, xlo, send = pl.pallas_call(
+    fine = shape((geo.nz, geo.chunks, NF * NF * SUB, LANES))
+    middle = shape((geo.nz, geo.chunks, NM * NM * SUB, LANES))
+    lowest = shape((geo.nz, geo.chunks, NC * NC * SUB, LANES))
+    wide = shape((nblk, 2 * geo.lanes, LANES), jnp.bfloat16)
+
+    xhi, xlo, names = call(
+        functools.partial(factor_kernel, geo=geo, nblk=nblk),
+        "factor",
+        [vmem, vmem],
+        [wide, wide, shape((geo.planes, LANES))],
+        [],
+        factor_own,
+        factor_par,
+    )
+    res, inv, cur, resm, invm, curm, gfac, send = call(
         functools.partial(down_kernel, geo=geo, nblk=nblk, prow=prow),
-        out_shape=[
-            shape(fine),
-            shape(fine),
-            shape(fine),
-            shape(middle),
-            shape(middle),
-            shape(middle),
-            shape((geo.nz, geo.chunks, SUB, LANES)),
-            shape(wide, jnp.bfloat16),
-            shape(wide, jnp.bfloat16),
-            shape((geo.planes, (nblk + 1) * LANES)),
-        ],
-        in_specs=[vmem, vmem, smem, vmem, vmem],
-        out_specs=[vmem] * 10,
-        scratch_shapes=[
-            pltpu.VMEM(fine, f32),
-            pltpu.VMEM(middle, f32),
-            pltpu.VMEM(lowest, f32),
-            pltpu.VMEM((1, 1, NM * NM * SUB, LANES), f32),
-        ],
-        compiler_params=params,
-        name="down",
-    )(own, par, eig_top, masks, table)
+        "down",
+        [vmem, vmem, smem] + [vmem] * 5,
+        [fine] * 3
+        + [middle] * 3
+        + [shape((geo.nz, geo.chunks, SUB, LANES)), shape((geo.planes, (nblk + 1) * LANES))],
+        [fine, middle, lowest, shape((1, 1, NM * NM * SUB, LANES))],
+        own, par, eig_top, masks, table, xhi, xlo, names,
+    )
 
     parts = [send]
-    for d in range(1, gz):
-        parts.append(lax.ppermute(send, "gz", [((i + d) % gz, i) for i in range(gz)]))
-    solved = pl.pallas_call(
+    for d in range(gz - 1, 0, -1):
+        pairs = [((i + d) % gz, i) for i in range(gz)]
+        if gz & (gz - 1) == 0:
+            pairs = [(i ^ d, i) for i in range(gz)]
+        parts.append(lax.ppermute(send, "gz", pairs))
+    (solved,) = call(
         functools.partial(coarse_kernel, geo=geo, nblk=nblk, peers=gz),
-        out_shape=shape((SUB, geo.lanes)),
-        in_specs=[vmem] * (gz + 3),
-        out_specs=vmem,
-        compiler_params=params,
-        name="coarse",
-    )(*parts, xhi, xlo, masks)
+        "coarse",
+        [vmem] * (gz + 3),
+        [shape((SUB, geo.lanes))],
+        [],
+        *parts, xhi, xlo, masks,
+    )
 
     solved_before = lax.ppermute(solved, "gz", ring)
     solved_after = lax.ppermute(solved, "gz", back)
-    out = pl.pallas_call(
+    (out,) = call(
         functools.partial(up_kernel, geo=geo),
-        out_shape=shape((geo.ne, NF**3)),
-        in_specs=[vmem] * (geo.nz + 7) + [smem, vmem, vmem],
-        out_specs=vmem,
-        scratch_shapes=[
-            pltpu.VMEM(fine, f32),
-            pltpu.VMEM(middle, f32),
-            pltpu.VMEM(fine, f32),
-            pltpu.VMEM(middle, f32),
-            pltpu.VMEM(fine, f32),
-            pltpu.VMEM(middle, f32),
-            pltpu.VMEM(lowest, f32),
-            pltpu.VMEM((geo.lanes, NF**3), f32),
-        ],
-        compiler_params=params,
-        name="up",
-    )(
+        "up",
+        [vmem] * (geo.nz + 7) + [smem, vmem, vmem],
+        [shape((geo.ne, NF**3))],
+        [fine, middle, fine, middle, fine, middle, lowest, shape((geo.lanes, NF**3))],
         solved_before, solved, solved_after,
         res, inv, cur, resm, invm, curm, gfac, eig_top, masks, table,
     )

time: 62.6 us -> 57.2 us (0.914)
  starting transfers between devices: 15.8 us -> 22.2 us
  Pallas kernels: 19.8 us -> 14.5 us
  waiting for transfers between devices: 22.8 us -> 17.9 us
  local copies, waits for them, and re-layouts: 3.7 us -> 2.11 us
    ppermute x7 -> x11, starting transfers between devices: 7.45 us -> 13.6 us  [the longest x6 8.97 us: across_chips(): parts.append(lax.ppermute(value, ('gx', 'gy'), pairs))]
    pallas_call x3 -> x5, Pallas kernels: 19.8 us -> 14.5 us  [call(): pl.pallas_call(body, out_shape=list(outs), in_specs=specs, out_specs=[vme...]
    ppermute x7 -> x11, waiting for transfers between devices: 11.4 us -> 6.76 us  [the longest x6 3.01 us: across_chips(): parts.append(lax.ppermute(value, ('gx', 'gy'), pairs))]
    ppermute x1, waiting for transfers between devices: 0.01 us -> 1.61 us  [on_device(): after = lax.ppermute(block, 'gz', back)]
    ppermute x1, waiting for transfers between devices: 5.72 us -> 4.12 us  [on_device(): before = lax.ppermute(block, 'gz', ring)]
    reshape x3 -> x0, local copies, waits for them, and re-layouts: 1.54 us -> none  [the longest x2 0.78 us: on_device(): nodal = residual_in.reshape(geo.ne, words, LANES).transpose(1, 0, 2)]
    unnamed x24 -> x14, local copies, waits for them, and re-layouts: 2.15 us -> 2.11 us
  transfers between devices with their start and end apart: 11 -> 15, of which waited for: 9 -> 11; matrix products, arithmetic and copies ran while one was open for 0% -> 0% of each run, Pallas kernels for 0% -> 0%
where the time goes in v1:
time: 57.2 us; the launch traced here: 57 us
  starting transfers between devices  22.2 us (39%)
  waiting for transfers between devices  17.9 us (31%)
  Pallas kernels  14.5 us (25%)
  local copies, waits for them, and re-layouts  2.11 us (4%)
    pallas_call x5, Pallas kernels, call(): pl.pallas_call(body, out_shape=list(outs), in_specs=specs, out_specs=[vme...  14.5 us
    ppermute x6, starting transfers between devices, across_chips(): parts.append(lax.ppermute(value, ('gx', 'gy'), pairs))  8.97 us
    ppermute x1, starting transfers between devices, on_device(): after = lax.ppermute(block, 'gz', back)  5.08 us
    ppermute x3, starting transfers between devices, on_device(): parts.append(lax.ppermute(send, 'gz', pairs))  4.44 us
    ppermute x1, waiting for transfers between devices, on_device(): before = lax.ppermute(block, 'gz', ring)  4.12 us
    ppermute x1, waiting for transfers between devices, on_device(): solved_before = lax.ppermute(solved, 'gz', ring)  4.08 us
    ppermute x1, starting transfers between devices, on_device(): solved_after = lax.ppermute(solved, 'gz', back)  3.57 us
    ppermute x6, waiting for transfers between devices, across_chips(): parts.append(lax.ppermute(value, ('gx', 'gy'), pairs))  3.01 us
  transfers between devices with their start and end apart: 15, of which 11 were waited for; matrix products, arithmetic and copies ran while one was open for 0% of the time, Pallas kernels for 0%

profile of v1, /device:TPU:0, one launch (start us, length us, event | category | flops | bytes accessed | tf_op | source)
XLA Modules:
  0.0 57.0 jit_solution(14346131401129894826)
XLA Ops:
  0.0 0.0 copy-start.2
  0.0 0.8 %copy-done.2 = f32[1,2,8,512]{3,2,1,0:T(8,128)S(1)} copy-done((f32[1,2,8,512]{3,2,1,0:T(8,128)S(1)}, f32[1,2,8,512]{3,2,1,0:T(8,128)}, u32[]{:S(2)}) %copy-start.2) | copy-done | bytes 32792
  0.8 0.0 copy-start.3
  0.8 0.7 %copy-done.3 = f32[3,1,2,8]{3,2,1,0:T(2,128)S(1)} copy-done((f32[3,1,2,8]{3,2,1,0:T(2,128)S(1)}, f32[3,1,2,8]{3,2,1,0:T(2,128)}, u32[]{:S(2)}) %copy-start.3) | copy-done | bytes 216
  1.4 0.1 pack.1
  1.5 5.1 %collective-permute-start.1 = (f32[72,128]{1,0:T(8,128)S(1)}, f32[72,128]{1,0:T(8,128)S(1)}, u32[]{:S(2)}, u32[]{:S(2)}) collective-permute-start(f32[72,128]{1,0:T(8,128)S(1)} %pack.1), channel_id=1, source_target_pairs={{1,0},{2,1},{3,2},{0,3},{5,4},{6,5},{7,6},{4,7},{9,8},{10,9},{11,1... | collective-permute-start | bytes 110600 | tf_op jit(solution)/shard_map/ppermute | solution.py:710
  6.6 0.0 collective-permute-start
  6.6 0.0 copy-done.6
  6.6 0.0 copy-start.5
  6.6 1.6 %collective-permute-done.1 = f32[72,128]{1,0:T(8,128)S(1)} collective-permute-done((f32[72,128]{1,0:T(8,128)S(1)}, f32[72,128]{1,0:T(8,128)S(1)}, u32[]{:S(2)}, u32[]{:S(2)}) %collective-permute-start.1) | collective-permute-done | bytes 36896 | tf_op jit(solution)/shard_map/ppermute | solution.py:710
  8.2 4.1 %collective-permute-done = f32[72,128]{1,0:T(8,128)S(1)} collective-permute-done((f32[72,128]{1,0:T(8,128)S(1)}, f32[72,128]{1,0:T(8,128)S(1)}, u32[]{:S(2)}, u32[]{:S(2)}) %collective-permute-start) | collective-permute-done | bytes 36896 | tf_op jit(solution)/shard_map/ppermute | solution.py:709
  12.4 1.6 %collective-permute-start.3 = (f32[216,128]{1,0:T(8,128)S(1)}, f32[216,128]{1,0:T(8,128)S(1)}, u32[]{:S(2)}, u32[]{:S(2)}) collective-permute-start(f32[216,128]{1,0:T(8,128)S(1)} %get-tuple-element.28), channel_id=1, source_target_pairs={{16,0},{20,4},{24,8},{28,12},{0,16},{4,20},{8,24},{12,28},{17,1},{... | collective-permute-start | bytes 331784 | tf_op jit(solution)/shard_map/ppermute | solution.py:690
  14.0 1.5 %collective-permute-start.2 = (f32[216,128]{1,0:T(8,128)S(1)}, f32[216,128]{1,0:T(8,128)S(1)}, u32[]{:S(2)}, u32[]{:S(2)}) collective-permute-start(f32[216,128]{1,0:T(8,128)S(1)} %get-tuple-element.28), channel_id=1, source_target_pairs={{8,0},{12,4},{0,8},{4,12},{24,16},{28,20},{16,24},{20,28},{9,1},{1... | collective-permute-start | bytes 331784 | tf_op jit(solution)/shard_map/ppermute | solution.py:690
  15.5 0.5 collective-permute-start.4
  15.9 0.0 copy-done.5
  15.9 1.6 %collective-permute-start.7 = (f32[152,128]{1,0:T(8,128)S(1)}, f32[152,128]{1,0:T(8,128)S(1)}, u32[]{:S(2)}, u32[]{:S(2)}) collective-permute-start(f32[152,128]{1,0:T(8,128)S(1)} %get-tuple-element.30), channel_id=1, source_target_pairs={{16,0},{20,4},{24,8},{28,12},{0,16},{4,20},{8,24},{12,28},{17,1},{... | collective-permute-start | bytes 233480 | tf_op jit(solution)/shard_map/ppermute | solution.py:690
  17.5 1.5 %collective-permute-start.6 = (f32[152,128]{1,0:T(8,128)S(1)}, f32[152,128]{1,0:T(8,128)S(1)}, u32[]{:S(2)}, u32[]{:S(2)}) collective-permute-start(f32[152,128]{1,0:T(8,128)S(1)} %get-tuple-element.30), channel_id=1, source_target_pairs={{8,0},{12,4},{0,8},{4,12},{24,16},{28,20},{16,24},{20,28},{9,1},{1... | collective-permute-start | bytes 233480 | tf_op jit(solution)/shard_map/ppermute | solution.py:690
  19.0 0.2 collective-permute-done.3
  19.2 2.3 %collective-permute-start.8 = (f32[152,128]{1,0:T(8,128)S(1)}, f32[152,128]{1,0:T(8,128)S(1)}, u32[]{:S(2)}, u32[]{:S(2)}) collective-permute-start(f32[152,128]{1,0:T(8,128)S(1)} %get-tuple-element.30), channel_id=1, source_target_pairs={{24,0},{28,4},{16,8},{20,12},{8,16},{12,20},{0,24},{4,28},{25,1},{... | collective-permute-start | bytes 233480 | tf_op jit(solution)/shard_map/ppermute | solution.py:690
  21.6 0.0 collective-permute-done.2
  21.6 0.6 collective-permute-done.4
  22.2 0.1 collective-permute-start.5
  22.2 0.2 collective-permute-done.7
  22.4 0.0 collective-permute-done.6
  22.4 2.1 %collective-permute-done.8 = f32[152,128]{1,0:T(8,128)S(1)} collective-permute-done((f32[152,128]{1,0:T(8,128)S(1)}, f32[152,128]{1,0:T(8,128)S(1)}, u32[]{:S(2)}, u32[]{:S(2)}) %collective-permute-start.8) | collective-permute-done | bytes 77856 | tf_op jit(solution)/shard_map/ppermute | solution.py:690
  24.5 0.0 copy-start
  24.5 0.1 collective-permute-start.9
  24.6 1.6 %collective-permute-done.9.par = f32[4,152,128]{2,1,0:T(8,128)S(1)} collective-permute-done((f32[4,152,128]{2,1,0:T(8,128)S(1)}, f32[4,152,128]{2,1,0:T(8,128)S(1)}, u32[]{:S(2)}, u32[]{:S(2)}) %collective-permute-start.9) | collective-permute-done | bytes 311328 | tf_op jit(solution)/shard_map/ppermute | solution.py:696
  26.2 0.1 factor.1
  26.3 0.0 copy-start.1
  26.3 0.0 collective-permute-done.5.par
  26.3 0.0 copy-start.4
  26.3 0.0 copy-done
  26.4 0.6 %copy-done.1 = f32[8,128]{1,0:T(8,128)S(1)} copy-done((f32[8,128]{1,0:T(8,128)S(1)}, f32[8,128]{1,0:T(8,128)}, u32[]{:S(2)}) %copy-start.1) | copy-done | bytes 4120
  27.0 0.0 copy-done.4
  27.0 7.3 %down.1 = (f32[3,1,512,128]{3,2,1,0:T(8,128)S(1)}, f32[3,1,512,128]{3,2,1,0:T(8,128)S(1)}, f32[3,1,512,128]{3,2,1,0:T(8,128)S(1)}, f32[3,1,128,128]{3,2,1,0:T(8,...) custom-call(f32[4,216,128]{2,1,0:T(8,128)S(1)} %pad_maximum_fusion.o, ...), custom_call_target="tpu_custom_call" | custom-call | tf_op jit(solution)/shard_map/down/pallas_call | solution.py:664
  34.3 0.1 collective-permute-start.12
  34.4 0.4 collective-permute-start.11
  34.8 4.0 %collective-permute-start.10 = (f32[8,896]{1,0:T(8,128)S(1)}, f32[8,896]{1,0:T(8,128)S(1)}, u32[]{:S(2)}, u32[]{:S(2)}) collective-permute-start(f32[8,896]{1,0:T(8,128)S(1)} %get-tuple-element.19.refs_0_), channel_id=1, source_target_pairs={{3,0},{2,1},{1,2},{0,3},{7,4},{6,5},{5,6},{4,7},{11,8},{10,9},{9,1... | collective-permute-start | bytes 86024 | tf_op jit(solution)/shard_map/ppermute | solution.py:755
  38.8 0.0 collective-permute-done.12.refs_3_
  38.8 0.5 collective-permute-done.11.refs_2_
  39.2 1.7 %collective-permute-done.10.refs_1_ = f32[8,896]{1,0:T(8,128)S(1)} collective-permute-done((f32[8,896]{1,0:T(8,128)S(1)}, f32[8,896]{1,0:T(8,128)S(1)}, u32[]{:S(2)}, u32[]{:S(2)}) %collective-permute-start.10) | collective-permute-done | bytes 28704 | tf_op jit(solution)/shard_map/ppermute | solution.py:755
  40.9 0.7 %coarse.1.refs_1_ = f32[8,128]{1,0:T(8,128)S(1)} custom-call(f32[8,896]{1,0:T(8,128)S(1)} %get-tuple-element.19.refs_0_, f32[8,896]{1,0:T(8,128)S(1)} %collective-permute-done.10.refs_1_, f32[8,896]{1,0:T(8,128)S(1)} %collective-permute-done.11.refs_2_, f32[8,896]{1,0:T(8,128)S(1)} %collective-permute-done.12.refs_3_, ...), custom_call_target="tpu_custom_call" | custom-call | tf_op jit(solution)/shard_map/coarse/pallas_call | solution.py:664
  41.7 3.6 %collective-permute-start.14 = (f32[8,128]{1,0:T(8,128)S(1)}, f32[8,128]{1,0:T(8,128)S(1)}, u32[]{:S(2)}, u32[]{:S(2)}) collective-permute-start(f32[8,128]{1,0:T(8,128)S(1)} %coarse.1.refs_1_), channel_id=1, source_target_pairs={{1,0},{2,1},{3,2},{0,3},{5,4},{6,5},{7,6},{4,7},{9,8},{10,9},{11,1... | collective-permute-start | bytes 12296 | tf_op jit(solution)/shard_map/ppermute | solution.py:766
  45.3 0.0 collective-permute-start.13
  45.3 1.3 %collective-permute-done.14.refs_2_ = f32[8,128]{1,0:T(8,128)S(1)} collective-permute-done((f32[8,128]{1,0:T(8,128)S(1)}, f32[8,128]{1,0:T(8,128)S(1)}, u32[]{:S(2)}, u32[]{:S(2)}) %collective-permute-start.14) | collective-permute-done | bytes 4128 | tf_op jit(solution)/shard_map/ppermute | solution.py:766
  46.6 4.1 %collective-permute-done.13.refs_0_ = f32[8,128]{1,0:T(8,128)S(1)} collective-permute-done((f32[8,128]{1,0:T(8,128)S(1)}, f32[8,128]{1,0:T(8,128)S(1)}, u32[]{:S(2)}, u32[]{:S(2)}) %collective-permute-start.13) | collective-permute-done | bytes 4128 | tf_op jit(solution)/shard_map/ppermute | solution.py:765
  50.7 6.3 %up.1 = f32[16,512]{1,0:T(8,128)} custom-call(f32[8,128]{1,0:T(8,128)S(1)} %collective-permute-done.13.refs_0_, f32[8,128]{1,0:T(8,128)S(1)} %coarse.1.refs_1_, f32[8,128]{1,0:T(8,128)S(1)} %collective-permute-done.14.refs_2_, f32[3,1,512,128]{3,2,1,0:T(8,128)S(1)} %get-tuple-element.20.refs_3_, f32[3,1,512,128]{3,2,1,0:T(8,128)S(1)} %get-tuple-element.21.refs_4_, ...), custom_call_target="tpu_custom_call" | custom-call | tf_op jit(solution)/shard_map/up/pallas_call | solution.py:664
  (6 shorter events, 0.1 us)
Async XLA Ops:
  0.0 0.8 %copy-start.2 = (f32[1,2,8,512]{3,2,1,0:T(8,128)S(1)}, f32[1,2,8,512]{3,2,1,0:T(8,128)}, u32[]{:S(2)}) copy-start(f32[1,2,8,512]{3,2,1,0:T(8,128)} %param.7) | copy-start | bytes 98308
  0.8 0.7 %copy-start.3 = (f32[3,1,2,8]{3,2,1,0:T(2,128)S(1)}, f32[3,1,2,8]{3,2,1,0:T(2,128)}, u32[]{:S(2)}) copy-start(f32[3,1,2,8]{3,2,1,0:T(2,128)} %geometry.1) | copy-start | bytes 580
  1.4 5.2 %copy-start.6 = (s32[1,1,1,6]{3,2,1,0:T(1,128)S(1)}, s32[1,1,1,6]{3,2,1,0:T(1,128)}, u32[]{:S(2)}) copy-start(s32[1,1,1,6]{3,2,1,0:T(1,128)} %param.11) | copy-start | bytes 76
  1.5 6.7 %collective-permute-start.1 = (f32[72,128]{1,0:T(8,128)S(1)}, f32[72,128]{1,0:T(8,128)S(1)}, u32[]{:S(2)}, u32[]{:S(2)}) collective-permute-start(f32[72,128]{1,0:T(8,128)S(1)} %pack.1), channel_id=1, source_target_pairs={{1,0},{2,1},{3,2},{0,3},{5,4},{6,5},{7,6},{4,7},{9,8},{10,9},{11,1... | collective-permute-start | bytes 110600 | tf_op jit(solution)/shard_map/ppermute | solution.py:710
  6.6 5.8 %collective-permute-start = (f32[72,128]{1,0:T(8,128)S(1)}, f32[72,128]{1,0:T(8,128)S(1)}, u32[]{:S(2)}, u32[]{:S(2)}) collective-permute-start(f32[72,128]{1,0:T(8,128)S(1)} %pack.1), channel_id=1, source_target_pairs={{0,1},{1,2},{2,3},{3,0},{4,5},{5,6},{6,7},{7,4},{8,9},{9,10},{10,1... | collective-permute-start | bytes 110600 | tf_op jit(solution)/shard_map/ppermute | solution.py:709
  6.6 9.3 %copy-start.5 = (f32[1,3,8,6,128]{4,2,3,1,0:T(8,128)S(1)}, f32[1,3,8,6,128]{4,2,3,1,0:T(8,128)}, u32[]{:S(2)}) copy-start(f32[1,3,8,6,128]{4,2,3,1,0:T(8,128)} %param.10) | copy-start | bytes 221188
  12.4 6.8 %collective-permute-start.3 = (f32[216,128]{1,0:T(8,128)S(1)}, f32[216,128]{1,0:T(8,128)S(1)}, u32[]{:S(2)}, u32[]{:S(2)}) collective-permute-start(f32[216,128]{1,0:T(8,128)S(1)} %get-tuple-element.28), channel_id=1, source_target_pairs={{16,0},{20,4},{24,8},{28,12},{0,16},{4,20},{8,24},{12,28},{17,1},{... | collective-permute-start | bytes 331784 | tf_op jit(solution)/shard_map/ppermute | solution.py:690
  14.0 7.6 %collective-permute-start.2 = (f32[216,128]{1,0:T(8,128)S(1)}, f32[216,128]{1,0:T(8,128)S(1)}, u32[]{:S(2)}, u32[]{:S(2)}) collective-permute-start(f32[216,128]{1,0:T(8,128)S(1)} %get-tuple-element.28), channel_id=1, source_target_pairs={{8,0},{12,4},{0,8},{4,12},{24,16},{28,20},{16,24},{20,28},{9,1},{1... | collective-permute-start | bytes 331784 | tf_op jit(solution)/shard_map/ppermute | solution.py:690
  15.5 6.7 %collective-permute-start.4 = (f32[216,128]{1,0:T(8,128)S(1)}, f32[216,128]{1,0:T(8,128)S(1)}, u32[]{:S(2)}, u32[]{:S(2)}) collective-permute-start(f32[216,128]{1,0:T(8,128)S(1)} %get-tuple-element.28), channel_id=1, source_target_pairs={{24,0},{28,4},{16,8},{20,12},{8,16},{12,20},{0,24},{4,28},{25,1},{... | collective-permute-start | bytes 331784 | tf_op jit(solution)/shard_map/ppermute | solution.py:690
  15.9 6.5 %collective-permute-start.7 = (f32[152,128]{1,0:T(8,128)S(1)}, f32[152,128]{1,0:T(8,128)S(1)}, u32[]{:S(2)}, u32[]{:S(2)}) collective-permute-start(f32[152,128]{1,0:T(8,128)S(1)} %get-tuple-element.30), channel_id=1, source_target_pairs={{16,0},{20,4},{24,8},{28,12},{0,16},{4,20},{8,24},{12,28},{17,1},{... | collective-permute-start | bytes 233480 | tf_op jit(solution)/shard_map/ppermute | solution.py:690
  17.5 4.9 %collective-permute-start.6 = (f32[152,128]{1,0:T(8,128)S(1)}, f32[152,128]{1,0:T(8,128)S(1)}, u32[]{:S(2)}, u32[]{:S(2)}) collective-permute-start(f32[152,128]{1,0:T(8,128)S(1)} %get-tuple-element.30), channel_id=1, source_target_pairs={{8,0},{12,4},{0,8},{4,12},{24,16},{28,20},{16,24},{20,28},{9,1},{1... | collective-permute-start | bytes 233480 | tf_op jit(solution)/shard_map/ppermute | solution.py:690
  19.2 5.3 %collective-permute-start.8 = (f32[152,128]{1,0:T(8,128)S(1)}, f32[152,128]{1,0:T(8,128)S(1)}, u32[]{:S(2)}, u32[]{:S(2)}) collective-permute-start(f32[152,128]{1,0:T(8,128)S(1)} %get-tuple-element.30), channel_id=1, source_target_pairs={{24,0},{28,4},{16,8},{20,12},{8,16},{12,20},{0,24},{4,28},{25,1},{... | collective-permute-start | bytes 233480 | tf_op jit(solution)/shard_map/ppermute | solution.py:690
  22.2 4.2 %collective-permute-start.5 = (f32[4,216,128]{2,1,0:T(8,128)S(1)}, f32[4,216,128]{2,1,0:T(8,128)S(1)}, u32[]{:S(2)}, u32[]{:S(2)}) collective-permute-start(f32[4,216,128]{2,1,0:T(8,128)S(1)} %pad_maximum_fusion.own), channel_id=1, source_target_pairs={{0,4},{4,0},{8,12},{12,8},{1,5},{5,1},{9,13},{13,9},{2,6},{6,2},{1... | collective-permute-start | bytes 1327112 | tf_op jit(solution)/shard_map/ppermute | solution.py:696
  24.5 1.8 %copy-start = (f32[272,128]{1,0:T(8,128)S(1)}, f32[272,128]{1,0:T(8,128)}, u32[]{:S(2)}) copy-start(f32[272,128]{1,0:T(8,128)} %constant.8.clone.tref.refs_12_) | copy-start | bytes 417796
  24.5 1.7 %collective-permute-start.9 = (f32[4,152,128]{2,1,0:T(8,128)S(1)}, f32[4,152,128]{2,1,0:T(8,128)S(1)}, u32[]{:S(2)}, u32[]{:S(2)}) collective-permute-start(f32[4,152,128]{2,1,0:T(8,128)S(1)} %pad_maximum_fusion.1.own), channel_id=1, source_target_pairs={{0,4},{4,0},{8,12},{12,8},{1,5},{5,1},{9,13},{13,9},{2,6},{6,2},{1... | collective-permute-start | bytes 933896 | tf_op jit(solution)/shard_map/ppermute | solution.py:696
  26.3 0.7 %copy-start.1 = (f32[8,128]{1,0:T(8,128)S(1)}, f32[8,128]{1,0:T(8,128)}, u32[]{:S(2)}) copy-start(f32[8,128]{1,0:T(8,128)} %constant.7.clone.mref.refs_6_.refs_11_) | copy-start | bytes 12292
  26.3 0.7 %copy-start.4 = (f32[2]{0:T(128)S(1)}, f32[2]{0:T(128)}, u32[]{:S(2)}) copy-start(f32[2]{0:T(128)} %refs_10_.1) | copy-start | bytes 28
  34.3 4.5 %collective-permute-start.12 = (f32[8,896]{1,0:T(8,128)S(1)}, f32[8,896]{1,0:T(8,128)S(1)}, u32[]{:S(2)}, u32[]{:S(2)}) collective-permute-start(f32[8,896]{1,0:T(8,128)S(1)} %get-tuple-element.19.refs_0_), channel_id=1, source_target_pairs={{1,0},{0,1},{3,2},{2,3},{5,4},{4,5},{7,6},{6,7},{9,8},{8,9},{11,10... | collective-permute-start | bytes 86024 | tf_op jit(solution)/shard_map/ppermute | solution.py:755
  34.4 4.8 %collective-permute-start.11 = (f32[8,896]{1,0:T(8,128)S(1)}, f32[8,896]{1,0:T(8,128)S(1)}, u32[]{:S(2)}, u32[]{:S(2)}) collective-permute-start(f32[8,896]{1,0:T(8,128)S(1)} %get-tuple-element.19.refs_0_), channel_id=1, source_target_pairs={{2,0},{3,1},{0,2},{1,3},{6,4},{7,5},{4,6},{5,7},{10,8},{11,9},{8,1... | collective-permute-start | bytes 86024 | tf_op jit(solution)/shard_map/ppermute | solution.py:755
  34.8 6.2 %collective-permute-start.10 = (f32[8,896]{1,0:T(8,128)S(1)}, f32[8,896]{1,0:T(8,128)S(1)}, u32[]{:S(2)}, u32[]{:S(2)}) collective-permute-start(f32[8,896]{1,0:T(8,128)S(1)} %get-tuple-element.19.refs_0_), channel_id=1, source_target_pairs={{3,0},{2,1},{1,2},{0,3},{7,4},{6,5},{5,6},{4,7},{11,8},{10,9},{9,1... | collective-permute-start | bytes 86024 | tf_op jit(solution)/shard_map/ppermute | solution.py:755
  41.7 4.9 %collective-permute-start.14 = (f32[8,128]{1,0:T(8,128)S(1)}, f32[8,128]{1,0:T(8,128)S(1)}, u32[]{:S(2)}, u32[]{:S(2)}) collective-permute-start(f32[8,128]{1,0:T(8,128)S(1)} %coarse.1.refs_1_), channel_id=1, source_target_pairs={{1,0},{2,1},{3,2},{0,3},{5,4},{6,5},{7,6},{4,7},{9,8},{10,9},{11,1... | collective-permute-start | bytes 12296 | tf_op jit(solution)/shard_map/ppermute | solution.py:766
  45.3 5.4 %collective-permute-start.13 = (f32[8,128]{1,0:T(8,128)S(1)}, f32[8,128]{1,0:T(8,128)S(1)}, u32[]{:S(2)}, u32[]{:S(2)}) collective-permute-start(f32[8,128]{1,0:T(8,128)S(1)} %coarse.1.refs_1_), channel_id=1, source_target_pairs={{0,1},{1,2},{2,3},{3,0},{4,5},{5,6},{6,7},{7,4},{8,9},{9,10},{10,1... | collective-permute-start | bytes 12296 | tf_op jit(solution)/shard_map/ppermute | solution.py:765

commit v2 on v1

--- a/solution.py
+++ b/solution.py
@@ -9,11 +9,13 @@
 from jax.experimental.pallas import tpu as pltpu
 from jax.sharding import PartitionSpec as P
 
+
 NF = 8
 NM = 4
 NC = 2
 LANES = 128
 SUB = 8
+MAX_EVERYWHERE = 2 << 20
 SIGMA = 0.55 / 0.45
 RHO0 = 1.0 / SIGMA
 RHO1 = 1.0 / (2.0 * SIGMA - RHO0)
@@ -34,7 +36,7 @@
     node_list = []
     for index in range(points):
         guess = -math.cos(math.pi * index / degree)
-        for sweep in range(100):
+        for _ in range(100):
             high_val, low_val = legendre_pair(guess, degree)
             guess = guess - (guess * high_val - low_val) / (points * high_val)
         node_list.append(guess)
@@ -127,7 +129,7 @@
 
 
 TABLE, TINDEX = build_tables()
-MASK_Y_LO, MASK_Y_HI, MASK_Z_LO, MASK_Z_HI, FAC_Y_LO, FAC_Y_HI, DEV_ID, TOP_ROW = range(8)
+MASK_Y_LO, MASK_Y_HI, MASK_Z_LO, MASK_Z_HI, FAC_Y_LO, FAC_Y_HI, TOP_ROW, NEXT_Z = range(8)
 
 
 class Geo:
@@ -140,6 +142,25 @@
         self.half = gy // 2 if gy % 2 == 0 else gy
         self.cores = gy // self.half
         self.chunks = self.lanes // LANES
+        self.mid = 1
+
+    def window(self, nz, mid=1):
+        out = Geo(self.gx, self.gy, self.cy, self.cz, nz)
+        out.mid = mid
+        return out
+
+    def owners(self, everywhere):
+        lane = np.arange(self.lanes)
+        y = (lane // self.cz) % self.wy
+        x = lane // (self.cz * self.wy)
+        last = x * self.gy + self.gy - 1
+        if everywhere:
+            parts = [zb * self.planes + lane // self.ne for zb in range(self.nz)]
+            zb = self.wy - 1 - y
+            parts.append(np.where(zb < self.nz, zb * self.planes + last, -1))
+        else:
+            parts = [lane // self.ne, np.where(y == self.wy - 1, last, -1)]
+        return np.tile(np.concatenate(parts).astype(np.float32), (SUB, 1))
 
     def masks(self):
         lane = np.arange(self.lanes)
@@ -152,8 +173,8 @@
         out[MASK_Z_HI] = z < self.cz - 1
         out[FAC_Y_LO] = np.where(y > 0, 0.5, 1.0)
         out[FAC_Y_HI] = np.where(y < self.wy - 1, 0.5, 1.0)
-        out[DEV_ID] = lane // self.ne
         out[TOP_ROW] = y == self.wy - 1
+        out[NEXT_Z] = z < self.cz // 2
         return out
 
 
@@ -182,14 +203,6 @@
         return carry
 
     lax.fori_loop(0, geo.nz * geo.chunks, step, 0)
-
-
-def loop(count, body):
-    def step(pos, carry):
-        body(pos)
-        return carry
-
-    lax.fori_loop(0, count, step, 0)
 
 
 def rows8(pos):
@@ -329,9 +342,12 @@
     for_tiles(geo, tile)
 
 
+def scales(ref, level):
+    return ref[2 * level : 2 * level + 1, :], ref[2 * level + 1 : 2 * level + 2, :]
+
+
 def first_smooth(res, inv, cur, tmp, mref, gref, tref, geo, level, top):
-    first = 1.0 / (0.55 * top)
-    second = 2.0 * RHO1 / (0.45 * top)
+    first, second = top
 
     def start(zb, ch, row):
         value = 1.0 / tmp[zb, ch, row, :]
@@ -354,8 +370,7 @@
 
 
 def next_smooth(res, inv, cur, step, tmp, mref, gref, tref, geo, level, top):
-    first = 1.0 / (0.55 * top)
-    second = 2.0 * RHO1 / (0.45 * top)
+    first, second = top
     apply_local(cur, tmp, gref, tref, geo, level)
     gather_sum(tmp, mref, geo, level.n)
 
@@ -409,7 +424,7 @@
     for_tiles(geo, body)
 
 
-def prolong_add(src, cur, tref, geo, nf, nc, table, name):
+def prolong_add(src, base, cur, tref, geo, nf, nc, table, name):
     def body(zb, ch):
         ln = lane_ds(ch)
         columns = [tab(tref, name, c) for c in range(nc)]
@@ -423,7 +438,7 @@
             mixed = combine([part[a][b] for a in range(nc)], table)
             for a in range(nf):
                 row = rows8(a * nf + b)
-                cur[zb, ch, row, :] = cur[zb, ch, row, :] + mixed[a]
+                cur[zb, ch, row, :] = base[zb, ch, row, :] + mixed[a]
 
     for_tiles(geo, body)
 
@@ -460,40 +475,92 @@
     return piece
 
 
-def pack_kernel(residual, geometry, out, *, geo):
+def pack_kernel(
+    residual, geometry, factor, ids, eig, block, rows, keep, give, scale, metric, names, tops,
+    sems, *, geo,
+):
     words = NF**3 // LANES
-    for blk in range(words):
-        out[pl.ds(blk * geo.ne, geo.ne), :] = residual[:, pl.ds(blk * LANES, LANES)]
-    factors = [geometry[:, 0, y, :] for y in range(geo.cy)]
+    nblk = ids.shape[-1]
+    base, kept, given = rows.shape[0], keep.shape[0], nblk * geo.cz - keep.shape[0]
+    pieces = [
+        (
+            residual.at[:, pl.ds(blk * LANES, LANES)],
+            block.at[pl.ds(blk * geo.ne, geo.ne), :],
+        )
+        for blk in range(words)
+    ]
+    pieces += [
+        (geometry, metric),
+        (ids, names),
+        (eig, tops),
+        (factor.at[pl.ds(0, base), :], rows),
+        (factor.at[pl.ds(base, kept), :], keep),
+        (factor.at[pl.ds(base + kept, given), :], give.at[pl.ds(0, given), :]),
+    ]
+    copies = [
+        pltpu.make_async_copy(source, target, sems.at[pos])
+        for pos, (source, target) in enumerate(pieces)
+    ]
+    for copy in copies:
+        copy.start()
+    if given < kept:
+        give[pl.ds(given, kept - given), :] = jnp.zeros((kept - given, LANES), jnp.float32)
+    for copy in copies:
+        copy.wait()
+    lines = []
+    for level in range(2):
+        lines.append(jnp.full((1, LANES), 1.0 / (0.55 * tops[level]), jnp.float32))
+        lines.append(jnp.full((1, LANES), 2.0 * RHO1 / (0.45 * tops[level]), jnp.float32))
+    lines.append(jnp.zeros((SUB - 4, LANES), jnp.float32))
+    scale[...] = jnp.concatenate(lines, axis=0)
+    factors = [metric[:, 0, y, :] for y in range(geo.cy)]
     factors.append(jnp.zeros((3, LANES - geo.ne), jnp.float32))
-    out[pl.ds(words * geo.ne, SUB), :] = jnp.concatenate(
-        [jnp.concatenate(factors, axis=1), jnp.zeros((SUB - 3, LANES), jnp.float32)], axis=0
+    line = names[0, 0].astype(jnp.float32)
+    line = jnp.concatenate([line, jnp.zeros((1, LANES - nblk), jnp.float32)], axis=1)
+    block[pl.ds(words * geo.ne, SUB), :] = jnp.concatenate(
+        [jnp.concatenate(factors, axis=1), line, jnp.zeros((SUB - 4, LANES), jnp.float32)],
+        axis=0,
     )
 
 
-def factor_kernel(own, par, xhi, xlo, labels, *, geo, nblk):
+def mark_kernel(value, out):
+    out[...] = value[...]
+
+
+def factor_kernel(own, par, xhi, xlo, *, geo, nblk, everywhere):
     piece = pieces_of(own, par, geo)
     devices = [(ix, iy) for ix in range(geo.gx) for iy in range(geo.gy)]
-
-    def start(slot, k):
-        return (slot * nblk + k) * geo.cz
+    size = own.shape[1] // (geo.nz if everywhere else 1)
+    blocks = range(geo.nz if everywhere else 1)
+    kept = (nblk + 1) // 2
+    tops = geo.cy * nblk * geo.cz
+
+    def top(zb, ix, k):
+        side, pos = (1, k) if k < kept else (2, k - kept)
+        return piece(ix, geo.gy - side, zb * size + tops + pos * geo.cz, geo.cz)
 
     for k in range(nblk):
         rows = [
-            piece(ix, iy, start(slot, k), geo.cz) for ix, iy in devices for slot in range(geo.cy)
+            piece(ix, iy, zb * size + (slot * nblk + k) * geo.cz, geo.cz)
+            for zb in blocks
+            for ix, iy in devices
+            for slot in range(geo.cy)
         ]
         for ix in range(geo.gx):
-            rows.append(jnp.zeros(((geo.wy - 1) * geo.cz, LANES), jnp.float32))
-            rows.append(piece(ix, geo.gy - 1, start(geo.cy, k), geo.cz))
+            for y in range(geo.wy):
+                zb = geo.wy - 1 - y
+                if zb in blocks:
+                    rows.append(top(zb, ix, k))
+                else:
+                    rows.append(jnp.zeros((geo.cz, LANES), jnp.float32))
         high, rest = split(jnp.concatenate(rows, axis=0))
         xhi[k] = high
         xlo[k] = rest
-    for pos, (ix, iy) in enumerate(devices):
-        labels[pl.ds(pos, 1), :] = piece(ix, iy, start(geo.cy + 1, 0), SUB)[0:1]
-
-
-def down_kernel(own, par, eig, mref, tref, xhi, xlo, labels, *refs, geo, nblk, prow):
-    res, inv, cur, resm, invm, curm, gref, send, tmp, tmpm, low, buf = refs
+
+
+def fine_kernel(
+    own, par, eig, mref, tref, res, inv, cur, resm, gref, labels, tmp, buf, *, geo, prow, everywhere
+):
     piece = pieces_of(own, par, geo)
     devices = [(ix, iy) for ix in range(geo.gx) for iy in range(geo.gy)]
     per_chunk = LANES // geo.ne
@@ -507,144 +574,202 @@
                 res[zb, ch, pl.ds(blk * LANES, LANES), :] = square.T
             total = None
             for pos, (ix, iy) in enumerate(group):
-                part = roll(piece(ix, iy, zb * prow + words * geo.ne, SUB), pos * geo.ne)
+                part = piece(ix, iy, zb * prow + words * geo.ne, SUB)
+                if everywhere or zb == geo.mid:
+                    row = (zb if everywhere else 0) * geo.planes + ix * geo.gy + iy
+                    labels[pl.ds(row, 1), :] = part[3:4]
+                part = roll(part, pos * geo.ne)
                 total = part if total is None else total + part
             gref[zb, ch] = total
     gather_sum(res, mref, geo, NF)
     local_diagonal(tmp, gref, tref, geo, FINE)
     gather_sum(tmp, mref, geo, NF)
-    first_smooth(res, inv, cur, tmp, mref, gref, tref, geo, FINE, eig[0])
+    first_smooth(res, inv, cur, tmp, mref, gref, tref, geo, FINE, scales(eig, 0))
     restrict(res, tmp, resm, mref, tref, geo, NF, NM, UP_F, "rz8", buf)
     gather_sum(resm, mref, geo, NM)
+
+
+def merge(src, dst, mref, geo):
+    def body(pos):
+        pos = pl.multiple_of(pos * SUB, SUB)
+        for ch in range(geo.chunks):
+            low_half = mref[NEXT_Z : NEXT_Z + 1, lane_ds(ch)] > 0.5
+            row = pl.ds(pos, SUB)
+            dst[0, ch, row, :] = src[geo.mid, ch, row, :]
+            dst[1, ch, row, :] = jnp.where(
+                low_half, src[geo.mid + 1, ch, row, :], src[geo.mid - 1, ch, row, :]
+            )
+
+    count = src.shape[2] // SUB
+    lax.fori_loop(0, count, lambda pos, carry: (body(pos), carry)[1], 0, unroll=min(count, 16))
+
+
+def middle_kernel(*refs, geo, everywhere):
+    res, inv, cur, resm, gref, eig, mref, tref = refs[:8]
+    merged, owned = refs[8:15], refs[15]
+    invm, curm, tmpm, low, buf = refs[16:]
     local_diagonal(tmpm, gref, tref, geo, MID)
     gather_sum(tmpm, mref, geo, NM)
-    first_smooth(resm, invm, curm, tmpm, mref, gref, tref, geo, MID, eig[1])
+    first_smooth(resm, invm, curm, tmpm, mref, gref, tref, geo, MID, scales(eig, 1))
     restrict(resm, tmpm, low, mref, tref, geo, NM, NC, UP_C, "rz4", buf)
-
-    mid = geo.nz // 2
     z_lo = mref[MASK_Z_LO : MASK_Z_LO + 1, :] > 0.5
     y_lo = mref[MASK_Y_LO : MASK_Y_LO + 1, :]
     top = mref[TOP_ROW : TOP_ROW + 1, :]
+    xs = geo.wy * geo.cz
 
     def node(zb, a, b, c):
         return wide_load(low, zb, pl.ds((a * NC + b) * SUB + c, 1), geo)
 
-    grid = [
-        [
-            node(mid, a, b, 0)
-            + jnp.where(
-                z_lo, roll(node(mid, a, b, 1), 1), roll(node(mid - 1, a, b, 1), -(geo.cz - 1))
-            )
-            for b in range(NC)
-        ]
-        for a in range(NC)
-    ]
-    xs = geo.wy * geo.cz
-    floor = [grid[a][0] + y_lo * roll(grid[a][1], geo.cz) for a in range(NC)]
-    base = floor[0] + roll(floor[1], xs)
-    ceil = top * (grid[0][1] + roll(grid[1][1], xs))
-    which = mref[DEV_ID : DEV_ID + 1, :]
-    lane_dev = jnp.broadcast_to(which, (geo.planes, geo.lanes))
-    row_dev = lax.broadcasted_iota(jnp.int32, (geo.planes, geo.lanes), 0).astype(jnp.float32)
-    mine = lane_dev == row_dev
-    owned = jnp.concatenate(
-        [jnp.where(mine, base, 0.0), jnp.where(mine, ceil, 0.0)], axis=1
+    def along_z(zb, a, b):
+        before = roll(node((zb - 1) % geo.nz, a, b, 1), -(geo.cz - 1))
+        return node(zb, a, b, 0) + jnp.where(z_lo, roll(node(zb, a, b, 1), 1), before)
+
+    tops = None
+    blocks = range(geo.nz) if everywhere else [geo.mid]
+    for pos, zb in enumerate(blocks):
+        grid = [[along_z(zb, a, b) for b in range(NC)] for a in range(NC)]
+        floor = [grid[a][0] + y_lo * roll(grid[a][1], geo.cz) for a in range(NC)]
+        owned[:, pl.ds(pos * geo.lanes, geo.lanes)] = jnp.broadcast_to(
+            floor[0] + roll(floor[1], xs), (SUB, geo.lanes)
+        )
+        ceil = top * (grid[0][1] + roll(grid[1][1], xs))
+        ceil = roll(ceil, -geo.cz * pos)
+        tops = ceil if tops is None else tops + ceil
+    owned[:, pl.ds(len(blocks) * geo.lanes, geo.lanes)] = jnp.broadcast_to(
+        tops, (SUB, geo.lanes)
     )
-    for k in range(nblk):
-        send[:, pl.ds(k * LANES, LANES)] = dot3(owned, xhi[k], xlo[k], ((1,), (0,)))
+    for source, target in zip((res, inv, cur, resm, invm, curm, gref), merged):
+        merge(source, target, mref, geo)
+
+
+def owner_mask(owners, count):
+    width = owners.shape[1]
+    row = lax.broadcasted_iota(jnp.int32, (count, width), 0).astype(jnp.float32)
+    return jnp.broadcast_to(owners[0:1, :], (count, width)) == row
+
+
+def contributions(owned, owners, xhi, xlo, nblk, count):
+    spread = jnp.broadcast_to(owned[0:1, :], (count, owned.shape[1]))
+    spread = jnp.where(owner_mask(owners, count), spread, 0.0)
+    return [dot3(spread, xhi[k], xlo[k], ((1,), (0,))) for k in range(nblk)]
+
+
+def pick_columns(values, labels, own_labels, nblk):
+    count = own_labels.shape[0]
+    every = labels.shape[0]
+    id_rows = jnp.concatenate([own_labels[:, k : k + 1] for k in range(nblk)], axis=0)
+    picked = None
+    per_step = nblk if nblk * every <= 1024 else 1
+    for k0 in range(0, nblk, per_step):
+        ks = range(k0, k0 + per_step)
+        cols = jnp.concatenate([labels[:, k : k + 1] for k in ks], axis=0)
+        id_lanes = jnp.broadcast_to(cols, (cols.shape[0], LANES)).T[0:1]
+        hit = (id_rows == id_lanes).astype(jnp.bfloat16)
+        high, rest = split(jnp.concatenate([values[k] for k in ks], axis=0))
+        part = dot(hit, high, ((1,), (0,))) + dot(hit, rest, ((1,), (0,)))
+        picked = part if picked is None else picked + part
+    return [picked[k * count : (k + 1) * count] for k in range(nblk)]
+
+
+def solve_rows(picked, owners, xhi, xlo):
+    full = None
+    for k, value in enumerate(picked):
+        part = dot3(value, xhi[k], xlo[k], ((1,), (1,)))
+        full = part if full is None else full + part
+    mine = owner_mask(owners, full.shape[0])
+    return jnp.sum(jnp.where(mine, full, 0.0), axis=0, keepdims=True)
+
+
+def send_kernel(owned, owners, xhi, xlo, labels, send, *, geo, nblk):
+    for k, value in enumerate(contributions(owned, owners, xhi, xlo, nblk, geo.planes)):
+        send[:, pl.ds(k * LANES, LANES)] = value
     send[:, pl.ds(nblk * LANES, LANES)] = labels[...]
 
 
 def coarse_kernel(*refs, geo, nblk, peers):
     parts = refs[:peers]
-    xhi, xlo, mref, out = refs[peers:]
-    own_ids = parts[0][:, pl.ds(nblk * LANES, LANES)]
-    id_rows = jnp.concatenate([own_ids[:, k : k + 1] for k in range(nblk)], axis=0)
-    picked = None
-    per_step = nblk if nblk * peers * geo.planes <= 1024 else 1
-    for k0 in range(0, nblk, per_step):
-        ks = range(k0, k0 + per_step)
-        values = jnp.concatenate(
-            [parts[p][:, pl.ds(k * LANES, LANES)] for k in ks for p in range(peers)], axis=0
-        )
-        cols = jnp.concatenate(
-            [parts[p][:, pl.ds(nblk * LANES, LANES)][:, k : k + 1] for k in ks for p in range(peers)],
-            axis=0,
-        )
-        id_lanes = jnp.broadcast_to(cols, (cols.shape[0], LANES)).T[0:1]
-        hit = (id_rows == id_lanes).astype(jnp.bfloat16)
-        high, rest = split(values)
-        part = dot(hit, high, ((1,), (0,))) + dot(hit, rest, ((1,), (0,)))
-        picked = part if picked is None else picked + part
-    full = None
-    for k in range(nblk):
-        part = dot3(
-            picked[k * geo.planes : (k + 1) * geo.planes], xhi[k], xlo[k], ((1,), (1,))
-        )
-        full = part if full is None else full + part
-    which = mref[DEV_ID : DEV_ID + 1, :]
-    lane_dev = jnp.broadcast_to(which, (geo.planes, geo.lanes))
-    row_dev = lax.broadcasted_iota(jnp.int32, (geo.planes, geo.lanes), 0).astype(jnp.float32)
-    mine = lane_dev == row_dev
-    for pos in range(2):
-        value = full[:, pos * geo.lanes : (pos + 1) * geo.lanes]
-        out[pl.ds(pos, 1), :] = jnp.sum(
-            jnp.where(mine, value, 0.0), axis=0, keepdims=True
-        )
-
-
-def up_kernel(*refs, geo):
-    solved = refs[: geo.nz]
-    res, inv, cur_in, resm, invm, curm_in, gref, eig, mref, tref = refs[geo.nz : geo.nz + 10]
-    out, cur, curm, tmp, tmpm, step, stepm, low, turned = refs[geo.nz + 10 :]
+    xhi, xlo, owners, out = refs[peers:]
+    values = [
+        jnp.concatenate([part[:, pl.ds(k * LANES, LANES)] for part in parts], axis=0)
+        for k in range(nblk + 1)
+    ]
+    own_labels = parts[0][:, pl.ds(nblk * LANES, LANES)]
+    picked = pick_columns(values[:nblk], values[nblk], own_labels, nblk)
+    solved = solve_rows(picked, owners, xhi, xlo)
+    out[pl.ds(0, 1), :] = solved[:, : geo.lanes]
+    out[pl.ds(1, 1), :] = solved[:, geo.lanes :]
+
+
+def rise(solved, state, consts, out, scratch, geo):
+    res, inv, cur_in, resm, invm, curm_in, gref = state
+    eig, mref, tref = consts
+    cur, curm, tmp, tmpm, step, stepm, low, turned = scratch
     y_hi = mref[MASK_Y_HI : MASK_Y_HI + 1, :] > 0.5
     z_hi = mref[MASK_Z_HI : MASK_Z_HI + 1, :] > 0.5
     xs = geo.wy * geo.cz
     levels = []
-    for zb in range(geo.nz):
-        base = solved[zb][0:1, :]
-        ceil = solved[zb][1:2, :]
+    for base, ceil in solved:
         upper = jnp.where(y_hi, roll(base, -geo.cz), ceil)
         flat = [base, upper]
         levels.append([flat, [roll(v, -xs) for v in flat]])
-    for zb in range(geo.nz):
-        for a in range(NC):
-            for b in range(NC):
-                here = levels[zb][a][b]
-                after = levels[(zb + 1) % geo.nz][a][b]
-                row = (a * NC + b) * SUB
-                wide_store(low, zb, pl.ds(row, 1), geo, here)
-                deep = jnp.where(z_hi, roll(here, -1), roll(after, geo.cz - 1))
-                wide_store(low, zb, pl.ds(row + 1, 1), geo, deep)
-
-    def copy_mid(zb, ch, row):
-        curm[zb, ch, row, :] = curm_in[zb, ch, row, :]
-
-    def copy_fine(zb, ch, row):
-        cur[zb, ch, row, :] = cur_in[zb, ch, row, :]
-
-    each_row(geo, NM, copy_mid)
-    each_row(geo, NF, copy_fine)
-    prolong_add(low, curm, tref, geo, NM, NC, UP_C, "pz4")
-    next_smooth(resm, invm, curm, stepm, tmpm, mref, gref, tref, geo, MID, eig[1])
-    prolong_add(curm, cur, tref, geo, NF, NM, UP_F, "pz8")
-    next_smooth(res, inv, cur, step, tmp, mref, gref, tref, geo, FINE, eig[0])
+    low_half = mref[NEXT_Z : NEXT_Z + 1, :] > 0.5
+    for a in range(NC):
+        for b in range(NC):
+            flat = [levels[zb][a][b] for zb in range(3)]
+            deep = [
+                jnp.where(z_hi, roll(flat[zb], -1), roll(flat[(zb + 1) % 3], geo.cz - 1))
+                for zb in range(3)
+            ]
+            for c, value in enumerate((flat, deep)):
+                row = pl.ds((a * NC + b) * SUB + c, 1)
+                wide_store(low, 0, row, geo, value[1])
+                wide_store(low, 1, row, geo, jnp.where(low_half, value[2], value[0]))
+    prolong_add(low, curm_in, curm, tref, geo, NM, NC, UP_C, "pz4")
+    next_smooth(resm, invm, curm, stepm, tmpm, mref, gref, tref, geo, MID, scales(eig, 1))
+    prolong_add(curm, cur_in, cur, tref, geo, NF, NM, UP_F, "pz8")
+    next_smooth(res, inv, cur, step, tmp, mref, gref, tref, geo, FINE, scales(eig, 0))
     words = NF**3 // LANES
-    mid = geo.nz // 2
     for ch in range(geo.chunks):
         for blk in range(words):
             turned[pl.ds(ch * LANES, LANES), pl.ds(blk * LANES, LANES)] = cur[
-                mid, ch, pl.ds(blk * LANES, LANES), :
+                geo.mid, ch, pl.ds(blk * LANES, LANES), :
             ].T
     my = lax.axis_index("gx") * geo.gy + lax.axis_index("gy")
     out[...] = turned[pl.ds(pl.multiple_of(my * geo.ne, SUB), geo.ne), :]
 
 
-def on_device(residual_in, geometry, eig_top, coarse_rows, block_ids, sizes):
+def up_kernel(*refs, geo):
+    blocks = [(ref[0:1, :], ref[1:2, :]) for ref in refs[:3]]
+    rest = refs[3:]
+    rise(blocks, rest[:7], rest[7:10], rest[10], rest[11:], geo)
+
+
+def finish_kernel(owned, owners, xhi, xlo, labels, *refs, geo, nblk):
+    values = contributions(owned, owners, xhi, xlo, nblk, labels.shape[0])
+    names = labels[...]
+    picked = pick_columns(values, names, names, nblk)
+    solved = solve_rows(picked, owners, xhi, xlo)
+    near = geo.window(2, 0)
+    tops = solved[:, geo.nz * geo.lanes :]
+    blocks = [
+        (solved[:, zb * geo.lanes : (zb + 1) * geo.lanes], roll(tops, geo.cz * zb))
+        for zb in range(3)
+    ]
+    rise(blocks, refs[:7], refs[7:10], refs[10], refs[11:], near)
+
+
+def holds_all(gx, gy, gz, cy, cz):
+    nodes = gx * gy * gz * cy * cz * NF**3
+    return 3 <= gz <= gy * cy and nodes * 4 <= MAX_EVERYWHERE
+
+
+def on_device(residual_in, geometry, eig_top, coarse_rows, block_ids, sizes, everywhere):
     gx, gy, gz = sizes
     cx, cy, cz = residual_in.shape[:3]
     nblk = coarse_rows.shape[3]
     geo = Geo(gx, gy, cy, cz, 3)
+    if everywhere:
+        geo = geo.window(gz)
     ok = cx == 1 and cz % SUB == 0 and LANES % geo.ne == 0 and geo.lanes % LANES == 0
     if not ok or coarse_rows.shape[4] != LANES or geo.planes % SUB:
         raise ValueError("block shape")
@@ -658,7 +783,7 @@
     def shape(dims, kind=f32):
         return jax.ShapeDtypeStruct(dims, kind)
 
-    def call(body, name, specs, outs, scratch, *operands):
+    def call(body, specs, outs, scratch, *operands, extra=()):
         kept = list(operands) + list(outs) + list(scratch)
         total = sum(math.prod(a.shape) * a.dtype.itemsize for a in kept)
         return pl.pallas_call(
@@ -666,11 +791,10 @@
             out_shape=list(outs),
             in_specs=specs,
             out_specs=[vmem] * len(outs),
-            scratch_shapes=[pltpu.VMEM(a.shape, a.dtype) for a in scratch],
+            scratch_shapes=[pltpu.VMEM(a.shape, a.dtype) for a in scratch] + list(extra),
             compiler_params=pltpu.CompilerParams(
                 vmem_limit_bytes=min(total + (3 << 20), 60 << 20)
             ),
-            name=name,
         )(*operands)
 
     def rank(ix, ih, core):
@@ -688,90 +812,129 @@
                         for core in range(cores)
                     ]
                     parts.append(lax.ppermute(value, ("gx", "gy"), pairs))
-        return jnp.stack(parts)
+        return parts
 
     def between_cores(value):
         if cores == 1:
             return value
         return lax.ppermute(value, "gy", [(i, i ^ 1) for i in range(gy)])
 
-    (block,) = call(
+    hbm = pl.BlockSpec(memory_space=pltpu.HBM)
+    factor = coarse_rows.reshape(cy + 1, cz, nblk, LANES).transpose(0, 2, 1, 3)
+    part = shape(((nblk + 1) // 2 * cz, LANES))
+    block, factor, keep, give, scale = call(
         functools.partial(pack_kernel, geo=geo),
-        "pack",
+        [hbm] * 5,
+        [shape((prow, LANES)), shape((cy * nblk * cz, LANES)), part, part, shape((SUB, LANES))],
+        [shape(geometry.shape), jax.ShapeDtypeStruct(block_ids.shape, block_ids.dtype)],
+        *[
+            pltpu.with_memory_space_constraint(value, pltpu.HBM)
+            for value in (
+                residual_in.reshape(geo.ne, NF**3),
+                geometry,
+                factor.reshape(slots * nblk, LANES),
+                block_ids,
+                eig_top,
+            )
+        ],
+        extra=[pltpu.SMEM((2,), f32), pltpu.SemaphoreType.DMA((NF**3 // LANES + 6,))],
+    )
+    marks = [call(mark_kernel, [vmem], [shape((SUB, LANES))], [], scale)[0] for _ in range(2)]
+
+    def from_block(value, offset):
+        return lax.ppermute(value, "gz", [((i + offset) % gz, i) for i in range(gz)])
+
+    def along_z(value):
+        order = list(range(2, geo.nz - 1)) + [-1, 1]
+        got = {offset: from_block(value, offset) for offset in order}
+        got[0] = value
+        return jnp.concatenate([got[offset] for offset in sorted(got)], axis=0)
+
+    taken = lax.ppermute(give, "gy", [(gy - 1, gy - 2)])
+    keep = jnp.where(lax.axis_index("gy") == gy - 1, keep, taken)
+    factor = jnp.concatenate([factor, keep], axis=0)
+    column = along_z(block)
+    if everywhere:
+        factor = along_z(factor)
+    own = jnp.stack(across_chips(column))
+    par = between_cores(own)
+    factor_own = across_chips(factor)
+
+    masks = jnp.asarray(geo.masks())
+    owners = jnp.asarray(geo.owners(everywhere))
+    table = jnp.asarray(TABLE)
+    count = geo.planes * (geo.nz if everywhere else 1)
+    width = owners.shape[1]
+    near = geo.window(2, 0)
+
+    def field(where, points):
+        return shape((where.nz, where.chunks, points * points * SUB, LANES))
+
+    fine, middle, lowest = (field(geo, points) for points in (NF, NM, NC))
+    buf = shape((1, 1, NM * NM * SUB, LANES))
+    metric = shape((geo.nz, geo.chunks, SUB, LANES))
+    res, inv, cur, resm, gfac, names = call(
+        functools.partial(fine_kernel, geo=geo, prow=prow, everywhere=everywhere),
+        [vmem] * 5,
+        [fine] * 3 + [middle, metric, shape((count, LANES))],
+        [fine, buf],
+        own, par, marks[1], masks, table,
+    )
+    factor_par = jnp.stack([between_cores(part) for part in factor_own])
+    factor_own = jnp.stack(factor_own)
+    fine2, middle2 = (field(near, points) for points in (NF, NM))
+    *merged, owned = call(
+        functools.partial(middle_kernel, geo=geo, everywhere=everywhere),
+        [vmem] * 8,
+        [fine2] * 3
+        + [middle2] * 3
+        + [shape((2, geo.chunks, SUB, LANES)), shape((SUB, width))],
+        [middle, middle, middle, lowest, buf],
+        res, inv, cur, resm, gfac, marks[0], masks, table,
+    )
+    wide = shape((nblk, width, LANES), jnp.bfloat16)
+    xhi, xlo = call(
+        functools.partial(factor_kernel, geo=geo, nblk=nblk, everywhere=everywhere),
         [vmem, vmem],
-        [shape((prow, LANES))],
+        [wide, wide],
         [],
-        residual_in.reshape(geo.ne, NF**3),
-        geometry,
+        factor_own, factor_par,
     )
-    ring = [(i, (i + 1) % gz) for i in range(gz)]
-    back = [((i + 1) % gz, i) for i in range(gz)]
-    before = lax.ppermute(block, "gz", ring)
-    after = lax.ppermute(block, "gz", back)
-
-    labels = jnp.pad(
-        block_ids.reshape(1, nblk).astype(f32), ((0, SUB - 1), (0, LANES - nblk))
+    state = (*merged, scale, masks, table)
+    kinds = [vmem] * 10
+    final = shape((geo.ne, NF**3))
+    scratch = [fine2, middle2] * 3 + [field(near, NC), shape((geo.lanes, NF**3))]
+    if everywhere:
+        (out,) = call(
+            functools.partial(finish_kernel, geo=geo, nblk=nblk),
+            [vmem] * 5 + kinds,
+            [final],
+            scratch,
+            owned, owners, xhi, xlo, names, *state,
+        )
+        return out.reshape(cx, cy, cz, NF**3)
+
+    (send,) = call(
+        functools.partial(send_kernel, geo=geo, nblk=nblk),
+        [vmem] * 5,
+        [shape((geo.planes, (nblk + 1) * LANES))],
+        [],
+        owned, owners, xhi, xlo, names,
     )
-    factor = coarse_rows.reshape(cy + 1, cz, nblk, LANES).transpose(0, 2, 1, 3)
-    factor = jnp.concatenate([factor.reshape(slots * nblk, LANES), labels], axis=0)
-    factor_own = across_chips(factor)
-    factor_par = between_cores(factor_own)
-
-    own = across_chips(jnp.concatenate([before, block, after], axis=0))
-    par = between_cores(own)
-
-    masks = jnp.asarray(geo.masks())
-    table = jnp.asarray(TABLE)
-    fine = shape((geo.nz, geo.chunks, NF * NF * SUB, LANES))
-    middle = shape((geo.nz, geo.chunks, NM * NM * SUB, LANES))
-    lowest = shape((geo.nz, geo.chunks, NC * NC * SUB, LANES))
-    wide = shape((nblk, 2 * geo.lanes, LANES), jnp.bfloat16)
-
-    xhi, xlo, names = call(
-        functools.partial(factor_kernel, geo=geo, nblk=nblk),
-        "factor",
-        [vmem, vmem],
-        [wide, wide, shape((geo.planes, LANES))],
-        [],
-        factor_own,
-        factor_par,
-    )
-    res, inv, cur, resm, invm, curm, gfac, send = call(
-        functools.partial(down_kernel, geo=geo, nblk=nblk, prow=prow),
-        "down",
-        [vmem, vmem, smem] + [vmem] * 5,
-        [fine] * 3
-        + [middle] * 3
-        + [shape((geo.nz, geo.chunks, SUB, LANES)), shape((geo.planes, (nblk + 1) * LANES))],
-        [fine, middle, lowest, shape((1, 1, NM * NM * SUB, LANES))],
-        own, par, eig_top, masks, table, xhi, xlo, names,
-    )
-
-    parts = [send]
-    for d in range(gz - 1, 0, -1):
-        pairs = [((i + d) % gz, i) for i in range(gz)]
-        if gz & (gz - 1) == 0:
-            pairs = [(i ^ d, i) for i in range(gz)]
-        parts.append(lax.ppermute(send, "gz", pairs))
+    parts = [send] + [from_block(send, offset) for offset in range(1, gz)]
     (solved,) = call(
         functools.partial(coarse_kernel, geo=geo, nblk=nblk, peers=gz),
-        "coarse",
         [vmem] * (gz + 3),
         [shape((SUB, geo.lanes))],
         [],
-        *parts, xhi, xlo, masks,
+        *parts, xhi, xlo, owners,
     )
-
-    solved_before = lax.ppermute(solved, "gz", ring)
-    solved_after = lax.ppermute(solved, "gz", back)
     (out,) = call(
         functools.partial(up_kernel, geo=geo),
-        "up",
-        [vmem] * (geo.nz + 7) + [smem, vmem, vmem],
-        [shape((geo.ne, NF**3))],
-        [fine, middle, fine, middle, fine, middle, lowest, shape((geo.lanes, NF**3))],
-        solved_before, solved, solved_after,
-        res, inv, cur, resm, invm, curm, gfac, eig_top, masks, table,
+        [vmem] * 3 + kinds,
+        [final],
+        scratch,
+        from_block(solved, -1), solved, from_block(solved, 1), *state,
     )
     return out.reshape(cx, cy, cz, NF**3)
 
@@ -786,10 +949,18 @@
         P("gx", "gy", "gz", None),
     )
     out_specs = P("gx", "gy", "gz", None)
-    return jax.shard_map(
-        functools.partial(on_device, sizes=sizes),
-        mesh=mesh,
-        in_specs=in_specs,
-        out_specs=out_specs,
-        check_vma=False,
-    )
+
+    def program(residual_in, geometry, eig_top, coarse_rows, block_ids):
+        gx, gy, gz = sizes
+        cy, cz = residual_in.shape[1] // gy, residual_in.shape[2] // gz
+        everywhere = holds_all(gx, gy, gz, cy, cz)
+
+        def body(*blocks):
+            return on_device(*blocks, sizes=sizes, everywhere=everywhere)
+
+        step = jax.shard_map(
+            body, mesh=mesh, in_specs=in_specs, out_specs=out_specs, check_vma=False
+        )
+        return step(residual_in, geometry, eig_top, coarse_rows, block_ids)
+
+    return program

time: 57.2 us -> 51.8 us (0.906)
  waiting for transfers between devices: 17.9 us -> 12.7 us
  Pallas kernels: 14.5 us -> 15.8 us
  starting transfers between devices: 22.2 us -> 21.4 us
  local copies, waits for them, and re-layouts: 2.11 us -> 1.33 us
    ppermute x7, waiting for transfers between devices: 13.3 us -> 0.99 us  [the longest x6 0.98 us: from_block(): lax.ppermute(value, 'gz', [((i + offset) % gz, i) for i in range(gz)])]
    ppermute x6, waiting for transfers between devices: 3.01 us -> 10.4 us  [across_chips(): parts.append(lax.ppermute(value, ('gx', 'gy'), pairs))]
    ppermute x7, starting transfers between devices: 13.1 us -> 10.9 us  [the longest x6 10.2 us: from_block(): lax.ppermute(value, 'gz', [((i + offset) % gz, i) for i in range(gz)])]
    pallas_call x5 -> x6, Pallas kernels: 14.5 us -> 15.8 us  [call(): pl.pallas_call(body, out_shape=list(outs), in_specs=specs, out_specs=[vme...]
    ppermute x2 -> x5, starting transfers between devices: 0.14 us -> 1.08 us  [between_cores(): return lax.ppermute(value, 'gy', [(i, i ^ 1) for i in range(gy)])]
    unnamed x14 -> x13, local copies, waits for them, and re-layouts: 2.11 us -> 1.32 us
    ppermute x2 -> x5, waiting for transfers between devices: 1.59 us -> 1.27 us  [between_cores(): return lax.ppermute(value, 'gy', [(i, i ^ 1) for i in range(gy)])]
  transfers between devices with their start and end apart: 15 -> 18, of which waited for: 11 -> 7; matrix products, arithmetic and copies ran while one was open for 0% -> 0% of each run, Pallas kernels for 0% -> 1%
where the time goes in v2:
time: 51.8 us; the launch traced here: 51.5 us
  starting transfers between devices  21.4 us (41%)
  Pallas kernels  15.8 us (31%)
  waiting for transfers between devices  12.7 us (25%)
  local copies, waits for them, and re-layouts  1.33 us (3%)
    pallas_call x6, Pallas kernels, call(): pl.pallas_call(body, out_shape=list(outs), in_specs=specs, out_specs=[vme...  15.8 us
    ppermute x6, waiting for transfers between devices, across_chips(): parts.append(lax.ppermute(value, ('gx', 'gy'), pairs))  10.4 us
    ppermute x6, starting transfers between devices, from_block(): lax.ppermute(value, 'gz', [((i + offset) % gz, i) for i in range(gz)])  10.2 us
    ppermute x6, starting transfers between devices, across_chips(): parts.append(lax.ppermute(value, ('gx', 'gy'), pairs))  9.5 us
    unnamed x13, local copies, waits for them, and re-layouts  1.32 us
    ppermute x5, waiting for transfers between devices, between_cores(): return lax.ppermute(value, 'gy', [(i, i ^ 1) for i in range(gy)])  1.27 us
    ppermute x5, starting transfers between devices, between_cores(): return lax.ppermute(value, 'gy', [(i, i ^ 1) for i in range(gy)])  1.08 us
  transfers between devices with their start and end apart: 18, of which 7 were waited for; matrix products, arithmetic and copies ran while one was open for 0% of the time, Pallas kernels for 1%

profile of v2, /device:TPU:0, one launch (start us, length us, event | category | flops | bytes accessed | tf_op | source)
XLA Modules:
  0.0 51.5 jit_solution(5727163594250002332)
XLA Ops:
  0.0 1.1 %shard_map.82 = (f32[72,128]{1,0:T(8,128)S(1)}, f32[96,128]{1,0:T(8,128)S(1)}, f32[24,128]{1,0:T(8,128)S(1)}, f32[24,128]{1,0:T(8,128)S(1)}, f32[8,128]{1,0:T(8,128)S(1)}) custom-call(f32[16,512]{1,0:T(8,128)} %bitcast.32, f32[3,1,2,8]{3,2,1,0:T(2,128)} %geometry.1, f32[144,128]{1,0:T(8,128)} %bitcast.31, s32[1,1,1,6]{3,2,1,0:T(1,128)} %ids.1, f32[2]{0:T(128)} %eig.1), custom_call_target="tpu_custom_call" | custom-call | tf_op jit(solution)/shard_map/pallas_call | solution.py:789
  1.1 0.7 %collective-permute-start.7 = (f32[24,128]{1,0:T(8,128)S(1)}, f32[24,128]{1,0:T(8,128)S(1)}, u32[]{:S(2)}, u32[]{:S(2)}) collective-permute-start(f32[24,128]{1,0:T(8,128)S(1)} %get-tuple-element.36), channel_id=1, source_target_pairs={{12,8},{13,9},{14,10},{15,11},{28,24},{29,25},{30,26},{31,27}} | collective-permute-start | bytes 36872 | tf_op jit(solution)/shard_map/ppermute | solution.py:853
  1.7 3.1 %collective-permute-start = (f32[72,128]{1,0:T(8,128)S(1)}, f32[72,128]{1,0:T(8,128)S(1)}, u32[]{:S(2)}, u32[]{:S(2)}) collective-permute-start(f32[72,128]{1,0:T(8,128)S(1)} %get-tuple-element.26), channel_id=1, source_target_pairs={{3,0},{0,1},{1,2},{2,3},{7,4},{4,5},{5,6},{6,7},{11,8},{8,9},{9,10... | collective-permute-start | bytes 110600 | tf_op jit(solution)/shard_map/ppermute | solution.py:845
  4.8 2.1 %collective-permute-start.1 = (f32[72,128]{1,0:T(8,128)S(1)}, f32[72,128]{1,0:T(8,128)S(1)}, u32[]{:S(2)}, u32[]{:S(2)}) collective-permute-start(f32[72,128]{1,0:T(8,128)S(1)} %get-tuple-element.26), channel_id=1, source_target_pairs={{1,0},{2,1},{3,2},{0,3},{5,4},{6,5},{7,6},{4,7},{9,8},{10,9},{11,1... | collective-permute-start | bytes 110600 | tf_op jit(solution)/shard_map/ppermute | solution.py:845
  6.9 0.9 %collective-permute-start.2 = (f32[72,128]{1,0:T(8,128)S(1)}, f32[72,128]{1,0:T(8,128)S(1)}, u32[]{:S(2)}, u32[]{:S(2)}) collective-permute-start(f32[72,128]{1,0:T(8,128)S(1)} %get-tuple-element.26), channel_id=1, source_target_pairs={{2,0},{3,1},{0,2},{1,3},{6,4},{7,5},{4,6},{5,7},{10,8},{11,9},{8,1... | collective-permute-start | bytes 110600 | tf_op jit(solution)/shard_map/ppermute | solution.py:845
  7.9 0.0 collective-permute-done.7
  7.9 1.6 %collective-permute-start.8 = (f32[120,128]{1,0:T(8,128)S(1)}, f32[120,128]{1,0:T(8,128)S(1)}, u32[]{:S(2)}, u32[]{:S(2)}) collective-permute-start(f32[120,128]{1,0:T(8,128)S(1)} %pad_maximum_fusion.3), channel_id=1, source_target_pairs={{3,0},{0,1},{1,2},{2,3},{7,4},{4,5},{5,6},{6,7},{11,8},{8,9},{9,10... | collective-permute-start | bytes 184328 | tf_op jit(solution)/shard_map/ppermute | solution.py:845
  9.5 2.2 %collective-permute-start.9 = (f32[120,128]{1,0:T(8,128)S(1)}, f32[120,128]{1,0:T(8,128)S(1)}, u32[]{:S(2)}, u32[]{:S(2)}) collective-permute-start(f32[120,128]{1,0:T(8,128)S(1)} %pad_maximum_fusion.3), channel_id=1, source_target_pairs={{1,0},{2,1},{3,2},{0,3},{5,4},{6,5},{7,6},{4,7},{9,8},{10,9},{11,1... | collective-permute-start | bytes 184328 | tf_op jit(solution)/shard_map/ppermute | solution.py:845
  11.8 0.0 collective-permute-done
  11.8 0.2 collective-permute-start.10
  12.0 0.0 collective-permute-done.1
  12.0 0.8 %collective-permute-done.2 = f32[72,128]{1,0:T(8,128)S(1)} collective-permute-done((f32[72,128]{1,0:T(8,128)S(1)}, f32[72,128]{1,0:T(8,128)S(1)}, u32[]{:S(2)}, u32[]{:S(2)}) %collective-permute-start.2) | collective-permute-done | bytes 36896 | tf_op jit(solution)/shard_map/ppermute | solution.py:845
  12.8 3.0 %collective-permute-start.5 = (f32[288,128]{1,0:T(8,128)S(1)}, f32[288,128]{1,0:T(8,128)S(1)}, u32[]{:S(2)}, u32[]{:S(2)}) collective-permute-start(f32[288,128]{1,0:T(8,128)S(1)} %constant_dynamic-update-slice_fusion), channel_id=1, source_target_pairs={{24,0},{28,4},{16,8},{20,12},{8,16},{12,20},{0,24},{4,28},{25,1},{... | collective-permute-start | bytes 442376 | tf_op jit(solution)/shard_map/ppermute | solution.py:814
  15.8 0.5 collective-permute-start.4
  16.3 0.0 collective-permute-done.8
  16.3 0.4 collective-permute-start.3
  16.8 0.0 collective-permute-done.9
  16.8 0.2 collective-permute-done.10
  17.0 4.0 %collective-permute-start.13 = (f32[480,128]{1,0:T(8,128)S(1)}, f32[480,128]{1,0:T(8,128)S(1)}, u32[]{:S(2)}, u32[]{:S(2)}) collective-permute-start(f32[480,128]{1,0:T(8,128)S(1)} %constant_dynamic-update-slice_fusion.4), channel_id=1, source_target_pairs={{24,0},{28,4},{16,8},{20,12},{8,16},{12,20},{0,24},{4,28},{25,1},{... | collective-permute-start | bytes 737288 | tf_op jit(solution)/shard_map/ppermute | solution.py:814
  21.0 0.5 collective-permute-start.12
  21.5 0.0 collective-permute-done.5
  21.5 1.0 %collective-permute-start.11 = (f32[480,128]{1,0:T(8,128)S(1)}, f32[480,128]{1,0:T(8,128)S(1)}, u32[]{:S(2)}, u32[]{:S(2)}) collective-permute-start(f32[480,128]{1,0:T(8,128)S(1)} %constant_dynamic-update-slice_fusion.4), channel_id=1, source_target_pairs={{8,0},{12,4},{0,8},{4,12},{24,16},{28,20},{16,24},{20,28},{9,1},{1... | collective-permute-start | bytes 737288 | tf_op jit(solution)/shard_map/ppermute | solution.py:814
  22.5 1.6 %collective-permute-done.4 = f32[288,128]{1,0:T(8,128)S(1)} collective-permute-done((f32[288,128]{1,0:T(8,128)S(1)}, f32[288,128]{1,0:T(8,128)S(1)}, u32[]{:S(2)}, u32[]{:S(2)}) %collective-permute-start.4) | collective-permute-done | bytes 147488 | tf_op jit(solution)/shard_map/ppermute | solution.py:814
  24.1 0.0 collective-permute-done.3
  24.2 0.1 collective-permute-start.6
  24.2 0.5 collective-permute-start.14
  24.7 4.6 %collective-permute-done.13 = f32[480,128]{1,0:T(8,128)S(1)} collective-permute-done((f32[480,128]{1,0:T(8,128)S(1)}, f32[480,128]{1,0:T(8,128)S(1)}, u32[]{:S(2)}, u32[]{:S(2)}) %collective-permute-start.13) | collective-permute-done | bytes 245792 | tf_op jit(solution)/shard_map/ppermute | solution.py:814
  29.3 0.0 collective-permute-start.17
  29.3 4.2 %collective-permute-done.12 = f32[480,128]{1,0:T(8,128)S(1)} collective-permute-done((f32[480,128]{1,0:T(8,128)S(1)}, f32[480,128]{1,0:T(8,128)S(1)}, u32[]{:S(2)}, u32[]{:S(2)}) %collective-permute-start.12) | collective-permute-done | bytes 245792 | tf_op jit(solution)/shard_map/ppermute | solution.py:814
  33.6 0.0 collective-permute-start.16
  33.6 0.0 collective-permute-done.11
  33.6 0.5 collective-permute-start.15
  34.1 0.1 pad_maximum_fusion.own
  34.1 0.0 collective-permute-done.14
  34.2 0.0 collective-permute-done.17
  34.2 0.9 %collective-permute-done.16 = f32[480,128]{1,0:T(8,128)S(1)} collective-permute-done((f32[480,128]{1,0:T(8,128)S(1)}, f32[480,128]{1,0:T(8,128)S(1)}, u32[]{:S(2)}, u32[]{:S(2)}) %collective-permute-start.16) | collective-permute-done | bytes 245792 | tf_op jit(solution)/shard_map/ppermute | solution.py:820
  35.1 0.4 collective-permute-done.15
  35.4 0.1 pad_maximum_fusion.1.par
  35.5 0.0 copy-start
  35.5 0.0 copy-start.1
  35.5 0.3 shard_map.86
  35.8 0.0 collective-permute-done.6.par
  35.8 0.6 %copy-done = f32[272,128]{1,0:T(8,128)S(1)} copy-done((f32[272,128]{1,0:T(8,128)S(1)}, f32[272,128]{1,0:T(8,128)}, u32[]{:S(2)}) %copy-start) | copy-done | bytes 139288
  36.4 6.2 %shard_map.84 = (f32[4,1,512,128]{3,2,1,0:T(8,128)S(1)}, f32[4,1,512,128]{3,2,1,0:T(8,128)S(1)}, f32[4,1,512,128]{3,2,1,0:T(8,128)S(1)}, f32[4,1,128,128]{3,2,1,...) custom-call(f32[4,288,128]{2,1,0:T(8,128)S(1)} %pad_maximum_fusion.2.own, ...), custom_call_target="tpu_custom_call" | custom-call | tf_op jit(solution)/shard_map/pallas_call | solution.py:789
  42.6 2.0 %shard_map.85 = (f32[2,1,512,128]{3,2,1,0:T(8,128)S(1)}, f32[2,1,512,128]{3,2,1,0:T(8,128)S(1)}, f32[2,1,512,128]{3,2,1,0:T(8,128)S(1)}, f32[2,1,128,128]{3,2,1,...) custom-call(f32[4,1,512,128]{3,2,1,0:T(8,128)S(1)} %get-tuple-elemen, ...), custom_call_target="tpu_custom_call" | custom-call | tf_op jit(solution)/shard_map/pallas_call | solution.py:789
  44.7 0.0 copy-start.2
  44.7 0.7 %copy-done.2 = f32[8,640]{1,0:T(8,128)S(1)} copy-done((f32[8,640]{1,0:T(8,128)S(1)}, f32[8,640]{1,0:T(8,128)}, u32[]{:S(2)}) %copy-start.2) | copy-done | bytes 20504
  45.4 6.1 %shard_map.87 = f32[16,512]{1,0:T(8,128)} custom-call(f32[8,640]{1,0:T(8,128)S(1)} %get-tuple-element.33.owned, f32[8,640]{1,0:T(8,128)S(1)} %copy-done.2, bf16[6,640,128]{2,1,0:T(8,128)(2,1)S(1)} %get-tuple-element.37.xhi, bf16[6,640,128]{2,1,0:T(8,128)(2,1)S(1)} %get-tuple-element.38.xlo, f32[32,128]{1,0:T(8,128)S(1)} %get-tuple-element.39.labels, ...), custom_call_target="tpu_custom_call" | custom-call | tf_op jit(solution)/shard_map/pallas_call | solution.py:789
  (14 shorter events, 0.1 us)
Async XLA Ops:
  1.1 6.8 %collective-permute-start.7 = (f32[24,128]{1,0:T(8,128)S(1)}, f32[24,128]{1,0:T(8,128)S(1)}, u32[]{:S(2)}, u32[]{:S(2)}) collective-permute-start(f32[24,128]{1,0:T(8,128)S(1)} %get-tuple-element.36), channel_id=1, source_target_pairs={{12,8},{13,9},{14,10},{15,11},{28,24},{29,25},{30,26},{31,27}} | collective-permute-start | bytes 36872 | tf_op jit(solution)/shard_map/ppermute | solution.py:853
  1.7 10.0 %collective-permute-start = (f32[72,128]{1,0:T(8,128)S(1)}, f32[72,128]{1,0:T(8,128)S(1)}, u32[]{:S(2)}, u32[]{:S(2)}) collective-permute-start(f32[72,128]{1,0:T(8,128)S(1)} %get-tuple-element.26), channel_id=1, source_target_pairs={{3,0},{0,1},{1,2},{2,3},{7,4},{4,5},{5,6},{6,7},{11,8},{8,9},{9,10... | collective-permute-start | bytes 110600 | tf_op jit(solution)/shard_map/ppermute | solution.py:845
  4.8 7.1 %collective-permute-start.1 = (f32[72,128]{1,0:T(8,128)S(1)}, f32[72,128]{1,0:T(8,128)S(1)}, u32[]{:S(2)}, u32[]{:S(2)}) collective-permute-start(f32[72,128]{1,0:T(8,128)S(1)} %get-tuple-element.26), channel_id=1, source_target_pairs={{1,0},{2,1},{3,2},{0,3},{5,4},{6,5},{7,6},{4,7},{9,8},{10,9},{11,1... | collective-permute-start | bytes 110600 | tf_op jit(solution)/shard_map/ppermute | solution.py:845
  6.9 5.8 %collective-permute-start.2 = (f32[72,128]{1,0:T(8,128)S(1)}, f32[72,128]{1,0:T(8,128)S(1)}, u32[]{:S(2)}, u32[]{:S(2)}) collective-permute-start(f32[72,128]{1,0:T(8,128)S(1)} %get-tuple-element.26), channel_id=1, source_target_pairs={{2,0},{3,1},{0,2},{1,3},{6,4},{7,5},{4,6},{5,7},{10,8},{11,9},{8,1... | collective-permute-start | bytes 110600 | tf_op jit(solution)/shard_map/ppermute | solution.py:845
  7.9 8.4 %collective-permute-start.8 = (f32[120,128]{1,0:T(8,128)S(1)}, f32[120,128]{1,0:T(8,128)S(1)}, u32[]{:S(2)}, u32[]{:S(2)}) collective-permute-start(f32[120,128]{1,0:T(8,128)S(1)} %pad_maximum_fusion.3), channel_id=1, source_target_pairs={{3,0},{0,1},{1,2},{2,3},{7,4},{4,5},{5,6},{6,7},{11,8},{8,9},{9,10... | collective-permute-start | bytes 184328 | tf_op jit(solution)/shard_map/ppermute | solution.py:845
  9.5 7.3 %collective-permute-start.9 = (f32[120,128]{1,0:T(8,128)S(1)}, f32[120,128]{1,0:T(8,128)S(1)}, u32[]{:S(2)}, u32[]{:S(2)}) collective-permute-start(f32[120,128]{1,0:T(8,128)S(1)} %pad_maximum_fusion.3), channel_id=1, source_target_pairs={{1,0},{2,1},{3,2},{0,3},{5,4},{6,5},{7,6},{4,7},{9,8},{10,9},{11,1... | collective-permute-start | bytes 184328 | tf_op jit(solution)/shard_map/ppermute | solution.py:845
  11.8 5.2 %collective-permute-start.10 = (f32[120,128]{1,0:T(8,128)S(1)}, f32[120,128]{1,0:T(8,128)S(1)}, u32[]{:S(2)}, u32[]{:S(2)}) collective-permute-start(f32[120,128]{1,0:T(8,128)S(1)} %pad_maximum_fusion.3), channel_id=1, source_target_pairs={{2,0},{3,1},{0,2},{1,3},{6,4},{7,5},{4,6},{5,7},{10,8},{11,9},{8,1... | collective-permute-start | bytes 184328 | tf_op jit(solution)/shard_map/ppermute | solution.py:845
  12.8 8.8 %collective-permute-start.5 = (f32[288,128]{1,0:T(8,128)S(1)}, f32[288,128]{1,0:T(8,128)S(1)}, u32[]{:S(2)}, u32[]{:S(2)}) collective-permute-start(f32[288,128]{1,0:T(8,128)S(1)} %constant_dynamic-update-slice_fusion), channel_id=1, source_target_pairs={{24,0},{28,4},{16,8},{20,12},{8,16},{12,20},{0,24},{4,28},{25,1},{... | collective-permute-start | bytes 442376 | tf_op jit(solution)/shard_map/ppermute | solution.py:814
  15.8 8.3 %collective-permute-start.4 = (f32[288,128]{1,0:T(8,128)S(1)}, f32[288,128]{1,0:T(8,128)S(1)}, u32[]{:S(2)}, u32[]{:S(2)}) collective-permute-start(f32[288,128]{1,0:T(8,128)S(1)} %constant_dynamic-update-slice_fusion), channel_id=1, source_target_pairs={{16,0},{20,4},{24,8},{28,12},{0,16},{4,20},{8,24},{12,28},{17,1},{... | collective-permute-start | bytes 442376 | tf_op jit(solution)/shard_map/ppermute | solution.py:814
  16.3 7.8 %collective-permute-start.3 = (f32[288,128]{1,0:T(8,128)S(1)}, f32[288,128]{1,0:T(8,128)S(1)}, u32[]{:S(2)}, u32[]{:S(2)}) collective-permute-start(f32[288,128]{1,0:T(8,128)S(1)} %constant_dynamic-update-slice_fusion), channel_id=1, source_target_pairs={{8,0},{12,4},{0,8},{4,12},{24,16},{28,20},{16,24},{20,28},{9,1},{1... | collective-permute-start | bytes 442376 | tf_op jit(solution)/shard_map/ppermute | solution.py:814
  17.0 12.3 %collective-permute-start.13 = (f32[480,128]{1,0:T(8,128)S(1)}, f32[480,128]{1,0:T(8,128)S(1)}, u32[]{:S(2)}, u32[]{:S(2)}) collective-permute-start(f32[480,128]{1,0:T(8,128)S(1)} %constant_dynamic-update-slice_fusion.4), channel_id=1, source_target_pairs={{24,0},{28,4},{16,8},{20,12},{8,16},{12,20},{0,24},{4,28},{25,1},{... | collective-permute-start | bytes 737288 | tf_op jit(solution)/shard_map/ppermute | solution.py:814
  21.0 12.5 %collective-permute-start.12 = (f32[480,128]{1,0:T(8,128)S(1)}, f32[480,128]{1,0:T(8,128)S(1)}, u32[]{:S(2)}, u32[]{:S(2)}) collective-permute-start(f32[480,128]{1,0:T(8,128)S(1)} %constant_dynamic-update-slice_fusion.4), channel_id=1, source_target_pairs={{16,0},{20,4},{24,8},{28,12},{0,16},{4,20},{8,24},{12,28},{17,1},{... | collective-permute-start | bytes 737288 | tf_op jit(solution)/shard_map/ppermute | solution.py:814
  21.5 12.0 %collective-permute-start.11 = (f32[480,128]{1,0:T(8,128)S(1)}, f32[480,128]{1,0:T(8,128)S(1)}, u32[]{:S(2)}, u32[]{:S(2)}) collective-permute-start(f32[480,128]{1,0:T(8,128)S(1)} %constant_dynamic-update-slice_fusion.4), channel_id=1, source_target_pairs={{8,0},{12,4},{0,8},{4,12},{24,16},{28,20},{16,24},{20,28},{9,1},{1... | collective-permute-start | bytes 737288 | tf_op jit(solution)/shard_map/ppermute | solution.py:814
  24.2 11.7 %collective-permute-start.6 = (f32[4,288,128]{2,1,0:T(8,128)S(1)}, f32[4,288,128]{2,1,0:T(8,128)S(1)}, u32[]{:S(2)}, u32[]{:S(2)}) collective-permute-start(f32[4,288,128]{2,1,0:T(8,128)S(1)} %pad_maximum_fusion.2.own), channel_id=1, source_target_pairs={{0,4},{4,0},{8,12},{12,8},{1,5},{5,1},{9,13},{13,9},{2,6},{6,2},{1... | collective-permute-start | bytes 1769480 | tf_op jit(solution)/shard_map/ppermute | solution.py:820
  24.2 9.9 %collective-permute-start.14 = (f32[480,128]{1,0:T(8,128)S(1)}, f32[480,128]{1,0:T(8,128)S(1)}, u32[]{:S(2)}, u32[]{:S(2)}) collective-permute-start(f32[480,128]{1,0:T(8,128)S(1)} %constant_dynamic-update-slice_fusion.4), channel_id=1, source_target_pairs={{0,4},{4,0},{8,12},{12,8},{1,5},{5,1},{9,13},{13,9},{2,6},{6,2},{1... | collective-permute-start | bytes 737288 | tf_op jit(solution)/shard_map/ppermute | solution.py:820
  29.3 4.8 %collective-permute-start.17 = (f32[480,128]{1,0:T(8,128)S(1)}, f32[480,128]{1,0:T(8,128)S(1)}, u32[]{:S(2)}, u32[]{:S(2)}) collective-permute-start(f32[480,128]{1,0:T(8,128)S(1)} %collective-permute-done.13), channel_id=1, source_target_pairs={{0,4},{4,0},{8,12},{12,8},{1,5},{5,1},{9,13},{13,9},{2,6},{6,2},{1... | collective-permute-start | bytes 737288 | tf_op jit(solution)/shard_map/ppermute | solution.py:820
  33.6 1.5 %collective-permute-start.16 = (f32[480,128]{1,0:T(8,128)S(1)}, f32[480,128]{1,0:T(8,128)S(1)}, u32[]{:S(2)}, u32[]{:S(2)}) collective-permute-start(f32[480,128]{1,0:T(8,128)S(1)} %collective-permute-done.12), channel_id=1, source_target_pairs={{0,4},{4,0},{8,12},{12,8},{1,5},{5,1},{9,13},{13,9},{2,6},{6,2},{1... | collective-permute-start | bytes 737288 | tf_op jit(solution)/shard_map/ppermute | solution.py:820
  33.6 1.8 %collective-permute-start.15 = (f32[480,128]{1,0:T(8,128)S(1)}, f32[480,128]{1,0:T(8,128)S(1)}, u32[]{:S(2)}, u32[]{:S(2)}) collective-permute-start(f32[480,128]{1,0:T(8,128)S(1)} %collective-permute-done.11), channel_id=1, source_target_pairs={{0,4},{4,0},{8,12},{12,8},{1,5},{5,1},{9,13},{13,9},{2,6},{6,2},{1... | collective-permute-start | bytes 737288 | tf_op jit(solution)/shard_map/ppermute | solution.py:820
  35.5 0.9 %copy-start = (f32[272,128]{1,0:T(8,128)S(1)}, f32[272,128]{1,0:T(8,128)}, u32[]{:S(2)}) copy-start(f32[272,128]{1,0:T(8,128)} %constant.15.clone.tref.refs_7_.refs_9_) | copy-start | bytes 417796
  35.5 0.9 %copy-start.1 = (f32[8,128]{1,0:T(8,128)S(1)}, f32[8,128]{1,0:T(8,128)}, u32[]{:S(2)}) copy-start(f32[8,128]{1,0:T(8,128)} %constant.13.clone.mref.refs_6_.refs_8_) | copy-start | bytes 12292
  44.7 0.7 %copy-start.2 = (f32[8,640]{1,0:T(8,128)S(1)}, f32[8,640]{1,0:T(8,128)}, u32[]{:S(2)}) copy-start(f32[8,640]{1,0:T(8,128)} %constant.14.clone.owners) | copy-start | bytes 61444

commit v3 on v2

--- a/solution.py
+++ b/solution.py
@@ -129,6 +129,19 @@
 
 
 TABLE, TINDEX = build_tables()
+
+
+def plane_products(level):
+    weight = np.diag(level.weights)
+    stiff = level.weights[:, None] * level.scaled
+    both = np.concatenate([np.kron(stiff, weight), np.kron(weight, stiff)], axis=0)
+    both = both.astype(np.float32)
+    high = both.astype(jnp.bfloat16)
+    low = (both - high.astype(np.float32)).astype(jnp.bfloat16)
+    return np.concatenate([high, high, low, low], axis=1)
+
+
+PLANES = plane_products(FINE)
 MASK_Y_LO, MASK_Y_HI, MASK_Z_LO, MASK_Z_HI, FAC_Y_LO, FAC_Y_HI, TOP_ROW, NEXT_Z = range(8)
 
 
@@ -150,17 +163,16 @@
         return out
 
     def owners(self, everywhere):
-        lane = np.arange(self.lanes)
-        y = (lane // self.cz) % self.wy
-        x = lane // (self.cz * self.wy)
-        last = x * self.gy + self.gy - 1
-        if everywhere:
-            parts = [zb * self.planes + lane // self.ne for zb in range(self.nz)]
-            zb = self.wy - 1 - y
-            parts.append(np.where(zb < self.nz, zb * self.planes + last, -1))
-        else:
-            parts = [lane // self.ne, np.where(y == self.wy - 1, last, -1)]
-        return np.tile(np.concatenate(parts).astype(np.float32), (SUB, 1))
+        blocks = self.nz if everywhere else 1
+        width = (blocks + 1) * self.lanes
+        place = lax.broadcasted_iota(jnp.int32, (1, width), 1)
+        base = lax.shift_right_logical(place, self.ne.bit_length() - 1)
+        rest = place - blocks * self.lanes
+        y = lax.shift_right_logical(rest, self.cz.bit_length() - 1) & (self.wy - 1)
+        x = lax.shift_right_logical(rest, (self.cz * self.wy).bit_length() - 1)
+        zb = self.wy - 1 - y
+        top = jnp.where(zb < blocks, zb * self.planes + x * self.gy + self.gy - 1, -1)
+        return jnp.where(rest < 0, base, top)
 
     def masks(self):
         lane = np.arange(self.lanes)
@@ -289,9 +301,35 @@
     return total
 
 
-def apply_local(src, dst, gref, tref, geo, level):
+def apply_fine(src, dst, gref, tref, pref, geo):
+    level = FINE
     n = level.n
-    kname, wname = ("kz8", "w8") if n == NF else ("kz4", "w4")
+
+    def body(zb, ch):
+        wc = tab(tref, "w8")
+        g0, g1, g2 = [gref[zb, ch, pl.ds(i, 1), :] for i in range(3)]
+        gw = g0 * wc
+        for b in range(n):
+            mixed = contract([src[zb, ch, rows8(a * n + b), :] for a in range(n)], level)
+            factors = [gw * (level.w[b] * level.w[a]) for a in range(n // 2)]
+            for a in range(n):
+                dst[zb, ch, rows8(a * n + b), :] = mixed[a] * factors[min(a, n - 1 - a)]
+        planes = pref[...]
+        for a in range(n):
+            slab = pl.ds(a * n * SUB, n * SUB)
+            high, low = split(src[zb, ch, slab, :])
+            data = jnp.concatenate([high, low, high, low], axis=0)
+            both = dot(planes, data, ((1,), (0,)))
+            total = both[: n * SUB] * g1 + both[n * SUB :] * g2
+            dst[zb, ch, slab, :] = (dst[zb, ch, slab, :] + total * level.w[a])
+
+    for_tiles(geo, body)
+
+
+def apply_middle(src, dst, gref, tref, geo):
+    level = MID
+    n = level.n
+    kname, wname = "kz4", "w4"
 
     def body(zb, ch):
         ln = lane_ds(ch)
@@ -346,7 +384,7 @@
     return ref[2 * level : 2 * level + 1, :], ref[2 * level + 1 : 2 * level + 2, :]
 
 
-def first_smooth(res, inv, cur, tmp, mref, gref, tref, geo, level, top):
+def first_smooth(res, inv, cur, tmp, mref, geo, level, top, operate):
     first, second = top
 
     def start(zb, ch, row):
@@ -355,7 +393,7 @@
         cur[zb, ch, row, :] = value * res[zb, ch, row, :] * first
 
     each_row(geo, level.n, start)
-    apply_local(cur, tmp, gref, tref, geo, level)
+    operate(cur, tmp)
     gather_sum(tmp, mref, geo, level.n)
 
     def finish(zb, ch, row):
@@ -365,13 +403,13 @@
         )
 
     each_row(geo, level.n, finish)
-    apply_local(cur, tmp, gref, tref, geo, level)
+    operate(cur, tmp)
     gather_sum(tmp, mref, geo, level.n)
 
 
-def next_smooth(res, inv, cur, step, tmp, mref, gref, tref, geo, level, top):
+def next_smooth(res, inv, cur, step, tmp, mref, geo, level, top, operate):
     first, second = top
-    apply_local(cur, tmp, gref, tref, geo, level)
+    operate(cur, tmp)
     gather_sum(tmp, mref, geo, level.n)
 
     def start(zb, ch, row):
@@ -380,7 +418,7 @@
         cur[zb, ch, row, :] = cur[zb, ch, row, :] + value
 
     each_row(geo, level.n, start)
-    apply_local(cur, tmp, gref, tref, geo, level)
+    operate(cur, tmp)
     gather_sum(tmp, mref, geo, level.n)
 
     def finish(zb, ch, row):
@@ -559,7 +597,8 @@
 
 
 def fine_kernel(
-    own, par, eig, mref, tref, res, inv, cur, resm, gref, labels, tmp, buf, *, geo, prow, everywhere
+    own, par, eig, mref, tref, pref, res, inv, cur, resm, gref, labels, tmp, buf,
+    *, geo, prow, everywhere
 ):
     piece = pieces_of(own, par, geo)
     devices = [(ix, iy) for ix in range(geo.gx) for iy in range(geo.gy)]
@@ -584,7 +623,8 @@
     gather_sum(res, mref, geo, NF)
     local_diagonal(tmp, gref, tref, geo, FINE)
     gather_sum(tmp, mref, geo, NF)
-    first_smooth(res, inv, cur, tmp, mref, gref, tref, geo, FINE, scales(eig, 0))
+    operate = functools.partial(apply_fine, gref=gref, tref=tref, pref=pref, geo=geo)
+    first_smooth(res, inv, cur, tmp, mref, geo, FINE, scales(eig, 0), operate)
     restrict(res, tmp, resm, mref, tref, geo, NF, NM, UP_F, "rz8", buf)
     gather_sum(resm, mref, geo, NM)
 
@@ -610,7 +650,8 @@
     invm, curm, tmpm, low, buf = refs[16:]
     local_diagonal(tmpm, gref, tref, geo, MID)
     gather_sum(tmpm, mref, geo, NM)
-    first_smooth(resm, invm, curm, tmpm, mref, gref, tref, geo, MID, scales(eig, 1))
+    operate = functools.partial(apply_middle, gref=gref, tref=tref, geo=geo)
+    first_smooth(resm, invm, curm, tmpm, mref, geo, MID, scales(eig, 1), operate)
     restrict(resm, tmpm, low, mref, tref, geo, NM, NC, UP_C, "rz4", buf)
     z_lo = mref[MASK_Z_LO : MASK_Z_LO + 1, :] > 0.5
     y_lo = mref[MASK_Y_LO : MASK_Y_LO + 1, :]
@@ -644,8 +685,8 @@
 
 def owner_mask(owners, count):
     width = owners.shape[1]
-    row = lax.broadcasted_iota(jnp.int32, (count, width), 0).astype(jnp.float32)
-    return jnp.broadcast_to(owners[0:1, :], (count, width)) == row
+    row = lax.broadcasted_iota(jnp.int32, (count, width), 0)
+    return jnp.broadcast_to(owners, (count, width)) == row
 
 
 def contributions(owned, owners, xhi, xlo, nblk, count):
@@ -680,7 +721,8 @@
     return jnp.sum(jnp.where(mine, full, 0.0), axis=0, keepdims=True)
 
 
-def send_kernel(owned, owners, xhi, xlo, labels, send, *, geo, nblk):
+def send_kernel(owned, xhi, xlo, labels, send, *, geo, nblk):
+    owners = geo.owners(False)
     for k, value in enumerate(contributions(owned, owners, xhi, xlo, nblk, geo.planes)):
         send[:, pl.ds(k * LANES, LANES)] = value
     send[:, pl.ds(nblk * LANES, LANES)] = labels[...]
@@ -688,7 +730,8 @@
 
 def coarse_kernel(*refs, geo, nblk, peers):
     parts = refs[:peers]
-    xhi, xlo, owners, out = refs[peers:]
+    xhi, xlo, out = refs[peers:]
+    owners = geo.owners(False)
     values = [
         jnp.concatenate([part[:, pl.ds(k * LANES, LANES)] for part in parts], axis=0)
         for k in range(nblk + 1)
@@ -702,7 +745,7 @@
 
 def rise(solved, state, consts, out, scratch, geo):
     res, inv, cur_in, resm, invm, curm_in, gref = state
-    eig, mref, tref = consts
+    eig, mref, tref, pref = consts
     cur, curm, tmp, tmpm, step, stepm, low, turned = scratch
     y_hi = mref[MASK_Y_HI : MASK_Y_HI + 1, :] > 0.5
     z_hi = mref[MASK_Z_HI : MASK_Z_HI + 1, :] > 0.5
@@ -725,9 +768,11 @@
                 wide_store(low, 0, row, geo, value[1])
                 wide_store(low, 1, row, geo, jnp.where(low_half, value[2], value[0]))
     prolong_add(low, curm_in, curm, tref, geo, NM, NC, UP_C, "pz4")
-    next_smooth(resm, invm, curm, stepm, tmpm, mref, gref, tref, geo, MID, scales(eig, 1))
+    operate = functools.partial(apply_middle, gref=gref, tref=tref, geo=geo)
+    next_smooth(resm, invm, curm, stepm, tmpm, mref, geo, MID, scales(eig, 1), operate)
     prolong_add(curm, cur_in, cur, tref, geo, NF, NM, UP_F, "pz8")
-    next_smooth(res, inv, cur, step, tmp, mref, gref, tref, geo, FINE, scales(eig, 0))
+    operate = functools.partial(apply_fine, gref=gref, tref=tref, pref=pref, geo=geo)
+    next_smooth(res, inv, cur, step, tmp, mref, geo, FINE, scales(eig, 0), operate)
     words = NF**3 // LANES
     for ch in range(geo.chunks):
         for blk in range(words):
@@ -741,10 +786,11 @@
 def up_kernel(*refs, geo):
     blocks = [(ref[0:1, :], ref[1:2, :]) for ref in refs[:3]]
     rest = refs[3:]
-    rise(blocks, rest[:7], rest[7:10], rest[10], rest[11:], geo)
-
-
-def finish_kernel(owned, owners, xhi, xlo, labels, *refs, geo, nblk):
+    rise(blocks, rest[:7], rest[7:11], rest[11], rest[12:], geo.window(2, 0))
+
+
+def finish_kernel(owned, xhi, xlo, labels, *refs, geo, nblk):
+    owners = geo.owners(True)
     values = contributions(owned, owners, xhi, xlo, nblk, labels.shape[0])
     names = labels[...]
     picked = pick_columns(values, names, names, nblk)
@@ -755,7 +801,7 @@
         (solved[:, zb * geo.lanes : (zb + 1) * geo.lanes], roll(tops, geo.cz * zb))
         for zb in range(3)
     ]
-    rise(blocks, refs[:7], refs[7:10], refs[10], refs[11:], near)
+    rise(blocks, refs[:7], refs[7:11], refs[11], refs[12:], near)
 
 
 def holds_all(gx, gy, gz, cy, cz):
@@ -771,6 +817,7 @@
     if everywhere:
         geo = geo.window(gz)
     ok = cx == 1 and cz % SUB == 0 and LANES % geo.ne == 0 and geo.lanes % LANES == 0
+    ok = ok and all(v & (v - 1) == 0 for v in (geo.ne, cz, geo.wy))
     if not ok or coarse_rows.shape[4] != LANES or geo.planes % SUB:
         raise ValueError("block shape")
     f32 = jnp.float32
@@ -861,10 +908,10 @@
     factor_own = across_chips(factor)
 
     masks = jnp.asarray(geo.masks())
-    owners = jnp.asarray(geo.owners(everywhere))
     table = jnp.asarray(TABLE)
+    planes = jnp.asarray(PLANES)
     count = geo.planes * (geo.nz if everywhere else 1)
-    width = owners.shape[1]
+    width = ((geo.nz if everywhere else 1) + 1) * geo.lanes
     near = geo.window(2, 0)
 
     def field(where, points):
@@ -875,10 +922,10 @@
     metric = shape((geo.nz, geo.chunks, SUB, LANES))
     res, inv, cur, resm, gfac, names = call(
         functools.partial(fine_kernel, geo=geo, prow=prow, everywhere=everywhere),
-        [vmem] * 5,
+        [vmem] * 6,
         [fine] * 3 + [middle, metric, shape((count, LANES))],
         [fine, buf],
-        own, par, marks[1], masks, table,
+        own, par, marks[1], masks, table, planes,
     )
     factor_par = jnp.stack([between_cores(part) for part in factor_own])
     factor_own = jnp.stack(factor_own)
@@ -900,34 +947,34 @@
         [],
         factor_own, factor_par,
     )
-    state = (*merged, scale, masks, table)
-    kinds = [vmem] * 10
+    state = (*merged, scale, masks, table, planes)
+    kinds = [vmem] * 11
     final = shape((geo.ne, NF**3))
     scratch = [fine2, middle2] * 3 + [field(near, NC), shape((geo.lanes, NF**3))]
     if everywhere:
         (out,) = call(
             functools.partial(finish_kernel, geo=geo, nblk=nblk),
-            [vmem] * 5 + kinds,
+            [vmem] * 4 + kinds,
             [final],
             scratch,
-            owned, owners, xhi, xlo, names, *state,
+            owned, xhi, xlo, names, *state,
         )
         return out.reshape(cx, cy, cz, NF**3)
 
     (send,) = call(
         functools.partial(send_kernel, geo=geo, nblk=nblk),
-        [vmem] * 5,
+        [vmem] * 4,
         [shape((geo.planes, (nblk + 1) * LANES))],
         [],
-        owned, owners, xhi, xlo, names,
+        owned, xhi, xlo, names,
     )
     parts = [send] + [from_block(send, offset) for offset in range(1, gz)]
     (solved,) = call(
         functools.partial(coarse_kernel, geo=geo, nblk=nblk, peers=gz),
-        [vmem] * (gz + 3),
+        [vmem] * (gz + 2),
         [shape((SUB, geo.lanes))],
         [],
-        *parts, xhi, xlo, owners,
+        *parts, xhi, xlo,
     )
     (out,) = call(
         functools.partial(up_kernel, geo=geo),

time: 51.8 us -> 50.5 us (0.975)
  local copies, waits for them, and re-layouts: 1.33 us -> 0.6 us
    unnamed x13, local copies, waits for them, and re-layouts: 1.32 us -> 0.6 us
where the time goes in v3:
time: 50.5 us; the launch traced here: 50.3 us
  starting transfers between devices  21.4 us (42%)
  Pallas kernels  15.3 us (30%)
  waiting for transfers between devices  12.7 us (25%)
  local copies, waits for them, and re-layouts  0.6 us (1%)
    pallas_call x6, Pallas kernels, call(): pl.pallas_call(body, out_shape=list(outs), in_specs=specs, out_specs=[vme...  15.3 us
    ppermute x6, waiting for transfers between devices, across_chips(): parts.append(lax.ppermute(value, ('gx', 'gy'), pairs))  10.4 us
    ppermute x6, starting transfers between devices, from_block(): lax.ppermute(value, 'gz', [((i + offset) % gz, i) for i in range(gz)])  10.2 us
    ppermute x6, starting transfers between devices, across_chips(): parts.append(lax.ppermute(value, ('gx', 'gy'), pairs))  9.5 us
    ppermute x5, waiting for transfers between devices, between_cores(): return lax.ppermute(value, 'gy', [(i, i ^ 1) for i in range(gy)])  1.27 us
    ppermute x5, starting transfers between devices, between_cores(): return lax.ppermute(value, 'gy', [(i, i ^ 1) for i in range(gy)])  1.08 us
  transfers between devices with their start and end apart: 18, of which 7 were waited for; matrix products, arithmetic and copies ran while one was open for 0% of the time, Pallas kernels for 1%

profile of v3, /device:TPU:0, one launch (start us, length us, event | category | flops | bytes accessed | tf_op | source)
XLA Modules:
  0.0 50.3 jit_solution(4403584589004432630)
XLA Ops:
  0.0 1.1 %shard_map.82 = (f32[72,128]{1,0:T(8,128)S(1)}, f32[96,128]{1,0:T(8,128)S(1)}, f32[24,128]{1,0:T(8,128)S(1)}, f32[24,128]{1,0:T(8,128)S(1)}, f32[8,128]{1,0:T(8,128)S(1)}) custom-call(f32[16,512]{1,0:T(8,128)} %bitcast.32, f32[3,1,2,8]{3,2,1,0:T(2,128)} %geometry.1, f32[144,128]{1,0:T(8,128)} %bitcast.31, s32[1,1,1,6]{3,2,1,0:T(1,128)} %ids.1, f32[2]{0:T(128)} %eig.1), custom_call_target="tpu_custom_call" | custom-call | tf_op jit(solution)/shard_map/pallas_call | solution.py:836
  1.1 0.7 %collective-permute-start.7 = (f32[24,128]{1,0:T(8,128)S(1)}, f32[24,128]{1,0:T(8,128)S(1)}, u32[]{:S(2)}, u32[]{:S(2)}) collective-permute-start(f32[24,128]{1,0:T(8,128)S(1)} %get-tuple-element.36), channel_id=1, source_target_pairs={{12,8},{13,9},{14,10},{15,11},{28,24},{29,25},{30,26},{31,27}} | collective-permute-start | bytes 36872 | tf_op jit(solution)/shard_map/ppermute | solution.py:900
  1.7 3.1 %collective-permute-start = (f32[72,128]{1,0:T(8,128)S(1)}, f32[72,128]{1,0:T(8,128)S(1)}, u32[]{:S(2)}, u32[]{:S(2)}) collective-permute-start(f32[72,128]{1,0:T(8,128)S(1)} %get-tuple-element.26), channel_id=1, source_target_pairs={{3,0},{0,1},{1,2},{2,3},{7,4},{4,5},{5,6},{6,7},{11,8},{8,9},{9,10... | collective-permute-start | bytes 110600 | tf_op jit(solution)/shard_map/ppermute | solution.py:892
  4.8 2.1 %collective-permute-start.1 = (f32[72,128]{1,0:T(8,128)S(1)}, f32[72,128]{1,0:T(8,128)S(1)}, u32[]{:S(2)}, u32[]{:S(2)}) collective-permute-start(f32[72,128]{1,0:T(8,128)S(1)} %get-tuple-element.26), channel_id=1, source_target_pairs={{1,0},{2,1},{3,2},{0,3},{5,4},{6,5},{7,6},{4,7},{9,8},{10,9},{11,1... | collective-permute-start | bytes 110600 | tf_op jit(solution)/shard_map/ppermute | solution.py:892
  6.9 0.9 %collective-permute-start.2 = (f32[72,128]{1,0:T(8,128)S(1)}, f32[72,128]{1,0:T(8,128)S(1)}, u32[]{:S(2)}, u32[]{:S(2)}) collective-permute-start(f32[72,128]{1,0:T(8,128)S(1)} %get-tuple-element.26), channel_id=1, source_target_pairs={{2,0},{3,1},{0,2},{1,3},{6,4},{7,5},{4,6},{5,7},{10,8},{11,9},{8,1... | collective-permute-start | bytes 110600 | tf_op jit(solution)/shard_map/ppermute | solution.py:892
  7.9 0.0 collective-permute-done.7
  7.9 1.6 %collective-permute-start.8 = (f32[120,128]{1,0:T(8,128)S(1)}, f32[120,128]{1,0:T(8,128)S(1)}, u32[]{:S(2)}, u32[]{:S(2)}) collective-permute-start(f32[120,128]{1,0:T(8,128)S(1)} %pad_maximum_fusion.3), channel_id=1, source_target_pairs={{3,0},{0,1},{1,2},{2,3},{7,4},{4,5},{5,6},{6,7},{11,8},{8,9},{9,10... | collective-permute-start | bytes 184328 | tf_op jit(solution)/shard_map/ppermute | solution.py:892
  9.5 2.2 %collective-permute-start.9 = (f32[120,128]{1,0:T(8,128)S(1)}, f32[120,128]{1,0:T(8,128)S(1)}, u32[]{:S(2)}, u32[]{:S(2)}) collective-permute-start(f32[120,128]{1,0:T(8,128)S(1)} %pad_maximum_fusion.3), channel_id=1, source_target_pairs={{1,0},{2,1},{3,2},{0,3},{5,4},{6,5},{7,6},{4,7},{9,8},{10,9},{11,1... | collective-permute-start | bytes 184328 | tf_op jit(solution)/shard_map/ppermute | solution.py:892
  11.8 0.0 collective-permute-done
  11.8 0.2 collective-permute-start.10
  12.0 0.0 collective-permute-done.1
  12.0 0.8 %collective-permute-done.2 = f32[72,128]{1,0:T(8,128)S(1)} collective-permute-done((f32[72,128]{1,0:T(8,128)S(1)}, f32[72,128]{1,0:T(8,128)S(1)}, u32[]{:S(2)}, u32[]{:S(2)}) %collective-permute-start.2) | collective-permute-done | bytes 36896 | tf_op jit(solution)/shard_map/ppermute | solution.py:892
  12.8 3.0 %collective-permute-start.5 = (f32[288,128]{1,0:T(8,128)S(1)}, f32[288,128]{1,0:T(8,128)S(1)}, u32[]{:S(2)}, u32[]{:S(2)}) collective-permute-start(f32[288,128]{1,0:T(8,128)S(1)} %constant_dynamic-update-slice_fusion), channel_id=1, source_target_pairs={{24,0},{28,4},{16,8},{20,12},{8,16},{12,20},{0,24},{4,28},{25,1},{... | collective-permute-start | bytes 442376 | tf_op jit(solution)/shard_map/ppermute | solution.py:861
  15.8 0.5 %collective-permute-start.4 = (f32[288,128]{1,0:T(8,128)S(1)}, f32[288,128]{1,0:T(8,128)S(1)}, u32[]{:S(2)}, u32[]{:S(2)}) collective-permute-start(f32[288,128]{1,0:T(8,128)S(1)} %constant_dynamic-update-slice_fusion), channel_id=1, source_target_pairs={{16,0},{20,4},{24,8},{28,12},{0,16},{4,20},{8,24},{12,28},{17,1},{... | collective-permute-start | bytes 442376 | tf_op jit(solution)/shard_map/ppermute | solution.py:861
  16.3 0.0 collective-permute-done.8
  16.3 0.4 collective-permute-start.3
  16.8 0.0 collective-permute-done.9
  16.8 0.2 collective-permute-done.10
  17.0 4.0 %collective-permute-start.13 = (f32[480,128]{1,0:T(8,128)S(1)}, f32[480,128]{1,0:T(8,128)S(1)}, u32[]{:S(2)}, u32[]{:S(2)}) collective-permute-start(f32[480,128]{1,0:T(8,128)S(1)} %constant_dynamic-update-slice_fusion.4), channel_id=1, source_target_pairs={{24,0},{28,4},{16,8},{20,12},{8,16},{12,20},{0,24},{4,28},{25,1},{... | collective-permute-start | bytes 737288 | tf_op jit(solution)/shard_map/ppermute | solution.py:861
  21.0 0.5 %collective-permute-start.12 = (f32[480,128]{1,0:T(8,128)S(1)}, f32[480,128]{1,0:T(8,128)S(1)}, u32[]{:S(2)}, u32[]{:S(2)}) collective-permute-start(f32[480,128]{1,0:T(8,128)S(1)} %constant_dynamic-update-slice_fusion.4), channel_id=1, source_target_pairs={{16,0},{20,4},{24,8},{28,12},{0,16},{4,20},{8,24},{12,28},{17,1},{... | collective-permute-start | bytes 737288 | tf_op jit(solution)/shard_map/ppermute | solution.py:861
  21.5 0.0 collective-permute-done.5
  21.5 1.0 %collective-permute-start.11 = (f32[480,128]{1,0:T(8,128)S(1)}, f32[480,128]{1,0:T(8,128)S(1)}, u32[]{:S(2)}, u32[]{:S(2)}) collective-permute-start(f32[480,128]{1,0:T(8,128)S(1)} %constant_dynamic-update-slice_fusion.4), channel_id=1, source_target_pairs={{8,0},{12,4},{0,8},{4,12},{24,16},{28,20},{16,24},{20,28},{9,1},{1... | collective-permute-start | bytes 737288 | tf_op jit(solution)/shard_map/ppermute | solution.py:861
  22.5 1.6 %collective-permute-done.4 = f32[288,128]{1,0:T(8,128)S(1)} collective-permute-done((f32[288,128]{1,0:T(8,128)S(1)}, f32[288,128]{1,0:T(8,128)S(1)}, u32[]{:S(2)}, u32[]{:S(2)}) %collective-permute-start.4) | collective-permute-done | bytes 147488 | tf_op jit(solution)/shard_map/ppermute | solution.py:861
  24.1 0.0 collective-permute-done.3
  24.2 0.1 collective-permute-start.6
  24.2 0.5 collective-permute-start.14
  24.7 4.6 %collective-permute-done.13 = f32[480,128]{1,0:T(8,128)S(1)} collective-permute-done((f32[480,128]{1,0:T(8,128)S(1)}, f32[480,128]{1,0:T(8,128)S(1)}, u32[]{:S(2)}, u32[]{:S(2)}) %collective-permute-start.13) | collective-permute-done | bytes 245792 | tf_op jit(solution)/shard_map/ppermute | solution.py:861
  29.3 0.0 collective-permute-start.17
  29.3 4.2 %collective-permute-done.12 = f32[480,128]{1,0:T(8,128)S(1)} collective-permute-done((f32[480,128]{1,0:T(8,128)S(1)}, f32[480,128]{1,0:T(8,128)S(1)}, u32[]{:S(2)}, u32[]{:S(2)}) %collective-permute-start.12) | collective-permute-done | bytes 245792 | tf_op jit(solution)/shard_map/ppermute | solution.py:861
  33.6 0.0 collective-permute-start.16
  33.6 0.0 collective-permute-done.11
  33.6 0.5 collective-permute-start.15
  34.1 0.1 pad_maximum_fusion.own
  34.1 0.0 collective-permute-done.14
  34.2 0.0 collective-permute-done.17
  34.2 0.9 %collective-permute-done.16 = f32[480,128]{1,0:T(8,128)S(1)} collective-permute-done((f32[480,128]{1,0:T(8,128)S(1)}, f32[480,128]{1,0:T(8,128)S(1)}, u32[]{:S(2)}, u32[]{:S(2)}) %collective-permute-start.16) | collective-permute-done | bytes 245792 | tf_op jit(solution)/shard_map/ppermute | solution.py:867
  35.1 0.4 collective-permute-done.15
  35.4 0.1 pad_maximum_fusion.1.par
  35.5 0.0 copy-start
  35.5 0.0 copy-start.1
  35.5 0.0 copy-start.2
  35.5 0.3 shard_map.86
  35.8 0.0 collective-permute-done.6.par
  35.9 0.5 %copy-done = f32[272,128]{1,0:T(8,128)S(1)} copy-done((f32[272,128]{1,0:T(8,128)S(1)}, f32[272,128]{1,0:T(8,128)}, u32[]{:S(2)}) %copy-start) | copy-done | bytes 139288
  36.4 0.0 copy-done.1
  36.4 5.9 %shard_map.84 = (f32[4,1,512,128]{3,2,1,0:T(8,128)S(1)}, f32[4,1,512,128]{3,2,1,0:T(8,128)S(1)}, f32[4,1,512,128]{3,2,1,0:T(8,128)S(1)}, f32[4,1,128,128]{3,2,1,...) custom-call(f32[4,288,128]{2,1,0:T(8,128)S(1)} %pad_maximum_fusion.2.own, ...), custom_call_target="tpu_custom_call" | custom-call | tf_op jit(solution)/shard_map/pallas_call | solution.py:836
  42.3 2.0 %shard_map.85 = (f32[2,1,512,128]{3,2,1,0:T(8,128)S(1)}, f32[2,1,512,128]{3,2,1,0:T(8,128)S(1)}, f32[2,1,512,128]{3,2,1,0:T(8,128)S(1)}, f32[2,1,128,128]{3,2,1,...) custom-call(f32[4,1,512,128]{3,2,1,0:T(8,128)S(1)} %get-tuple-elemen, ...), custom_call_target="tpu_custom_call" | custom-call | tf_op jit(solution)/shard_map/pallas_call | solution.py:836
  44.3 6.0 %shard_map.87 = f32[16,512]{1,0:T(8,128)} custom-call(f32[8,640]{1,0:T(8,128)S(1)} %get-tuple-element.33.owned, bf16[6,640,128]{2,1,0:T(8,128)(2,1)S(1)} %get-tuple-element.37.xhi, bf16[6,640,128]{2,1,0:T(8,128)(2,1)S(1)} %get-tuple-element.38.xlo, f32[32,128]{1,0:T(8,128)S(1)} %get-tuple-element.39.labels, ...), custom_call_target="tpu_custom_call" | custom-call | tf_op jit(solution)/shard_map/pallas_call | solution.py:836
  (14 shorter events, 0.1 us)
Async XLA Ops:
  1.1 6.8 %collective-permute-start.7 = (f32[24,128]{1,0:T(8,128)S(1)}, f32[24,128]{1,0:T(8,128)S(1)}, u32[]{:S(2)}, u32[]{:S(2)}) collective-permute-start(f32[24,128]{1,0:T(8,128)S(1)} %get-tuple-element.36), channel_id=1, source_target_pairs={{12,8},{13,9},{14,10},{15,11},{28,24},{29,25},{30,26},{31,27}} | collective-permute-start | bytes 36872 | tf_op jit(solution)/shard_map/ppermute | solution.py:900
  1.7 10.0 %collective-permute-start = (f32[72,128]{1,0:T(8,128)S(1)}, f32[72,128]{1,0:T(8,128)S(1)}, u32[]{:S(2)}, u32[]{:S(2)}) collective-permute-start(f32[72,128]{1,0:T(8,128)S(1)} %get-tuple-element.26), channel_id=1, source_target_pairs={{3,0},{0,1},{1,2},{2,3},{7,4},{4,5},{5,6},{6,7},{11,8},{8,9},{9,10... | collective-permute-start | bytes 110600 | tf_op jit(solution)/shard_map/ppermute | solution.py:892
  4.8 7.1 %collective-permute-start.1 = (f32[72,128]{1,0:T(8,128)S(1)}, f32[72,128]{1,0:T(8,128)S(1)}, u32[]{:S(2)}, u32[]{:S(2)}) collective-permute-start(f32[72,128]{1,0:T(8,128)S(1)} %get-tuple-element.26), channel_id=1, source_target_pairs={{1,0},{2,1},{3,2},{0,3},{5,4},{6,5},{7,6},{4,7},{9,8},{10,9},{11,1... | collective-permute-start | bytes 110600 | tf_op jit(solution)/shard_map/ppermute | solution.py:892
  6.9 5.8 %collective-permute-start.2 = (f32[72,128]{1,0:T(8,128)S(1)}, f32[72,128]{1,0:T(8,128)S(1)}, u32[]{:S(2)}, u32[]{:S(2)}) collective-permute-start(f32[72,128]{1,0:T(8,128)S(1)} %get-tuple-element.26), channel_id=1, source_target_pairs={{2,0},{3,1},{0,2},{1,3},{6,4},{7,5},{4,6},{5,7},{10,8},{11,9},{8,1... | collective-permute-start | bytes 110600 | tf_op jit(solution)/shard_map/ppermute | solution.py:892
  7.9 8.4 %collective-permute-start.8 = (f32[120,128]{1,0:T(8,128)S(1)}, f32[120,128]{1,0:T(8,128)S(1)}, u32[]{:S(2)}, u32[]{:S(2)}) collective-permute-start(f32[120,128]{1,0:T(8,128)S(1)} %pad_maximum_fusion.3), channel_id=1, source_target_pairs={{3,0},{0,1},{1,2},{2,3},{7,4},{4,5},{5,6},{6,7},{11,8},{8,9},{9,10... | collective-permute-start | bytes 184328 | tf_op jit(solution)/shard_map/ppermute | solution.py:892
  9.5 7.3 %collective-permute-start.9 = (f32[120,128]{1,0:T(8,128)S(1)}, f32[120,128]{1,0:T(8,128)S(1)}, u32[]{:S(2)}, u32[]{:S(2)}) collective-permute-start(f32[120,128]{1,0:T(8,128)S(1)} %pad_maximum_fusion.3), channel_id=1, source_target_pairs={{1,0},{2,1},{3,2},{0,3},{5,4},{6,5},{7,6},{4,7},{9,8},{10,9},{11,1... | collective-permute-start | bytes 184328 | tf_op jit(solution)/shard_map/ppermute | solution.py:892
  11.8 5.2 %collective-permute-start.10 = (f32[120,128]{1,0:T(8,128)S(1)}, f32[120,128]{1,0:T(8,128)S(1)}, u32[]{:S(2)}, u32[]{:S(2)}) collective-permute-start(f32[120,128]{1,0:T(8,128)S(1)} %pad_maximum_fusion.3), channel_id=1, source_target_pairs={{2,0},{3,1},{0,2},{1,3},{6,4},{7,5},{4,6},{5,7},{10,8},{11,9},{8,1... | collective-permute-start | bytes 184328 | tf_op jit(solution)/shard_map/ppermute | solution.py:892
  12.8 8.8 %collective-permute-start.5 = (f32[288,128]{1,0:T(8,128)S(1)}, f32[288,128]{1,0:T(8,128)S(1)}, u32[]{:S(2)}, u32[]{:S(2)}) collective-permute-start(f32[288,128]{1,0:T(8,128)S(1)} %constant_dynamic-update-slice_fusion), channel_id=1, source_target_pairs={{24,0},{28,4},{16,8},{20,12},{8,16},{12,20},{0,24},{4,28},{25,1},{... | collective-permute-start | bytes 442376 | tf_op jit(solution)/shard_map/ppermute | solution.py:861
  15.8 8.3 %collective-permute-start.4 = (f32[288,128]{1,0:T(8,128)S(1)}, f32[288,128]{1,0:T(8,128)S(1)}, u32[]{:S(2)}, u32[]{:S(2)}) collective-permute-start(f32[288,128]{1,0:T(8,128)S(1)} %constant_dynamic-update-slice_fusion), channel_id=1, source_target_pairs={{16,0},{20,4},{24,8},{28,12},{0,16},{4,20},{8,24},{12,28},{17,1},{... | collective-permute-start | bytes 442376 | tf_op jit(solution)/shard_map/ppermute | solution.py:861
  16.3 7.8 %collective-permute-start.3 = (f32[288,128]{1,0:T(8,128)S(1)}, f32[288,128]{1,0:T(8,128)S(1)}, u32[]{:S(2)}, u32[]{:S(2)}) collective-permute-start(f32[288,128]{1,0:T(8,128)S(1)} %constant_dynamic-update-slice_fusion), channel_id=1, source_target_pairs={{8,0},{12,4},{0,8},{4,12},{24,16},{28,20},{16,24},{20,28},{9,1},{1... | collective-permute-start | bytes 442376 | tf_op jit(solution)/shard_map/ppermute | solution.py:861
  17.0 12.3 %collective-permute-start.13 = (f32[480,128]{1,0:T(8,128)S(1)}, f32[480,128]{1,0:T(8,128)S(1)}, u32[]{:S(2)}, u32[]{:S(2)}) collective-permute-start(f32[480,128]{1,0:T(8,128)S(1)} %constant_dynamic-update-slice_fusion.4), channel_id=1, source_target_pairs={{24,0},{28,4},{16,8},{20,12},{8,16},{12,20},{0,24},{4,28},{25,1},{... | collective-permute-start | bytes 737288 | tf_op jit(solution)/shard_map/ppermute | solution.py:861
  21.0 12.5 %collective-permute-start.12 = (f32[480,128]{1,0:T(8,128)S(1)}, f32[480,128]{1,0:T(8,128)S(1)}, u32[]{:S(2)}, u32[]{:S(2)}) collective-permute-start(f32[480,128]{1,0:T(8,128)S(1)} %constant_dynamic-update-slice_fusion.4), channel_id=1, source_target_pairs={{16,0},{20,4},{24,8},{28,12},{0,16},{4,20},{8,24},{12,28},{17,1},{... | collective-permute-start | bytes 737288 | tf_op jit(solution)/shard_map/ppermute | solution.py:861
  21.5 12.0 %collective-permute-start.11 = (f32[480,128]{1,0:T(8,128)S(1)}, f32[480,128]{1,0:T(8,128)S(1)}, u32[]{:S(2)}, u32[]{:S(2)}) collective-permute-start(f32[480,128]{1,0:T(8,128)S(1)} %constant_dynamic-update-slice_fusion.4), channel_id=1, source_target_pairs={{8,0},{12,4},{0,8},{4,12},{24,16},{28,20},{16,24},{20,28},{9,1},{1... | collective-permute-start | bytes 737288 | tf_op jit(solution)/shard_map/ppermute | solution.py:861
  24.2 11.7 %collective-permute-start.6 = (f32[4,288,128]{2,1,0:T(8,128)S(1)}, f32[4,288,128]{2,1,0:T(8,128)S(1)}, u32[]{:S(2)}, u32[]{:S(2)}) collective-permute-start(f32[4,288,128]{2,1,0:T(8,128)S(1)} %pad_maximum_fusion.2.own), channel_id=1, source_target_pairs={{0,4},{4,0},{8,12},{12,8},{1,5},{5,1},{9,13},{13,9},{2,6},{6,2},{1... | collective-permute-start | bytes 1769480 | tf_op jit(solution)/shard_map/ppermute | solution.py:867
  24.2 9.9 %collective-permute-start.14 = (f32[480,128]{1,0:T(8,128)S(1)}, f32[480,128]{1,0:T(8,128)S(1)}, u32[]{:S(2)}, u32[]{:S(2)}) collective-permute-start(f32[480,128]{1,0:T(8,128)S(1)} %constant_dynamic-update-slice_fusion.4), channel_id=1, source_target_pairs={{0,4},{4,0},{8,12},{12,8},{1,5},{5,1},{9,13},{13,9},{2,6},{6,2},{1... | collective-permute-start | bytes 737288 | tf_op jit(solution)/shard_map/ppermute | solution.py:867
  29.3 4.8 %collective-permute-start.17 = (f32[480,128]{1,0:T(8,128)S(1)}, f32[480,128]{1,0:T(8,128)S(1)}, u32[]{:S(2)}, u32[]{:S(2)}) collective-permute-start(f32[480,128]{1,0:T(8,128)S(1)} %collective-permute-done.13), channel_id=1, source_target_pairs={{0,4},{4,0},{8,12},{12,8},{1,5},{5,1},{9,13},{13,9},{2,6},{6,2},{1... | collective-permute-start | bytes 737288 | tf_op jit(solution)/shard_map/ppermute | solution.py:867
  33.6 1.5 %collective-permute-start.16 = (f32[480,128]{1,0:T(8,128)S(1)}, f32[480,128]{1,0:T(8,128)S(1)}, u32[]{:S(2)}, u32[]{:S(2)}) collective-permute-start(f32[480,128]{1,0:T(8,128)S(1)} %collective-permute-done.12), channel_id=1, source_target_pairs={{0,4},{4,0},{8,12},{12,8},{1,5},{5,1},{9,13},{13,9},{2,6},{6,2},{1... | collective-permute-start | bytes 737288 | tf_op jit(solution)/shard_map/ppermute | solution.py:867
  33.6 1.8 %collective-permute-start.15 = (f32[480,128]{1,0:T(8,128)S(1)}, f32[480,128]{1,0:T(8,128)S(1)}, u32[]{:S(2)}, u32[]{:S(2)}) collective-permute-start(f32[480,128]{1,0:T(8,128)S(1)} %collective-permute-done.11), channel_id=1, source_target_pairs={{0,4},{4,0},{8,12},{12,8},{1,5},{5,1},{9,13},{13,9},{2,6},{6,2},{1... | collective-permute-start | bytes 737288 | tf_op jit(solution)/shard_map/ppermute | solution.py:867
  35.5 0.9 %copy-start = (f32[272,128]{1,0:T(8,128)S(1)}, f32[272,128]{1,0:T(8,128)}, u32[]{:S(2)}) copy-start(f32[272,128]{1,0:T(8,128)} %constant.14.clone.tref.refs_7_.refs_9_) | copy-start | bytes 417796
  35.5 0.9 %copy-start.1 = (bf16[128,256]{1,0:T(8,128)(2,1)S(1)}, bf16[128,256]{1,0:T(8,128)(2,1)}, u32[]{:S(2)}) copy-start(bf16[128,256]{1,0:T(8,128)(2,1)} %constant.15.clone.pref.refs_10_) | copy-start | bytes 196612
  35.5 0.9 %copy-start.2 = (f32[8,128]{1,0:T(8,128)S(1)}, f32[8,128]{1,0:T(8,128)}, u32[]{:S(2)}) copy-start(f32[8,128]{1,0:T(8,128)} %constant.13.clone.mref.refs_6_.refs_8_) | copy-start | bytes 12292

commit v4 on v3

--- a/solution.py
+++ b/solution.py
@@ -206,7 +206,7 @@
     return pl.ds(pl.multiple_of(chunk * LANES, LANES), LANES)
 
 
-def for_tiles(geo, body):
+def for_tiles(geo, body, unroll=1):
     def step(pos, carry):
         if geo.chunks == 1:
             body(pos, 0)
@@ -214,7 +214,7 @@
             body(pos // geo.chunks, pos % geo.chunks)
         return carry
 
-    lax.fori_loop(0, geo.nz * geo.chunks, step, 0)
+    lax.fori_loop(0, geo.nz * geo.chunks, step, 0, unroll=unroll)
 
 
 def rows8(pos):
@@ -321,9 +321,9 @@
             data = jnp.concatenate([high, low, high, low], axis=0)
             both = dot(planes, data, ((1,), (0,)))
             total = both[: n * SUB] * g1 + both[n * SUB :] * g2
-            dst[zb, ch, slab, :] = (dst[zb, ch, slab, :] + total * level.w[a])
-
-    for_tiles(geo, body)
+            dst[zb, ch, slab, :] = dst[zb, ch, slab, :] + total * level.w[a]
+
+    for_tiles(geo, body, unroll=2 if geo.nz * geo.chunks > 2 else 1)
 
 
 def apply_middle(src, dst, gref, tref, geo):
@@ -372,12 +372,12 @@
     for_tiles(geo, body)
 
 
-def each_row(geo, n, body):
+def each_row(geo, n, body, blocks=None):
     def tile(zb, ch):
         for row in range(n * n):
             body(zb, ch, rows8(row))
 
-    for_tiles(geo, tile)
+    for_tiles(geo if blocks is None else geo.window(blocks), tile)
 
 
 def scales(ref, level):
@@ -429,7 +429,7 @@
             + second * (inv[zb, ch, row, :] * left)
         )
 
-    each_row(geo, level.n, finish)
+    each_row(geo, level.n, finish, 1 if level.n == NF else None)
 
 
 def restrict(res, tmp, dst, mref, tref, geo, nf, nc, table, name, buf):
@@ -597,7 +597,8 @@
 
 
 def fine_kernel(
-    own, par, eig, mref, tref, pref, res, inv, cur, resm, gref, labels, tmp, buf,
+    own, par, eig, mref, tref, pref, res2, inv2, cur2, resm, gref, labels,
+    res, inv, cur, tmp, buf,
     *, geo, prow, everywhere
 ):
     piece = pieces_of(own, par, geo)
@@ -627,6 +628,8 @@
     first_smooth(res, inv, cur, tmp, mref, geo, FINE, scales(eig, 0), operate)
     restrict(res, tmp, resm, mref, tref, geo, NF, NM, UP_F, "rz8", buf)
     gather_sum(resm, mref, geo, NM)
+    for source, target in zip((res, inv, cur), (res2, inv2, cur2)):
+        merge(source, target, mref, geo)
 
 
 def merge(src, dst, mref, geo):
@@ -645,9 +648,9 @@
 
 
 def middle_kernel(*refs, geo, everywhere):
-    res, inv, cur, resm, gref, eig, mref, tref = refs[:8]
-    merged, owned = refs[8:15], refs[15]
-    invm, curm, tmpm, low, buf = refs[16:]
+    resm, gref, eig, mref, tref = refs[:5]
+    merged, owned = refs[5:9], refs[9]
+    invm, curm, tmpm, low, buf = refs[10:]
     local_diagonal(tmpm, gref, tref, geo, MID)
     gather_sum(tmpm, mref, geo, NM)
     operate = functools.partial(apply_middle, gref=gref, tref=tref, geo=geo)
@@ -679,7 +682,7 @@
     owned[:, pl.ds(len(blocks) * geo.lanes, geo.lanes)] = jnp.broadcast_to(
         tops, (SUB, geo.lanes)
     )
-    for source, target in zip((res, inv, cur, resm, invm, curm, gref), merged):
+    for source, target in zip((resm, invm, curm, gref), merged):
         merge(source, target, mref, geo)
 
 
@@ -920,24 +923,23 @@
     fine, middle, lowest = (field(geo, points) for points in (NF, NM, NC))
     buf = shape((1, 1, NM * NM * SUB, LANES))
     metric = shape((geo.nz, geo.chunks, SUB, LANES))
-    res, inv, cur, resm, gfac, names = call(
+    fine2, middle2 = (field(near, points) for points in (NF, NM))
+    *top, resm, gfac, names = call(
         functools.partial(fine_kernel, geo=geo, prow=prow, everywhere=everywhere),
         [vmem] * 6,
-        [fine] * 3 + [middle, metric, shape((count, LANES))],
-        [fine, buf],
+        [fine2] * 3 + [middle, metric, shape((count, LANES))],
+        [fine] * 4 + [buf],
         own, par, marks[1], masks, table, planes,
     )
     factor_par = jnp.stack([between_cores(part) for part in factor_own])
     factor_own = jnp.stack(factor_own)
-    fine2, middle2 = (field(near, points) for points in (NF, NM))
     *merged, owned = call(
         functools.partial(middle_kernel, geo=geo, everywhere=everywhere),
-        [vmem] * 8,
-        [fine2] * 3
-        + [middle2] * 3
+        [vmem] * 5,
+        [middle2] * 3
         + [shape((2, geo.chunks, SUB, LANES)), shape((SUB, width))],
         [middle, middle, middle, lowest, buf],
-        res, inv, cur, resm, gfac, marks[0], masks, table,
+        resm, gfac, marks[0], masks, table,
     )
     wide = shape((nblk, width, LANES), jnp.bfloat16)
     xhi, xlo = call(
@@ -947,7 +949,7 @@
         [],
         factor_own, factor_par,
     )
-    state = (*merged, scale, masks, table, planes)
+    state = (*top, *merged, scale, masks, table, planes)
     kinds = [vmem] * 11
     final = shape((geo.ne, NF**3))
     scratch = [fine2, middle2] * 3 + [field(near, NC), shape((geo.lanes, NF**3))]

time: 50.5 us -> 50.6 us (level)
  waiting for transfers between devices: 12.7 us -> 14.3 us
  Pallas kernels: 15.3 us -> 14.3 us
    ppermute x6, waiting for transfers between devices: 0.98 us -> 3.5 us  [from_block(): lax.ppermute(value, 'gz', [((i + offset) % gz, i) for i in range(gz)])]
    ppermute x6, waiting for transfers between devices: 10.4 us -> 9.34 us  [across_chips(): parts.append(lax.ppermute(value, ('gx', 'gy'), pairs))]
    pallas_call x6, Pallas kernels: 15.3 us -> 14.3 us  [call(): pl.pallas_call(body, out_shape=list(outs), in_specs=specs, out_specs=[vme...]
where the time goes in v4:
time: 50.6 us; the launch traced here: 50.5 us
  starting transfers between devices  20.9 us (41%)
  Pallas kernels  14.3 us (28%)
  waiting for transfers between devices  14.3 us (28%)
  local copies, waits for them, and re-layouts  0.61 us (1%)
    pallas_call x6, Pallas kernels, call(): pl.pallas_call(body, out_shape=list(outs), in_specs=specs, out_specs=[vme...  14.3 us
    ppermute x6, starting transfers between devices, from_block(): lax.ppermute(value, 'gz', [((i + offset) % gz, i) for i in range(gz)])  10.2 us
    ppermute x6, starting transfers between devices, across_chips(): parts.append(lax.ppermute(value, ('gx', 'gy'), pairs))  9.5 us
    ppermute x6, waiting for transfers between devices, across_chips(): parts.append(lax.ppermute(value, ('gx', 'gy'), pairs))  9.34 us
    ppermute x6, waiting for transfers between devices, from_block(): lax.ppermute(value, 'gz', [((i + offset) % gz, i) for i in range(gz)])  3.5 us
    ppermute x5, waiting for transfers between devices, between_cores(): return lax.ppermute(value, 'gy', [(i, i ^ 1) for i in range(gy)])  1.42 us
  transfers between devices with their start and end apart: 18, of which 7 were waited for; matrix products, arithmetic and copies ran while one was open for 0% of the time, Pallas kernels for 1%

profile of v4, /device:TPU:0, one launch (start us, length us, event | category | flops | bytes accessed | tf_op | source)
XLA Modules:
  0.0 50.5 jit_solution(10159914675408824334)
XLA Ops:
  0.0 1.1 %shard_map.82 = (f32[72,128]{1,0:T(8,128)S(1)}, f32[96,128]{1,0:T(8,128)S(1)}, f32[24,128]{1,0:T(8,128)S(1)}, f32[24,128]{1,0:T(8,128)S(1)}, f32[8,128]{1,0:T(8,128)S(1)}) custom-call(f32[16,512]{1,0:T(8,128)} %bitcast.32, f32[3,1,2,8]{3,2,1,0:T(2,128)} %geometry.1, f32[144,128]{1,0:T(8,128)} %bitcast.31, s32[1,1,1,6]{3,2,1,0:T(1,128)} %ids.1, f32[2]{0:T(128)} %eig.1), custom_call_target="tpu_custom_call" | custom-call | tf_op jit(solution)/shard_map/pallas_call | solution.py:839
  1.1 0.7 %collective-permute-start.7 = (f32[24,128]{1,0:T(8,128)S(1)}, f32[24,128]{1,0:T(8,128)S(1)}, u32[]{:S(2)}, u32[]{:S(2)}) collective-permute-start(f32[24,128]{1,0:T(8,128)S(1)} %get-tuple-element.30), channel_id=1, source_target_pairs={{12,8},{13,9},{14,10},{15,11},{28,24},{29,25},{30,26},{31,27}} | collective-permute-start | bytes 36872 | tf_op jit(solution)/shard_map/ppermute | solution.py:903
  1.7 4.1 %collective-permute-start.2 = (f32[72,128]{1,0:T(8,128)S(1)}, f32[72,128]{1,0:T(8,128)S(1)}, u32[]{:S(2)}, u32[]{:S(2)}) collective-permute-start(f32[72,128]{1,0:T(8,128)S(1)} %get-tuple-element.23), channel_id=1, source_target_pairs={{2,0},{3,1},{0,2},{1,3},{6,4},{7,5},{4,6},{5,7},{10,8},{11,9},{8,1... | collective-permute-start | bytes 110600 | tf_op jit(solution)/shard_map/ppermute | solution.py:895
  5.9 1.3 %collective-permute-start.1 = (f32[72,128]{1,0:T(8,128)S(1)}, f32[72,128]{1,0:T(8,128)S(1)}, u32[]{:S(2)}, u32[]{:S(2)}) collective-permute-start(f32[72,128]{1,0:T(8,128)S(1)} %get-tuple-element.23), channel_id=1, source_target_pairs={{1,0},{2,1},{3,2},{0,3},{5,4},{6,5},{7,6},{4,7},{9,8},{10,9},{11,1... | collective-permute-start | bytes 110600 | tf_op jit(solution)/shard_map/ppermute | solution.py:895
  7.2 0.7 %collective-permute-start = (f32[72,128]{1,0:T(8,128)S(1)}, f32[72,128]{1,0:T(8,128)S(1)}, u32[]{:S(2)}, u32[]{:S(2)}) collective-permute-start(f32[72,128]{1,0:T(8,128)S(1)} %get-tuple-element.23), channel_id=1, source_target_pairs={{3,0},{0,1},{1,2},{2,3},{7,4},{4,5},{5,6},{6,7},{11,8},{8,9},{9,10... | collective-permute-start | bytes 110600 | tf_op jit(solution)/shard_map/ppermute | solution.py:895
  7.9 0.0 collective-permute-done.7
  7.9 1.1 %collective-permute-start.10 = (f32[120,128]{1,0:T(8,128)S(1)}, f32[120,128]{1,0:T(8,128)S(1)}, u32[]{:S(2)}, u32[]{:S(2)}) collective-permute-start(f32[120,128]{1,0:T(8,128)S(1)} %pad_maximum_fusion.3), channel_id=1, source_target_pairs={{2,0},{3,1},{0,2},{1,3},{6,4},{7,5},{4,6},{5,7},{10,8},{11,9},{8,1... | collective-permute-start | bytes 184328 | tf_op jit(solution)/shard_map/ppermute | solution.py:895
  9.0 2.9 %collective-permute-start.9 = (f32[120,128]{1,0:T(8,128)S(1)}, f32[120,128]{1,0:T(8,128)S(1)}, u32[]{:S(2)}, u32[]{:S(2)}) collective-permute-start(f32[120,128]{1,0:T(8,128)S(1)} %pad_maximum_fusion.3), channel_id=1, source_target_pairs={{1,0},{2,1},{3,2},{0,3},{5,4},{6,5},{7,6},{4,7},{9,8},{10,9},{11,1... | collective-permute-start | bytes 184328 | tf_op jit(solution)/shard_map/ppermute | solution.py:895
  11.9 1.3 %collective-permute-done = f32[72,128]{1,0:T(8,128)S(1)} collective-permute-done((f32[72,128]{1,0:T(8,128)S(1)}, f32[72,128]{1,0:T(8,128)S(1)}, u32[]{:S(2)}, u32[]{:S(2)}) %collective-permute-start) | collective-permute-done | bytes 36896 | tf_op jit(solution)/shard_map/ppermute | solution.py:895
  13.2 0.0 collective-permute-start.8
  13.2 0.0 collective-permute-done.1
  13.2 0.0 collective-permute-done.2
  13.3 3.2 %collective-permute-start.5 = (f32[288,128]{1,0:T(8,128)S(1)}, f32[288,128]{1,0:T(8,128)S(1)}, u32[]{:S(2)}, u32[]{:S(2)}) collective-permute-start(f32[288,128]{1,0:T(8,128)S(1)} %constant_dynamic-update-slice_fusion), channel_id=1, source_target_pairs={{24,0},{28,4},{16,8},{20,12},{8,16},{12,20},{0,24},{4,28},{25,1},{... | collective-permute-start | bytes 442376 | tf_op jit(solution)/shard_map/ppermute | solution.py:864
  16.5 0.5 %collective-permute-start.4 = (f32[288,128]{1,0:T(8,128)S(1)}, f32[288,128]{1,0:T(8,128)S(1)}, u32[]{:S(2)}, u32[]{:S(2)}) collective-permute-start(f32[288,128]{1,0:T(8,128)S(1)} %constant_dynamic-update-slice_fusion), channel_id=1, source_target_pairs={{16,0},{20,4},{24,8},{28,12},{0,16},{4,20},{8,24},{12,28},{17,1},{... | collective-permute-start | bytes 442376 | tf_op jit(solution)/shard_map/ppermute | solution.py:864
  17.0 2.2 %collective-permute-done.8 = f32[120,128]{1,0:T(8,128)S(1)} collective-permute-done((f32[120,128]{1,0:T(8,128)S(1)}, f32[120,128]{1,0:T(8,128)S(1)}, u32[]{:S(2)}, u32[]{:S(2)}) %collective-permute-start.8) | collective-permute-done | bytes 61472 | tf_op jit(solution)/shard_map/ppermute | solution.py:895
  19.2 2.2 %collective-permute-start.3 = (f32[288,128]{1,0:T(8,128)S(1)}, f32[288,128]{1,0:T(8,128)S(1)}, u32[]{:S(2)}, u32[]{:S(2)}) collective-permute-start(f32[288,128]{1,0:T(8,128)S(1)} %constant_dynamic-update-slice_fusion), channel_id=1, source_target_pairs={{8,0},{12,4},{0,8},{4,12},{24,16},{28,20},{16,24},{20,28},{9,1},{1... | collective-permute-start | bytes 442376 | tf_op jit(solution)/shard_map/ppermute | solution.py:864
  21.4 0.0 collective-permute-done.9
  21.5 0.0 collective-permute-done.10
  21.5 1.0 %collective-permute-start.13 = (f32[480,128]{1,0:T(8,128)S(1)}, f32[480,128]{1,0:T(8,128)S(1)}, u32[]{:S(2)}, u32[]{:S(2)}) collective-permute-start(f32[480,128]{1,0:T(8,128)S(1)} %constant_dynamic-update-slice_fusion.4), channel_id=1, source_target_pairs={{24,0},{28,4},{16,8},{20,12},{8,16},{12,20},{0,24},{4,28},{25,1},{... | collective-permute-start | bytes 737288 | tf_op jit(solution)/shard_map/ppermute | solution.py:864
  22.5 0.6 %collective-permute-start.12 = (f32[480,128]{1,0:T(8,128)S(1)}, f32[480,128]{1,0:T(8,128)S(1)}, u32[]{:S(2)}, u32[]{:S(2)}) collective-permute-start(f32[480,128]{1,0:T(8,128)S(1)} %constant_dynamic-update-slice_fusion.4), channel_id=1, source_target_pairs={{16,0},{20,4},{24,8},{28,12},{0,16},{4,20},{8,24},{12,28},{17,1},{... | collective-permute-start | bytes 737288 | tf_op jit(solution)/shard_map/ppermute | solution.py:864
  23.2 0.0 collective-permute-done.5
  23.2 1.9 %collective-permute-start.11 = (f32[480,128]{1,0:T(8,128)S(1)}, f32[480,128]{1,0:T(8,128)S(1)}, u32[]{:S(2)}, u32[]{:S(2)}) collective-permute-start(f32[480,128]{1,0:T(8,128)S(1)} %constant_dynamic-update-slice_fusion.4), channel_id=1, source_target_pairs={{8,0},{12,4},{0,8},{4,12},{24,16},{28,20},{16,24},{20,28},{9,1},{1... | collective-permute-start | bytes 737288 | tf_op jit(solution)/shard_map/ppermute | solution.py:864
  25.1 0.0 collective-permute-done.4
  25.1 1.1 %collective-permute-done.3 = f32[288,128]{1,0:T(8,128)S(1)} collective-permute-done((f32[288,128]{1,0:T(8,128)S(1)}, f32[288,128]{1,0:T(8,128)S(1)}, u32[]{:S(2)}, u32[]{:S(2)}) %collective-permute-start.3) | collective-permute-done | bytes 147488 | tf_op jit(solution)/shard_map/ppermute | solution.py:864
  26.2 0.1 collective-permute-start.6
  26.2 0.5 collective-permute-start.14
  26.7 5.6 %collective-permute-done.13 = f32[480,128]{1,0:T(8,128)S(1)} collective-permute-done((f32[480,128]{1,0:T(8,128)S(1)}, f32[480,128]{1,0:T(8,128)S(1)}, u32[]{:S(2)}, u32[]{:S(2)}) %collective-permute-start.13) | collective-permute-done | bytes 245792 | tf_op jit(solution)/shard_map/ppermute | solution.py:864
  32.3 0.0 collective-permute-start.17
  32.4 1.1 %collective-permute-done.12 = f32[480,128]{1,0:T(8,128)S(1)} collective-permute-done((f32[480,128]{1,0:T(8,128)S(1)}, f32[480,128]{1,0:T(8,128)S(1)}, u32[]{:S(2)}, u32[]{:S(2)}) %collective-permute-start.12) | collective-permute-done | bytes 245792 | tf_op jit(solution)/shard_map/ppermute | solution.py:864
  33.4 0.0 collective-permute-start.16
  33.4 1.6 %collective-permute-done.11 = f32[480,128]{1,0:T(8,128)S(1)} collective-permute-done((f32[480,128]{1,0:T(8,128)S(1)}, f32[480,128]{1,0:T(8,128)S(1)}, u32[]{:S(2)}, u32[]{:S(2)}) %collective-permute-start.11) | collective-permute-done | bytes 245792 | tf_op jit(solution)/shard_map/ppermute | solution.py:864
  35.0 0.0 collective-permute-start.15
  35.0 0.1 pad_maximum_fusion.own
  35.1 0.0 collective-permute-done.14
  35.1 0.0 collective-permute-done.17
  35.1 0.0 collective-permute-done.16
  35.1 1.4 %collective-permute-done.15 = f32[480,128]{1,0:T(8,128)S(1)} collective-permute-done((f32[480,128]{1,0:T(8,128)S(1)}, f32[480,128]{1,0:T(8,128)S(1)}, u32[]{:S(2)}, u32[]{:S(2)}) %collective-permute-start.15) | collective-permute-done | bytes 245792 | tf_op jit(solution)/shard_map/ppermute | solution.py:870
  36.5 0.1 pad_maximum_fusion.1.par
  36.6 0.0 copy-start
  36.6 0.0 copy-start.1
  36.6 0.0 copy-start.2
  36.6 0.3 shard_map.86
  37.0 0.0 collective-permute-done.6.par
  37.0 0.5 %copy-done = f32[272,128]{1,0:T(8,128)S(1)} copy-done((f32[272,128]{1,0:T(8,128)S(1)}, f32[272,128]{1,0:T(8,128)}, u32[]{:S(2)}) %copy-start) | copy-done | bytes 139288
  37.5 0.0 copy-done.1
  37.5 5.3 %shard_map.84 = (f32[2,1,512,128]{3,2,1,0:T(8,128)S(1)}, f32[2,1,512,128]{3,2,1,0:T(8,128)S(1)}, f32[2,1,512,128]{3,2,1,0:T(8,128)S(1)}, f32[4,1,128,128]{3,2,1,...) custom-call(f32[4,288,128]{2,1,0:T(8,128)S(1)} %pad_maximum_fusion.2.own, ...), custom_call_target="tpu_custom_call" | custom-call | tf_op jit(solution)/shard_map/pallas_call | solution.py:839
  42.9 1.8 %shard_map.85 = (f32[2,1,128,128]{3,2,1,0:T(8,128)S(1)}, f32[2,1,128,128]{3,2,1,0:T(8,128)S(1)}, f32[2,1,128,128]{3,2,1,0:T(8,128)S(1)}, f32[2,1,8,128]{3,2,1,0:T(8,128)S(1)}, f32[8,640]{1,0:T(8,128)S(1)}) custom-call(f32[4,1,128,128]{3,2,1,0:T(8,128)S(1)} %get-tuple-element.25.refs_0_, f32[4,1,8,128]{3,2,1,0:T(8,128)S(1)} %get-tuple-element.26.refs_1_, ...), custom_call_target="tpu_custom_call" | custom-call | tf_op jit(solution)/shard_map/pallas_call | solution.py:839
  44.7 5.8 %shard_map.87 = f32[16,512]{1,0:T(8,128)} custom-call(f32[8,640]{1,0:T(8,128)S(1)} %get-tuple-element.27.owned, bf16[6,640,128]{2,1,0:T(8,128)(2,1)S(1)} %get-tuple-element.31.xhi, bf16[6,640,128]{2,1,0:T(8,128)(2,1)S(1)} %get-tuple-element.32.xlo, f32[32,128]{1,0:T(8,128)S(1)} %get-tuple-element.33.labels, ...), custom_call_target="tpu_custom_call" | custom-call | tf_op jit(solution)/shard_map/pallas_call | solution.py:839
  (14 shorter events, 0.1 us)
Async XLA Ops:
  1.1 6.8 %collective-permute-start.7 = (f32[24,128]{1,0:T(8,128)S(1)}, f32[24,128]{1,0:T(8,128)S(1)}, u32[]{:S(2)}, u32[]{:S(2)}) collective-permute-start(f32[24,128]{1,0:T(8,128)S(1)} %get-tuple-element.30), channel_id=1, source_target_pairs={{12,8},{13,9},{14,10},{15,11},{28,24},{29,25},{30,26},{31,27}} | collective-permute-start | bytes 36872 | tf_op jit(solution)/shard_map/ppermute | solution.py:903
  1.7 11.5 %collective-permute-start.2 = (f32[72,128]{1,0:T(8,128)S(1)}, f32[72,128]{1,0:T(8,128)S(1)}, u32[]{:S(2)}, u32[]{:S(2)}) collective-permute-start(f32[72,128]{1,0:T(8,128)S(1)} %get-tuple-element.23), channel_id=1, source_target_pairs={{2,0},{3,1},{0,2},{1,3},{6,4},{7,5},{4,6},{5,7},{10,8},{11,9},{8,1... | collective-permute-start | bytes 110600 | tf_op jit(solution)/shard_map/ppermute | solution.py:895
  5.9 7.3 %collective-permute-start.1 = (f32[72,128]{1,0:T(8,128)S(1)}, f32[72,128]{1,0:T(8,128)S(1)}, u32[]{:S(2)}, u32[]{:S(2)}) collective-permute-start(f32[72,128]{1,0:T(8,128)S(1)} %get-tuple-element.23), channel_id=1, source_target_pairs={{1,0},{2,1},{3,2},{0,3},{5,4},{6,5},{7,6},{4,7},{9,8},{10,9},{11,1... | collective-permute-start | bytes 110600 | tf_op jit(solution)/shard_map/ppermute | solution.py:895
  7.2 6.0 %collective-permute-start = (f32[72,128]{1,0:T(8,128)S(1)}, f32[72,128]{1,0:T(8,128)S(1)}, u32[]{:S(2)}, u32[]{:S(2)}) collective-permute-start(f32[72,128]{1,0:T(8,128)S(1)} %get-tuple-element.23), channel_id=1, source_target_pairs={{3,0},{0,1},{1,2},{2,3},{7,4},{4,5},{5,6},{6,7},{11,8},{8,9},{9,10... | collective-permute-start | bytes 110600 | tf_op jit(solution)/shard_map/ppermute | solution.py:895
  7.9 13.6 %collective-permute-start.10 = (f32[120,128]{1,0:T(8,128)S(1)}, f32[120,128]{1,0:T(8,128)S(1)}, u32[]{:S(2)}, u32[]{:S(2)}) collective-permute-start(f32[120,128]{1,0:T(8,128)S(1)} %pad_maximum_fusion.3), channel_id=1, source_target_pairs={{2,0},{3,1},{0,2},{1,3},{6,4},{7,5},{4,6},{5,7},{10,8},{11,9},{8,1... | collective-permute-start | bytes 184328 | tf_op jit(solution)/shard_map/ppermute | solution.py:895
  9.0 12.5 %collective-permute-start.9 = (f32[120,128]{1,0:T(8,128)S(1)}, f32[120,128]{1,0:T(8,128)S(1)}, u32[]{:S(2)}, u32[]{:S(2)}) collective-permute-start(f32[120,128]{1,0:T(8,128)S(1)} %pad_maximum_fusion.3), channel_id=1, source_target_pairs={{1,0},{2,1},{3,2},{0,3},{5,4},{6,5},{7,6},{4,7},{9,8},{10,9},{11,1... | collective-permute-start | bytes 184328 | tf_op jit(solution)/shard_map/ppermute | solution.py:895
  13.2 6.0 %collective-permute-start.8 = (f32[120,128]{1,0:T(8,128)S(1)}, f32[120,128]{1,0:T(8,128)S(1)}, u32[]{:S(2)}, u32[]{:S(2)}) collective-permute-start(f32[120,128]{1,0:T(8,128)S(1)} %pad_maximum_fusion.3), channel_id=1, source_target_pairs={{3,0},{0,1},{1,2},{2,3},{7,4},{4,5},{5,6},{6,7},{11,8},{8,9},{9,10... | collective-permute-start | bytes 184328 | tf_op jit(solution)/shard_map/ppermute | solution.py:895
  13.3 9.9 %collective-permute-start.5 = (f32[288,128]{1,0:T(8,128)S(1)}, f32[288,128]{1,0:T(8,128)S(1)}, u32[]{:S(2)}, u32[]{:S(2)}) collective-permute-start(f32[288,128]{1,0:T(8,128)S(1)} %constant_dynamic-update-slice_fusion), channel_id=1, source_target_pairs={{24,0},{28,4},{16,8},{20,12},{8,16},{12,20},{0,24},{4,28},{25,1},{... | collective-permute-start | bytes 442376 | tf_op jit(solution)/shard_map/ppermute | solution.py:864
  16.5 8.6 %collective-permute-start.4 = (f32[288,128]{1,0:T(8,128)S(1)}, f32[288,128]{1,0:T(8,128)S(1)}, u32[]{:S(2)}, u32[]{:S(2)}) collective-permute-start(f32[288,128]{1,0:T(8,128)S(1)} %constant_dynamic-update-slice_fusion), channel_id=1, source_target_pairs={{16,0},{20,4},{24,8},{28,12},{0,16},{4,20},{8,24},{12,28},{17,1},{... | collective-permute-start | bytes 442376 | tf_op jit(solution)/shard_map/ppermute | solution.py:864
  19.2 6.9 %collective-permute-start.3 = (f32[288,128]{1,0:T(8,128)S(1)}, f32[288,128]{1,0:T(8,128)S(1)}, u32[]{:S(2)}, u32[]{:S(2)}) collective-permute-start(f32[288,128]{1,0:T(8,128)S(1)} %constant_dynamic-update-slice_fusion), channel_id=1, source_target_pairs={{8,0},{12,4},{0,8},{4,12},{24,16},{28,20},{16,24},{20,28},{9,1},{1... | collective-permute-start | bytes 442376 | tf_op jit(solution)/shard_map/ppermute | solution.py:864
  21.5 10.8 %collective-permute-start.13 = (f32[480,128]{1,0:T(8,128)S(1)}, f32[480,128]{1,0:T(8,128)S(1)}, u32[]{:S(2)}, u32[]{:S(2)}) collective-permute-start(f32[480,128]{1,0:T(8,128)S(1)} %constant_dynamic-update-slice_fusion.4), channel_id=1, source_target_pairs={{24,0},{28,4},{16,8},{20,12},{8,16},{12,20},{0,24},{4,28},{25,1},{... | collective-permute-start | bytes 737288 | tf_op jit(solution)/shard_map/ppermute | solution.py:864
  22.5 10.9 %collective-permute-start.12 = (f32[480,128]{1,0:T(8,128)S(1)}, f32[480,128]{1,0:T(8,128)S(1)}, u32[]{:S(2)}, u32[]{:S(2)}) collective-permute-start(f32[480,128]{1,0:T(8,128)S(1)} %constant_dynamic-update-slice_fusion.4), channel_id=1, source_target_pairs={{16,0},{20,4},{24,8},{28,12},{0,16},{4,20},{8,24},{12,28},{17,1},{... | collective-permute-start | bytes 737288 | tf_op jit(solution)/shard_map/ppermute | solution.py:864
  23.2 11.9 %collective-permute-start.11 = (f32[480,128]{1,0:T(8,128)S(1)}, f32[480,128]{1,0:T(8,128)S(1)}, u32[]{:S(2)}, u32[]{:S(2)}) collective-permute-start(f32[480,128]{1,0:T(8,128)S(1)} %constant_dynamic-update-slice_fusion.4), channel_id=1, source_target_pairs={{8,0},{12,4},{0,8},{4,12},{24,16},{28,20},{16,24},{20,28},{9,1},{1... | collective-permute-start | bytes 737288 | tf_op jit(solution)/shard_map/ppermute | solution.py:864
  26.2 10.8 %collective-permute-start.6 = (f32[4,288,128]{2,1,0:T(8,128)S(1)}, f32[4,288,128]{2,1,0:T(8,128)S(1)}, u32[]{:S(2)}, u32[]{:S(2)}) collective-permute-start(f32[4,288,128]{2,1,0:T(8,128)S(1)} %pad_maximum_fusion.2.own), channel_id=1, source_target_pairs={{0,4},{4,0},{8,12},{12,8},{1,5},{5,1},{9,13},{13,9},{2,6},{6,2},{1... | collective-permute-start | bytes 1769480 | tf_op jit(solution)/shard_map/ppermute | solution.py:870
  26.2 8.9 %collective-permute-start.14 = (f32[480,128]{1,0:T(8,128)S(1)}, f32[480,128]{1,0:T(8,128)S(1)}, u32[]{:S(2)}, u32[]{:S(2)}) collective-permute-start(f32[480,128]{1,0:T(8,128)S(1)} %constant_dynamic-update-slice_fusion.4), channel_id=1, source_target_pairs={{0,4},{4,0},{8,12},{12,8},{1,5},{5,1},{9,13},{13,9},{2,6},{6,2},{1... | collective-permute-start | bytes 737288 | tf_op jit(solution)/shard_map/ppermute | solution.py:870
  32.3 2.8 %collective-permute-start.17 = (f32[480,128]{1,0:T(8,128)S(1)}, f32[480,128]{1,0:T(8,128)S(1)}, u32[]{:S(2)}, u32[]{:S(2)}) collective-permute-start(f32[480,128]{1,0:T(8,128)S(1)} %collective-permute-done.13), channel_id=1, source_target_pairs={{0,4},{4,0},{8,12},{12,8},{1,5},{5,1},{9,13},{13,9},{2,6},{6,2},{1... | collective-permute-start | bytes 737288 | tf_op jit(solution)/shard_map/ppermute | solution.py:870
  33.4 1.7 %collective-permute-start.16 = (f32[480,128]{1,0:T(8,128)S(1)}, f32[480,128]{1,0:T(8,128)S(1)}, u32[]{:S(2)}, u32[]{:S(2)}) collective-permute-start(f32[480,128]{1,0:T(8,128)S(1)} %collective-permute-done.12), channel_id=1, source_target_pairs={{0,4},{4,0},{8,12},{12,8},{1,5},{5,1},{9,13},{13,9},{2,6},{6,2},{1... | collective-permute-start | bytes 737288 | tf_op jit(solution)/shard_map/ppermute | solution.py:870
  35.0 1.5 %collective-permute-start.15 = (f32[480,128]{1,0:T(8,128)S(1)}, f32[480,128]{1,0:T(8,128)S(1)}, u32[]{:S(2)}, u32[]{:S(2)}) collective-permute-start(f32[480,128]{1,0:T(8,128)S(1)} %collective-permute-done.11), channel_id=1, source_target_pairs={{0,4},{4,0},{8,12},{12,8},{1,5},{5,1},{9,13},{13,9},{2,6},{6,2},{1... | collective-permute-start | bytes 737288 | tf_op jit(solution)/shard_map/ppermute | solution.py:870
  36.6 0.9 %copy-start = (f32[272,128]{1,0:T(8,128)S(1)}, f32[272,128]{1,0:T(8,128)}, u32[]{:S(2)}) copy-start(f32[272,128]{1,0:T(8,128)} %constant.14.clone.tref.refs_4_.refs_9_) | copy-start | bytes 417796
  36.6 0.9 %copy-start.1 = (bf16[128,256]{1,0:T(8,128)(2,1)S(1)}, bf16[128,256]{1,0:T(8,128)(2,1)}, u32[]{:S(2)}) copy-start(bf16[128,256]{1,0:T(8,128)(2,1)} %constant.15.clone.pref.refs_10_) | copy-start | bytes 196612
  36.6 0.9 %copy-start.2 = (f32[8,128]{1,0:T(8,128)S(1)}, f32[8,128]{1,0:T(8,128)}, u32[]{:S(2)}) copy-start(f32[8,128]{1,0:T(8,128)} %constant.13.clone.mref.refs_3_.refs_8_) | copy-start | bytes 12292
